TPU v7x, 256 devices: a whole 4x4x8 slice. The times are simulated.
256 devices in a mesh: rec: 64 (over z, y, core), vocab: 4 (over x).
Axes of the slice: x: 4, y: 4, z: 8, core: 2. Of those that a mesh axis runs over, the one named last changes fastest.
Arguments:
- features: bfloat16 [256, 192, 1280], P('rec'), may hold values from -1000 to 1000
- head_weight: bfloat16 [1280, 32768], P(None, ('vocab', 'rec')), may hold values from -0.15625 to 0.15625
- labels: int32 [256, 128], P('rec'), may hold values from 0 to 32767
- audio_len: int32 [256], P(('rec', 'vocab')), may hold values from 1 to 192, as said below
- transcript_len: int32 [256], P(('rec', 'vocab')), may hold values from 1 to 128
Outputs:
- label_logprob: float32 [256, 192, 128], P(('rec', 'vocab'))
- path_score: float32 [256], P(('rec', 'vocab'))
Inputs may be any that keep to these rules, and one draw needn't show every extreme that they name: `audio_len`: each recording has at least as many frames in use as its transcript has labels.
All inputs are finite; a program needn't handle non-finite values.
Results may differ from a plain program's by a relative error of at most 0.00055.
Values may be sent and summed in bfloat16 or wider, within the bound.
No kernel may reach another device: no remote copies, remote signals or barrier semaphores. Data moves between devices by JAX's collectives and lax.ppermute only.
A program may use at most 128 MiB of HBM per device.

v0:
```python
import jax
import jax.numpy as jnp
from jax import lax
from jax.sharding import PartitionSpec as P

negative_fill = -1e30
block_frames = 64


def sent_to_all(array, axis):
    copies = jnp.broadcast_to(array, (lax.axis_size(axis), *array.shape))
    return lax.all_to_all(copies, axis, split_axis=0, concat_axis=0, tiled=True)


def gathered_once(array, axis):
    leaves = jax.tree.leaves(array)
    turns = sorted(range(len(leaves)), key=lambda k: -leaves[k].size)
    width = (1, *leaves[turns[0]].shape)[-1]
    lines = [
        jnp.pad(leaves[k].reshape(-1), (0, -leaves[k].size % width)).reshape(-1, width)
        for k in turns
    ]
    both, at, found = (sent_to_all(jnp.concatenate(lines), axis), 0, {})
    for k, line in zip(turns, lines):
        slab = both[:, at : at + len(line)].reshape(len(both), -1)
        found[k] = slab[:, : leaves[k].size].reshape(-1, *leaves[k].shape)
        at += len(line)
    numbers = iter(range(len(leaves)))
    return jax.tree.map(lambda _: found[next(numbers)], array)


def combined_pairwise(pieces, combine):
    while len(jax.tree.leaves(pieces)[0]) > 1:
        pieces = jax.vmap(combine)(
            *(jax.tree.map(lambda part: part[side::2], pieces) for side in (0, 1))
        )
    return jax.tree.map(lambda part: part[0], pieces)


def merged(array, axis, combine):
    pieces = gathered_once(array, axis)
    return combined_pairwise(pieces, combine)


def cut_along(array, dim, size):
    shape = array.shape
    pieces = array.reshape(*shape[:dim], size, shape[dim] // size, *shape[dim + 1 :])
    return jnp.moveaxis(pieces, dim, 0)


def sent_and_summed(array, axis, dim):
    size = lax.axis_size(axis)
    pieces = lax.all_to_all(cut_along(array, dim, size), axis, 0, 0, tiled=True)
    return jnp.sum(pieces.astype(jnp.float32), axis=0)


def viterbi(log_prob, audio_len, transcript_len):
    rec_count, frames, slots = log_prob.shape
    states = lax.iota(jnp.int32, slots)[None, :]
    target = states == transcript_len[:, None] - 1
    initial = jnp.where(states == 0, log_prob[:, 0, :], negative_fill)
    best_end = jnp.where(audio_len == 1, jnp.sum(jnp.where(target, initial, 0.0), 1), 0.0)

    def advance(current, emitted):
        shifted = jnp.concatenate(
            [jnp.full_like(current[:, :1], negative_fill), current[:, :-1]], 1
        )
        current = jnp.maximum(current, shifted) + emitted
        return (current, current)

    current = initial
    begin = 1
    while begin < frames:
        finish = min(frames, (begin // block_frames + 1) * block_frames)
        block_in = jnp.moveaxis(log_prob[:, begin:finish, :], 1, 0)
        current, block_scores = lax.scan(advance, current, block_in, unroll=2)
        frame_ids = begin + lax.iota(jnp.int32, finish - begin)
        hit = (frame_ids[:, None] == audio_len[None, :] - 1)[:, :, None] & target[None, :, :]
        reached = jnp.sum(jnp.where(hit, block_scores, 0.0), (0, 2))
        inside = (audio_len - 1 >= begin) & (audio_len - 1 < finish)
        best_end = jnp.where(inside, reached, best_end)
        begin = finish
    return best_end


def combine(first_pair, second_pair):
    top_a, sum_a = first_pair
    top_b, sum_b = second_pair
    row_top = jnp.maximum(top_a, top_b)
    return (row_top, sum_a * jnp.exp(top_a - row_top) + sum_b * jnp.exp(top_b - row_top))


def body(features, head_weight, labels, audio_len, transcript_len):
    rec_dev, frames, width = features.shape
    frame_rows = features.reshape(rec_dev * frames, width)
    shard_cols = head_weight.shape[1]
    groups = lax.axis_size("rec")
    vocab_count = lax.axis_size("vocab")
    vocab_index = lax.axis_index("vocab")
    gathered = lax.all_gather(head_weight, "rec", axis=1, tiled=True)
    logits = jnp.dot(frame_rows, gathered, preferred_element_type=jnp.float32)
    local_top = jnp.max(logits, 1)
    local_sum = jnp.sum(jnp.exp(logits - local_top[:, None]), 1)
    row_top, row_total = merged((local_top, local_sum), "vocab", combine)
    log_norm = (row_top + jnp.log(row_total)).reshape(rec_dev, frames)
    span_cols = shard_cols * groups
    rounded = logits.astype(jnp.bfloat16).reshape(rec_dev, frames, span_cols)
    shard_first = vocab_index * span_cols
    is_owned = (labels >= shard_first) & (labels < shard_first + span_cols)
    position = jnp.where(is_owned, labels - shard_first, -1)
    columns_iota = lax.iota(jnp.int32, span_cols)
    one_hot = (columns_iota[None, :, None] == position[:, None, :]).astype(jnp.bfloat16)
    picked = jnp.einsum("rfv,rvl->rfl", rounded, one_hot, preferred_element_type=jnp.float32)
    own_count = rec_dev // vocab_count
    own_start = vocab_index * own_count
    norm_part = lax.dynamic_slice_in_dim(log_norm, own_start, own_count, 0)
    own_part = sent_and_summed(picked.astype(jnp.bfloat16), "vocab", 0)
    log_prob = own_part - norm_part[:, :, None]
    return (log_prob, viterbi(log_prob, audio_len, transcript_len))


def solution(mesh):
    placed = (
        P("rec", None, None),
        P(None, ("vocab", "rec")),
        P("rec", None),
        P(("rec", "vocab")),
        P(("rec", "vocab")),
    )
    return jax.shard_map(
        body,
        mesh=mesh,
        in_specs=placed,
        out_specs=(P(("rec", "vocab"), None, None), P(("rec", "vocab"))),
        check_vma=False,
    )
```

profile of v0, /device:TPU:1, one launch (start us, length us, event | category | flops | bytes accessed | tf_op | source)
XLA Modules:
  0.0 232.3 jit_solution(12327565630726467600)
XLA Ops:
  7.2 0.7 all-gather.2.cloned.1.call-update
  9.3 0.7 subtract_select_fusion
  10.0 122.2 %all-gather.2.cloned.1.call-done = bf16[1280,8192]{1,0:T(8,128)(2,1)} async-done(((bf16[1280,128]{1,0:T(8,128)(2,1)}), bf16[1280,8192]{1,0:T(8,128)(2,1)}) %all-gather.2.cloned.1.call-update) | async-done | bytes 20971536 | tf_op jit(solution)/shard_map/all_gather | solution.py:100
  132.2 25.1 %fusion.31 = (f32[768]{0:T(1024)S(1)}, f32[768,8192]{1,0:T(8,128)}) fusion(bf16[768,1280]{1,0:T(8,128)(2,1)S(1)} %bitcast.123, bf16[1280,8192]{1,0:T(8,128)(2,1)} %all-gather.2.cloned.1.call-done), kind=kOutput, calls=%fused_computation.76 | convolution fusion | flops 16112417792 | bytes 48106496 | tf_op jit(solution)/shard_map/dot_general | solution.py:101
  157.3 22.7 %exponential_reduce_fusion = (f32[768]{0:T(1024)S(1)}, bf16[768,8192]{1,0:T(8,128)(2,1)}) fusion(f32[768,8192]{1,0:T(8,128)} %get-tuple-element.148, f32[768]{0:T(1024)S(1)} %get-tuple-element.147), kind=kLoop, calls=%fused_computation.36 | loop fusion | flops 18873600 | bytes 37754880 | tf_op jit(solution)/shard_map/reduce_sum | solution.py:103
  180.0 0.6 broadcast_in_dim.75
  180.7 4.0 %all-to-all-start.1 = ((f32[4,2,768]{2,1,0:T(2,128)}), f32[4,2,768]{2,1,0:T(2,128)S(1)}, u32[]{:S(2)}, u32[]{:S(2)}) async-start(f32[4,2,768]{2,1,0:T(2,128)} %broadcast_in_dim.75), calls=%async_computation.1 | async-start | bytes 49152 | tf_op jit(solution)/shard_map/all_to_all | solution.py:12
  184.6 8.0 %fusion.21 = bf16[4,1,192,128]{3,2,1,0:T(8,128)(2,1)} fusion(bf16[4,192,8192]{2,1,0:T(8,128)(2,1)} %bitcast.124, s32[4,128]{1,0:T(4,128)S(1)} %subtract_select_fusion), kind=kOutput, calls=%fused_computation.41 | convolution fusion | flops 1614905344 | bytes 12781568 | tf_op jit(solution)/shard_map/rfv,rvl->rfl/dot_general | solution.py:113
  192.6 4.2 %all-to-all-start = ((bf16[4,1,192,128]{3,2,1,0:T(8,128)(2,1)}), bf16[4,1,192,128]{3,2,1,0:T(8,128)(2,1)S(1)}, u32[]{:S(2)}, u32[]{:S(2)}) async-start(bf16[4,1,192,128]{3,2,1,0:T(8,128)(2,1)} %fusion.21), calls=%async_computation | async-start | bytes 393216 | tf_op jit(solution)/shard_map/all_to_all | solution.py:53
  197.1 4.9 %all-to-all-done = bf16[4,1,192,128]{3,2,1,0:T(8,128)(2,1)S(1)} async-done(((bf16[4,1,192,128]{3,2,1,0:T(8,128)(2,1)}), bf16[4,1,192,128]{3,2,1,0:T(8,128)(2,1)S(1)}, u32[]{:S(2)}, u32[]{:S(2)}) %all-to-all-start) | async-done | bytes 196640 | tf_op jit(solution)/shard_map/all_to_all | solution.py:53
  202.0 0.1 bitcast_subtract_fusion
  202.2 5.7 %while.36 = (s32[]{:T(128)}, f32[1,128]{1,0:T(1,128)S(1)}, f32[31,2,1,128]{3,1,2,0:T(2,128)S(1)}, f32[31,2,1,128]{3,2,1,0:T(1,128)S(1)}, s32[]{:T(128)}, /*index=5*/f32[1,1]{1,0:T(1,128)}, s32[]{:T(128)}, s32[]{}) while((s32[]{:T(128)}, f32[1,128]{1,0:T(1,128)S(1)}, f32[31,2,1,128]{3,1,2,0:T(2,128)S(1)}, f32[31,2,1,128]{3,2,1,0:T(1,128)S(1)}, ...), condition=%wide.region_4.5_spmd, body=%wide.region_3.4_spmd.sunk | while | flops 1027 | bytes 8305 | solution.py:76
  202.5 0.1 fusion.42
  202.7 0.1 fusion.42
  202.8 0.1 fusion.42
  203.2 0.1 fusion.42
  203.4 0.1 fusion.42
  203.6 0.1 fusion.42
  203.9 0.1 fusion.42
  204.1 0.1 fusion.42
  204.3 0.1 fusion.42
  204.7 0.1 fusion.42
  204.8 0.1 fusion.42
  205.4 0.1 fusion.42
  205.6 0.1 fusion.42
  205.9 0.1 fusion.42
  206.1 0.1 fusion.42
  206.3 0.1 fusion.42
  206.7 0.1 fusion.42
  206.8 0.1 fusion.42
  207.0 0.1 fusion.42
  207.4 0.1 fusion.42
  207.6 0.1 fusion.42
  207.8 0.1 fusion.42
  207.9 0.6 fusion.27
  208.5 5.8 %while.37 = (s32[]{:T(128)}, f32[1,128]{1,0:T(1,128)S(1)}, f32[32,2,1,128]{3,1,2,0:T(2,128)S(1)}, f32[32,2,1,128]{3,2,1,0:T(1,128)S(1)}, s32[]{:T(128)}, /*index=5*/f32[1,1]{1,0:T(1,128)}, s32[]{:T(128)}, s32[]{}) while((s32[]{:T(128)}, f32[1,128]{1,0:T(1,128)S(1)}, f32[32,2,1,128]{3,1,2,0:T(2,128)S(1)}, f32[32,2,1,128]{3,2,1,0:T(1,128)S(1)}, ...), condition=%wide.region_6.7_spmd, body=%wide.region_5.6_spmd.sunk | while | flops 1027 | bytes 8305 | solution.py:76
  208.7 0.1 fusion.44
  208.9 0.1 fusion.44
  209.3 0.1 fusion.44
  209.5 0.1 fusion.44
  209.7 0.1 fusion.44
  210.0 0.1 fusion.44
  210.2 0.1 fusion.44
  210.4 0.1 fusion.44
  210.8 0.1 fusion.44
  214.3 5.8 %while.38 = (s32[]{:T(128)}, f32[1,128]{1,0:T(1,128)S(1)}, f32[32,2,1,128]{3,1,2,0:T(2,128)S(1)}, f32[32,2,1,128]{3,2,1,0:T(1,128)S(1)}, s32[]{:T(128)}, /*index=5*/f32[1,1]{1,0:T(1,128)}, s32[]{:T(128)}, s32[]{}) while((s32[]{:T(128)}, f32[1,128]{1,0:T(1,128)S(1)}, f32[32,2,1,128]{3,1,2,0:T(2,128)S(1)}, f32[32,2,1,128]{3,2,1,0:T(1,128)S(1)}, ...), condition=%wide.region_8.9_spmd, body=%wide.region_7.8_spmd.sunk | while | flops 1027 | bytes 8305 | solution.py:76
  220.8 0.7 fusion.24
  222.2 0.8 fusion.23
  (380 shorter events, 14.7 us)
Async XLA Ops:
  7.2 125.0 %copy-start = (bf16[4,192,1280]{2,1,0:T(8,128)(2,1)S(1)}, bf16[4,192,1280]{2,1,0:T(8,128)(2,1)}, u32[]{:S(2)}) copy-start(bf16[4,192,1280]{2,1,0:T(8,128)(2,1)} %param.11) | copy-start | bytes 5898244
  7.2 125.0 %all-gather.2.cloned.1.call-start = ((), (), s32[]{:S(2)}) async-start(), calls=%async_computation.2 | async-start | bytes 21299200 | tf_op jit(solution)/shard_map/all_gather | solution.py:100
  180.7 11.9 %all-to-all-start.1 = ((f32[4,2,768]{2,1,0:T(2,128)}), f32[4,2,768]{2,1,0:T(2,128)S(1)}, u32[]{:S(2)}, u32[]{:S(2)}) async-start(f32[4,2,768]{2,1,0:T(2,128)} %broadcast_in_dim.75), calls=%async_computation.1 | async-start | bytes 49152 | tf_op jit(solution)/shard_map/all_to_all | solution.py:12
  192.6 9.4 %all-to-all-start = ((bf16[4,1,192,128]{3,2,1,0:T(8,128)(2,1)}), bf16[4,1,192,128]{3,2,1,0:T(8,128)(2,1)S(1)}, u32[]{:S(2)}, u32[]{:S(2)}) async-start(bf16[4,1,192,128]{3,2,1,0:T(8,128)(2,1)} %fusion.21), calls=%async_computation | async-start | bytes 393216 | tf_op jit(solution)/shard_map/all_to_all | solution.py:53
  202.1 22.2 %copy-start.1 = (f32[1,192,128]{2,1,0:T(8,128)}, f32[1,192,128]{2,1,0:T(8,128)S(1)}, u32[]{:S(2)}) copy-start(f32[1,192,128]{2,1,0:T(8,128)S(1)} %bitcast_subtract_fusion) | copy-start | bytes 294916
Sparse Core Ops, SparseCore 0:
  10.6 121.5 all-gather.1
where the time goes:
time: 233 us; the launch traced here: 232 us
  waiting for transfers between devices  128 us (55%)
  other arithmetic  41.4 us (18%)
  matrix products  33 us (14%)
  between operations  19.3 us (8%)
  starting transfers between devices  8.24 us (4%)
    all_gather x1, waiting for transfers between devices, body(): gathered = lax.all_gather(head_weight, 'rec', axis=1, tiled=True)  122 us
    dot_general x1, matrix products, body(): logits = jnp.dot(frame_rows, gathered, preferred_element_type=jnp.float32)  25.1 us
    reduce_sum x1, other arithmetic, body(): local_sum = jnp.sum(jnp.exp(logits - local_top[:, None]), 1)  22.7 us
    add x190, other arithmetic, advance(): current = jnp.maximum(current, shifted) + emitted  15 us
    dot_general x1, matrix products, body(): jnp.einsum('rfv,rvl->rfl', rounded, one_hot, preferred_element_type=jnp.f...  7.96 us
    all_to_all x1, waiting for transfers between devices, sent_and_summed(): pieces = lax.all_to_all(cut_along(array, dim, size), axis, 0, 0, tiled=True)  4.88 us
  transfers between devices with their start and end apart: 3, of which 2 were waited for; matrix products, arithmetic and copies ran while one was open for 4% of the time, Pallas kernels for 0%

commit v1 on v0

v1 whole, which is shorter than its diff:
```python
import functools

import jax
import jax.numpy as jnp
import numpy as np
from jax import lax
from jax.experimental import pallas as pl
from jax.experimental.pallas import tpu as pltpu
from jax.sharding import PartitionSpec as P

negative_fill = -1e30
NZ, NY = 8, 4
TILE = 256
BLOCK = 512
ANY = pl.BlockSpec(memory_space=pl.ANY)
VMEM = pl.BlockSpec(memory_space=pltpu.VMEM)
SMEM = pl.BlockSpec(memory_space=pltpu.SMEM)


def rec_index(z, y, core):
    return ((z % NZ) * NY + y % NY) * 2 + core


def moves(step0=None, step1=None, swap=0):
    pairs = []
    for core, step in ((0, step0), (1, step1)):
        if step is None:
            continue
        for z in range(NZ):
            for y in range(NY):
                pairs.append(
                    (rec_index(z, y, core), rec_index(z + step[0], y + step[1], core ^ swap))
                )
    return pairs


ZP, ZM, YP, YM = (1, 0), (-1, 0), (0, 1), (0, -1)


def place_tables():
    first = [(0, 0), (-1, 0), (1, 0), (-2, 0)]
    second = [(2, 0), (-3, 0), (3, 0), (4, 0)]
    table = np.zeros((2, NZ * NY), np.int32)
    blocks0 = [(first, 0), (first, -1), (first, 1), (first, -2), (second, -1), (second, 1), (second, 2), (second, 0)]
    for b, (subs, dy) in enumerate(blocks0):
        for s, (dz, _) in enumerate(subs):
            table[0, (dz % NZ) * NY + dy % NY] = b * 4 + s
    for b, dz in enumerate([0, -1, 1, -2, -3, 2, 3, 4]):
        for s, dy in enumerate([0, -1, 1, -2]):
            table[1, (dz % NZ) * NY + dy % NY] = b * 4 + s
    return table


def block_update(w_vmem, f_vmem, f_sems, f_copies, l_ref, m_ref, s_ref, fresh):
    tiles = f_vmem.shape[0]

    def tile_step(t, _):
        for k, copy in enumerate(f_copies):

            @pl.when(t == k * (tiles // len(f_copies)))
            def _(copy=copy):
                copy.wait()

        tile = lax.dot_general(
            w_vmem[...], f_vmem[t], (((1,), (1,)), ((), ())), preferred_element_type=jnp.float32
        )
        l_ref[2 * t] = tile[:, :128]
        l_ref[2 * t + 1] = tile[:, 128:]
        cube = tile.reshape(BLOCK // 8, 8, TILE)
        top = jnp.max(cube, 0)
        if not fresh:
            old = m_ref[t]
            top = jnp.maximum(top, old)
        total = jnp.sum(jnp.exp(cube - top[None]), 0)
        if not fresh:
            total = total + s_ref[t] * jnp.exp(old - top)
        m_ref[t] = top
        s_ref[t] = total
        return 0

    lax.fori_loop(0, tiles, tile_step, 0)


def take_rows(block, bounds, entries, l_ref, p_ref):
    def one(k, _):
        entry = entries[k]
        row = entry // 1024
        item = entry % 1024
        window = (item // 128) * 3 // 2
        p_ref[0, pl.ds(item, 1), :] = l_ref[window, pl.ds(row, 1), :]
        p_ref[1, pl.ds(item, 1), :] = l_ref[window + 1, pl.ds(row, 1), :]
        return 0

    lax.fori_loop(bounds[block], bounds[block + 1], one, 0)


def start_features(fa, fb, f_vmem, sems):
    half = f_vmem.shape[0] // 2
    copies = []
    for k, ref in enumerate((fa, fb)):
        copy = pltpu.make_async_copy(ref, f_vmem.at[pl.ds(k * half, half)], sems.at[k])
        copy.start()
        copies.append(copy)
    return copies


def first_kernel(bounds, entries, w, fa, fb, m_out, s_out, p_out, f_vmem, l_ref, sems):
    copies = start_features(fa, fb, f_vmem, sems)
    p_out[...] = jnp.zeros_like(p_out)
    block_update(w, f_vmem, sems, copies, l_ref, m_out, s_out, True)
    take_rows(0, bounds, entries, l_ref, p_out)


def next_kernel(block, bounds, entries, w, fa, fb, m_in, s_in, p_in, m_out, s_out, p_out, f_vmem, l_ref, sems):
    copies = start_features(fa, fb, f_vmem, sems)
    m_out[...] = m_in[...]
    s_out[...] = s_in[...]
    p_out[...] = p_in[...]
    block_update(w, f_vmem, sems, copies, l_ref, m_out, s_out, False)
    take_rows(block, bounds, entries, l_ref, p_out)


def last_kernel(where, bounds, entries, w0, w1a, w1b, fa, fb, m_in, s_in, p_in, *rest):
    outs, (m_ref, s_ref, p_ref, w_vmem, f_vmem, l_ref, lse_ref, sems, w_sems) = rest[:8], rest[8:]
    copies = start_features(fa, fb, f_vmem, sems)
    place, core = where[0], where[1]

    @pl.when(core == 0)
    def _():
        copy = pltpu.make_async_copy(w0, w_vmem, w_sems.at[0])
        copy.start()
        copy.wait()

    @pl.when(core == 1)
    def _():
        half = BLOCK // 2
        one = pltpu.make_async_copy(w1a, w_vmem.at[pl.ds(0, half)], w_sems.at[0])
        two = pltpu.make_async_copy(w1b, w_vmem.at[pl.ds(half, half)], w_sems.at[1])
        one.start()
        two.start()
        one.wait()
        two.wait()

    m_ref[...] = m_in[...]
    s_ref[...] = s_in[...]
    p_ref[...] = p_in[...]
    block_update(w_vmem, f_vmem, sems, copies, l_ref, m_ref, s_ref, False)
    take_rows(BLOCKS - 1, bounds, entries, l_ref, p_ref)
    for t in range(m_ref.shape[0]):
        top = jnp.max(m_ref[t], 0, keepdims=True)
        total = jnp.sum(s_ref[t] * jnp.exp(m_ref[t] - top), 0, keepdims=True)
        value = jnp.broadcast_to(top + jnp.log(total), (8, TILE))
        lse_ref[2 * t] = value[:, :128]
        lse_ref[2 * t + 1] = value[:, 128:]
    for half in range(2):
        for step in range(4):
            rec = half * 4 + (place + step) % 4
            out = outs[half * 4 + step]
            shift = (TILE - 64 * (rec % 2)) % TILE
            slots = pl.ds(pl.multiple_of(rec * 128, 128), 128)
            rows = jnp.concatenate([p_ref[0, slots, :], p_ref[1, slots, :]], 1)
            out[0:128, :] = pltpu.roll(rows, shift, 1).astype(jnp.bfloat16)
            window = rec * 3 // 2
            value = jnp.concatenate([lse_ref[window], lse_ref[window + 1]], 1)
            value = pltpu.roll(value, shift, 1)
            high = value.astype(jnp.bfloat16).astype(jnp.float32)
            middle = (value - high).astype(jnp.bfloat16).astype(jnp.float32)
            low = value - high - middle
            line = lax.broadcasted_iota(jnp.int32, (8, TILE), 0)
            parts = jnp.where(line == 0, high, jnp.where(line == 1, middle, jnp.where(line == 2, low, 0.0)))
            parts = jnp.concatenate([parts, jnp.zeros_like(parts)], 0)
            out[128:144, :] = parts.astype(jnp.bfloat16)


DEPTH = 8


def align_kernel(lengths, *refs):
    parts, (logprob, path, turned, scores) = refs[:8], refs[8:]
    frames = logprob.shape[0]
    picked = parts[0][0:128, :].astype(jnp.float32)
    for part in parts[1:]:
        picked = picked + part[0:128, :].astype(jnp.float32)
    norms = []
    for part in parts:
        lines = part[128:144, :].astype(jnp.float32)
        norms.append(lines[0:1] + lines[1:2] + lines[2:3])
    top = functools.reduce(jnp.maximum, norms)
    norm = top + jnp.log(sum(jnp.exp(value - top) for value in norms))
    table = (picked - norm).T[:frames]
    logprob[...] = table
    lanes = lax.broadcasted_iota(jnp.int32, (1, 128), 1)
    for d in range(DEPTH):
        turned[d] = table if d == 0 else pltpu.roll(table, d, 1)

    def advance(score, first, count):
        copies = [score] + [jnp.where(lanes < d, negative_fill, pltpu.roll(score, d, 1)) for d in range(1, count + 1)]
        for i in range(count):
            for d in range(count - i):
                emitted = turned[d, pl.ds(first + i, 1), :]
                copies[d] = jnp.maximum(copies[d], copies[d + 1]) + emitted
            scores[pl.ds(first + i, 1), :] = copies[0]
        return copies[0]

    score = jnp.where(lanes == 0, table[0:1], negative_fill)
    scores[0:1, :] = score
    score = advance(score, 1, DEPTH - 1)
    lax.fori_loop(1, frames // DEPTH, lambda b, now: advance(now, pl.multiple_of(b * DEPTH, DEPTH), DEPTH), score)
    final = scores[pl.ds(lengths[0] - 1, 1), :]
    hit = jnp.sum(jnp.where(lanes == lengths[1] - 1, final, 0.0), 1, keepdims=True)
    path[...] = jnp.broadcast_to(hit, path.shape)


BLOCKS = 8


def label_entries(labels, vocab_index, z, y, core):
    flat = labels.reshape(-1)
    local = flat % (NZ * NY * 256)
    owner = local // 128
    owner_core = owner % 2
    dy = (owner // 2 - y) % NY
    dz = (owner // (2 * NY) - z) % NZ
    table = jnp.where(core == 0, jnp.asarray(place_tables()[0]), jnp.asarray(place_tables()[1]))
    kinds = lax.iota(jnp.int32, NZ * NY)
    position = jnp.sum(jnp.where((dz * NY + dy)[:, None] == kinds[None], table[None], 0), 1)
    mine = (flat // (NZ * NY * 256) == vocab_index) & (owner_core == core)
    block = jnp.where(mine, position // 4, BLOCKS)
    row = position % 4 * 128 + local % 128
    ids = lax.iota(jnp.int32, flat.shape[0])
    sort_key = block * 1024 + ids
    rank = jnp.sum((sort_key[None, :] < sort_key[:, None]).astype(jnp.int32), 1)
    value = row * 1024 + ids
    entries = jnp.sum(jnp.where(rank[:, None] == ids[None, :], value[:, None], 0), 0)
    steps = lax.iota(jnp.int32, 16)
    bounds = jnp.sum((block[:, None] < steps[None, :]).astype(jnp.int32), 0)
    return bounds, entries


def body(features, head_weight, labels, audio_len, transcript_len):
    rec_dev, frames, width = features.shape
    rows = rec_dev * frames
    vocab_index = lax.axis_index("vocab")
    rec = lax.axis_index("rec")
    core, y, z = rec % 2, rec // 2 % NY, rec // (2 * NY)
    swap = moves((0, 0), (0, 0), 1)

    def send(array, step0, step1):
        return lax.ppermute(array, "rec", moves(step0, step1))

    own = head_weight.T
    a1 = send(own, ZP, YP)
    a2 = send(own, ZM, YM)
    tiles = rows // TILE
    fa = features.reshape(tiles, TILE, width)
    fb = lax.ppermute(features, "rec", swap).reshape(tiles, TILE, width)
    other_labels = lax.ppermute(labels, "rec", swap)
    bounds, entries = label_entries(jnp.concatenate([labels, other_labels]), vocab_index, z, y, core)
    a3 = send(a1, ZP, YP)
    c1 = jnp.concatenate([own, a1, a2, a3])
    b1 = send(c1, YP, ZP)
    b2 = send(c1, YM, ZM)
    a4 = send(a2, ZM, None)
    a5 = send(a3, ZP, None)
    a6 = send(a4, ZM, None)
    a7 = send(a6, ZM, None)
    c2 = jnp.concatenate([a4, a5, a6, a7])
    b3 = send(b1, YP, ZP)
    b4 = send(jnp.where(core == 0, c2, b3), YP, ZP)
    b5 = send(jnp.where(core == 0, c2, b2), YM, ZM)
    b6 = send(b5, YM, ZM)
    half = BLOCK // 2
    b7 = send(b4[:half], None, ZP)
    b8 = send(b6[half:], None, ZM)

    f32 = jnp.float32
    state = (
        jax.ShapeDtypeStruct((2 * tiles, 8, TILE), f32),
        jax.ShapeDtypeStruct((2 * tiles, 8, TILE), f32),
        jax.ShapeDtypeStruct((2, 8 * 128, 128), f32),
    )
    scratch = [
        pltpu.VMEM((2 * tiles, TILE, width), jnp.bfloat16),
        pltpu.VMEM((4 * tiles, BLOCK, 128), f32),
    ]
    cost = pl.CostEstimate(
        flops=2 * 2 * rows * BLOCK * width, bytes_accessed=8_000_000, transcendentals=2 * rows * BLOCK
    )
    carried = pl.pallas_call(
        first_kernel,
        out_shape=state,
        in_specs=[SMEM, SMEM, VMEM, ANY, ANY],
        out_specs=[VMEM] * 3,
        scratch_shapes=[*scratch, pltpu.SemaphoreType.DMA((2,))],
        cost_estimate=cost,
    )(bounds, entries, c1, fa, fb)
    for number, block in enumerate((b1, b2, b3, b4, b5, b6)):
        carried = pl.pallas_call(
            functools.partial(next_kernel, number + 1),
            out_shape=state,
            in_specs=[SMEM, SMEM, VMEM, ANY, ANY, VMEM, VMEM, VMEM],
            out_specs=[VMEM] * 3,
            scratch_shapes=[*scratch, pltpu.SemaphoreType.DMA((2,))],
            cost_estimate=cost,
        )(bounds, entries, block, fa, fb, *carried)
    payload = jax.ShapeDtypeStruct((144, TILE), jnp.bfloat16)
    sent = pl.pallas_call(
        last_kernel,
        out_shape=[payload] * 8,
        in_specs=[SMEM, SMEM, SMEM, ANY, ANY, ANY, ANY, ANY, VMEM, VMEM, VMEM],
        out_specs=[VMEM] * 8,
        scratch_shapes=[
            *(pltpu.VMEM(leaf.shape, leaf.dtype) for leaf in state),
            pltpu.VMEM((BLOCK, width), jnp.bfloat16),
            *scratch,
            pltpu.VMEM((4 * tiles, 8, 128), f32),
            pltpu.SemaphoreType.DMA((2,)),
            pltpu.SemaphoreType.DMA((2,)),
        ],
        cost_estimate=cost,
    )(jnp.stack([vocab_index, core]), bounds, entries, c2, b7, b8, fa, fb, *carried)
    vocabs = lax.axis_size("vocab")
    groups = lax.axis_size("rec")
    got = []
    for side in range(2):
        for step in range(vocabs):
            part = sent[side * 4 + step]
            if side or step:
                pairs = [
                    (g * vocabs + v, (g ^ side) * vocabs + (v + step) % vocabs)
                    for g in range(groups)
                    for v in range(vocabs)
                ]
                part = lax.ppermute(part, ("rec", "vocab"), pairs)
            got.append(part)
    log_prob, path = pl.pallas_call(
        align_kernel,
        out_shape=[jax.ShapeDtypeStruct((frames, 128), f32), jax.ShapeDtypeStruct((8, 128), f32)],
        in_specs=[SMEM, *([VMEM] * 8)],
        out_specs=[VMEM] * 2,
        scratch_shapes=[pltpu.VMEM((DEPTH, frames, 128), f32), pltpu.VMEM((frames, 128), f32)],
    )(jnp.concatenate([audio_len, transcript_len]), *got)
    return log_prob[None], path[0, :1]


def solution(mesh):
    placed = (
        P("rec", None, None),
        P(None, ("vocab", "rec")),
        P("rec", None),
        P(("rec", "vocab")),
        P(("rec", "vocab")),
    )
    return jax.shard_map(
        body,
        mesh=mesh,
        in_specs=placed,
        out_specs=(P(("rec", "vocab"), None, None), P(("rec", "vocab"))),
        check_vma=False,
    )
```

time: 233 us -> 185 us (0.79)
  Pallas kernels: 0 us -> 72.3 us
  waiting for transfers between devices: 128 us -> 63.3 us
  other arithmetic: 41.4 us -> 8.03 us
  matrix products: 33 us -> 0 us
  starting transfers between devices: 8.24 us -> 31.9 us
  between operations: 19.3 us -> 2.28 us
  local copies, waits for them, and re-layouts: 1.97 us -> 6.38 us
    all_gather x1 -> x0, waiting for transfers between devices: 122 us -> none  [body(): gathered = lax.all_gather(head_weight, 'rec', axis=1, tiled=True)]
    pallas_call x0 -> x9, Pallas kernels: none -> 72.3 us  [the longest x6 50.9 us: body(): pl.pallas_call(functools.partial(next_kernel, number + 1), out_shape=stat...]
    ppermute x0 -> x24, waiting for transfers between devices: none -> 63.3 us  [the longest x15 56.6 us: send(): return lax.ppermute(array, 'rec', moves(step0, step1))]
    dot_general x2 -> x0, matrix products: 33 us -> none  [the longest x1 25.1 us: body(): logits = jnp.dot(frame_rows, gathered, preferred_element_type=jnp.float32)]
    ppermute x0 -> x24, starting transfers between devices: none -> 31.9 us  [the longest x15 21.9 us: send(): return lax.ppermute(array, 'rec', moves(step0, step1))]
    reduce_sum x5 -> x4, other arithmetic: 24.9 us -> 2.53 us  [the longest x1 1.26 us: label_entries(): jnp.sum(jnp.where(rank[:, None] == ids[None, :], value[:, None], 0), 0)]
    add x192 -> x2, other arithmetic: 15 us -> 0.08 us  [the longest x1 0.04 us: label_entries(): sort_key = block * 1024 + ids]
    all_to_all x2 -> x0, starting transfers between devices: 8.2 us -> none  [the longest x1 4.23 us: sent_and_summed(): pieces = lax.all_to_all(cut_along(array, dim, size), axis, 0, 0, tiled=True)]
  transfers between devices with their start and end apart: 3 -> 24, of which waited for: 2 -> 9; matrix products, arithmetic and copies ran while one was open for 4% -> 3% of each run, Pallas kernels for 0% -> 32%
where the time goes in v1:
time: 185 us; the launch traced here: 184 us
  Pallas kernels  72.3 us (39%)
  waiting for transfers between devices  63.3 us (34%)
  starting transfers between devices  31.9 us (17%)
  other arithmetic  8.03 us (4%)
  local copies, waits for them, and re-layouts  6.38 us (3%)
  between operations  2.28 us (1%)
    ppermute x15, waiting for transfers between devices, send(): return lax.ppermute(array, 'rec', moves(step0, step1))  56.6 us
    pallas_call x6, Pallas kernels, body(): pl.pallas_call(functools.partial(next_kernel, number + 1), out_shape=stat...  50.9 us
    ppermute x15, starting transfers between devices, send(): return lax.ppermute(array, 'rec', moves(step0, step1))  21.9 us
    ppermute x7, starting transfers between devices, body(): part = lax.ppermute(part, ('rec', 'vocab'), pairs)  8.99 us
    pallas_call x1, Pallas kernels, body(): pl.pallas_call(last_kernel, out_shape=[payload] * 8, in_specs=[SMEM, SMEM...  8.97 us
    pallas_call x1, Pallas kernels, body(): pl.pallas_call(first_kernel, out_shape=state, in_specs=[SMEM, SMEM, VMEM,...  8.13 us
    pallas_call x1, Pallas kernels, body(): pl.pallas_call(align_kernel, out_shape=[jax.ShapeDtypeStruct((frames, 128...  4.32 us
    ppermute x7, waiting for transfers between devices, body(): part = lax.ppermute(part, ('rec', 'vocab'), pairs)  3.76 us
  transfers between devices with their start and end apart: 24, of which 9 were waited for; matrix products, arithmetic and copies ran while one was open for 3% of the time, Pallas kernels for 32%

profile of v1, /device:TPU:1, one launch (start us, length us, event | category | flops | bytes accessed | tf_op | source)
XLA Modules:
  0.0 184.3 jit_solution(7070947880196372044)
XLA Ops:
  0.6 1.1 copy.10
  1.8 2.2 %collective-permute-start.3 = (bf16[128,1280]{1,0:T(8,128)(2,1)S(1)}, bf16[128,1280]{1,0:T(8,128)(2,1)S(1)}, u32[]{:S(2)}, u32[]{:S(2)}) collective-permute-start(bf16[128,1280]{1,0:T(8,128)(2,1)S(1)} %bitcast.32), channel_id=1, source_target_pairs={{0,32},{8,40},{16,48},{24,56},{32,64},{40,72},{48,80},{56,88},{64,... | collective-permute-start | bytes 983048 | tf_op jit(solution)/shard_map/ppermute | solution.py:249
  4.0 1.5 collective-permute-start.1
  5.5 4.4 %collective-permute-done.3 = bf16[128,1280]{1,0:T(8,128)(2,1)S(1)} collective-permute-done((bf16[128,1280]{1,0:T(8,128)(2,1)S(1)}, bf16[128,1280]{1,0:T(8,128)(2,1)S(1)}, u32[]{:S(2)}, u32[]{:S(2)}) %collective-permute-start.3) | collective-permute-done | bytes 327712 | tf_op jit(solution)/shard_map/ppermute | solution.py:249
  10.2 6.8 %collective-permute-done.4 = bf16[128,1280]{1,0:T(8,128)(2,1)S(1)} collective-permute-done((bf16[128,1280]{1,0:T(8,128)(2,1)S(1)}, bf16[128,1280]{1,0:T(8,128)(2,1)S(1)}, u32[]{:S(2)}, u32[]{:S(2)}) %collective-permute-start.4) | collective-permute-done | bytes 327712 | tf_op jit(solution)/shard_map/ppermute | solution.py:249
  17.0 1.2 pad_maximum_fusion.w
  18.2 1.6 collective-permute-start.8
  19.8 0.7 collective-permute-start.2
  20.5 4.3 %collective-permute-start.12 = (bf16[512,1280]{1,0:T(8,128)(2,1)}, bf16[512,1280]{1,0:T(8,128)(2,1)}, u32[]{:S(2)}, u32[]{:S(2)}) collective-permute-start(bf16[512,1280]{1,0:T(8,128)(2,1)} %pad_maximum_fusion.w), channel_id=1, source_target_pairs={{0,24},{8,0},{16,8},{24,16},{32,56},{40,32},{48,40},{56,48},{64,88... | collective-permute-start | bytes 3932168 | tf_op jit(solution)/shard_map/ppermute | solution.py:249
  24.8 14.7 %collective-permute-done.8.w = bf16[512,1280]{1,0:T(8,128)(2,1)S(1)} collective-permute-done((bf16[512,1280]{1,0:T(8,128)(2,1)}, bf16[512,1280]{1,0:T(8,128)(2,1)S(1)}, u32[]{:S(2)}, u32[]{:S(2)}) %collective-permute-start.8) | collective-permute-done | bytes 1310752 | tf_op jit(solution)/shard_map/ppermute | solution.py:249
  39.6 0.7 collective-permute-start.6
  40.3 0.7 collective-permute-start.5
  41.0 0.7 collective-permute-start.7
  41.9 1.3 collective-permute-done.12.w
  43.2 17.9 %collective-permute-done.9.w = bf16[512,1280]{1,0:T(8,128)(2,1)} collective-permute-done((bf16[512,1280]{1,0:T(8,128)(2,1)S(1)}, bf16[512,1280]{1,0:T(8,128)(2,1)}, u32[]{:S(2)}, u32[]{:S(2)}) %collective-permute-start.9) | collective-permute-done | bytes 1310752 | tf_op jit(solution)/shard_map/ppermute | solution.py:249
  61.2 3.0 %broadcast_select_fusion = (bf16[512,1280]{1,0:T(8,128)(2,1)}, bf16[512,1280]{1,0:T(8,128)(2,1)S(1)}) fusion(bf16[512,1280]{1,0:T(8,128)(2,1)S(1)} %constant_dynamic-update-slice_fusion.w0, bf16[512,1280]{1,0:T(8,128)(2,1)} %collective-permute-done.12.w, pred[]{:T(512)S(6)} %eq.82, bf16[512,1280]{1,0:T(8,128)(2,1)} %collective-permute-done.9.w), kind=kLoop, calls=%fused_computation.4 | loop fusion | flops 1310720 | bytes 6553601 | tf_op jit(solution)/shard_map/jit(_where)/select_n | solution.py:270
  64.5 1.0 collective-permute-start.16
  65.6 0.6 pad_add_fusion.1.where
  66.2 3.0 %collective-permute-done = s32[4,128]{1,0:T(4,128)S(1)} collective-permute-done((s32[4,128]{1,0:T(4,128)S(1)}, s32[4,128]{1,0:T(4,128)S(1)}, u32[]{:S(2)}, u32[]{:S(2)}) %collective-permute-start) | collective-permute-done | bytes 2080 | tf_op jit(solution)/shard_map/ppermute | solution.py:257
  69.3 0.6 collective-permute-start.10
  69.8 11.4 %collective-permute-done.13.w = bf16[512,1280]{1,0:T(8,128)(2,1)} collective-permute-done((bf16[512,1280]{1,0:T(8,128)(2,1)}, bf16[512,1280]{1,0:T(8,128)(2,1)}, u32[]{:S(2)}, u32[]{:S(2)}) %collective-permute-start.13) | collective-permute-done | bytes 1310752 | tf_op jit(solution)/shard_map/ppermute | solution.py:249
  81.2 1.6 collective-permute-start.14
  82.9 0.6 convert_reduce_fusion.1.bounds
  83.6 0.6 convert_reduce_fusion
  84.1 1.3 select_reduce_fusion.entries
  85.4 8.1 %shard_map.86 = (f32[6,8,256]{2,1,0:T(8,128)}, f32[6,8,256]{2,1,0:T(8,128)}, f32[2,1024,128]{2,1,0:T(8,128)}) custom-call(s32[16]{0:T(128)} %convert_reduce_fusion.1.bounds, s32[1024]{0:T(1024)} %select_reduce_fusion.entries, bf16[512,1280]{1,0:T(8,128)(2,1)} %pad_maximum_fusion.w, bf16[3,256,1280]{2,1,0:T(8,128)(2,1)} %bitcast.24, ...), custom_call_target="tpu_custom_call" | custom-call | flops 2013265920 | bytes 8000000 | tf_op jit(solution)/shard_map/pallas_call | solution.py:289
  93.5 8.5 %shard_map.87 = (f32[6,8,256]{2,1,0:T(8,128)}, f32[6,8,256]{2,1,0:T(8,128)}, f32[2,1024,128]{2,1,0:T(8,128)}) custom-call(s32[16]{0:T(128)} %convert_reduce_fusion.1.bounds, s32[1024]{0:T(1024)} %select_reduce_fusion.entries, bf16[512,1280]{1,0:T(8,128)(2,1)} %copy-done.14, bf16[3,256,1280]{2,1,0:T(8,128)(2,1)} %bitcast.25, ...), custom_call_target="tpu_custom_call" | custom-call | flops 2013265920 | bytes 8000000 | tf_op jit(solution)/shard_map/pallas_call | solution.py:298
  102.0 8.5 %shard_map.88 = (f32[6,8,256]{2,1,0:T(8,128)}, f32[6,8,256]{2,1,0:T(8,128)}, f32[2,1024,128]{2,1,0:T(8,128)}) custom-call(s32[16]{0:T(128)} %convert_reduce_fusion.1.bounds, s32[1024]{0:T(1024)} %select_reduce_fusion.entries, bf16[512,1280]{1,0:T(8,128)(2,1)} %collective-permute-done.12.w, bf16[3,256,1280]{2,1,0:T(8,128)(2,1)} %bitcast.26, ...), custom_call_target="tpu_custom_call" | custom-call | flops 2013265920 | bytes 8000000 | tf_op jit(solution)/shard_map/pallas_call | solution.py:298
  110.5 1.1 slice.12
  111.7 2.1 %collective-permute-start.11 = (bf16[256,1280]{1,0:T(8,128)(2,1)S(1)}, bf16[256,1280]{1,0:T(8,128)(2,1)S(1)}, u32[]{:S(2)}, u32[]{:S(2)}) collective-permute-start(bf16[256,1280]{1,0:T(8,128)(2,1)S(1)} %slice.12), channel_id=1, source_target_pairs={{4,36},{12,44},{20,52},{28,60},{36,68},{44,76},{52,84},{60,92},{68... | collective-permute-start | bytes 1966088 | tf_op jit(solution)/shard_map/ppermute | solution.py:249
  113.8 1.1 slice.13
  114.9 4.6 %collective-permute-start.15 = (bf16[256,1280]{1,0:T(8,128)(2,1)S(1)}, bf16[256,1280]{1,0:T(8,128)(2,1)S(1)}, u32[]{:S(2)}, u32[]{:S(2)}) collective-permute-start(bf16[256,1280]{1,0:T(8,128)(2,1)S(1)} %slice.13), channel_id=1, source_target_pairs={{4,228},{12,236},{20,244},{28,252},{36,4},{44,12},{52,20},{60,28},... | collective-permute-start | bytes 1966088 | tf_op jit(solution)/shard_map/ppermute | solution.py:249
  119.5 8.6 %shard_map.89 = (f32[6,8,256]{2,1,0:T(8,128)}, f32[6,8,256]{2,1,0:T(8,128)}, f32[2,1024,128]{2,1,0:T(8,128)}) custom-call(s32[16]{0:T(128)} %convert_reduce_fusion.1.bounds, s32[1024]{0:T(1024)} %select_reduce_fusion.entries, bf16[512,1280]{1,0:T(8,128)(2,1)} %collective-permute-done.9.w, bf16[3,256,1280]{2,1,0:T(8,128)(2,1)} %bitcast.27, ...), custom_call_target="tpu_custom_call" | custom-call | flops 2013265920 | bytes 8000000 | tf_op jit(solution)/shard_map/pallas_call | solution.py:298
  128.1 8.4 %shard_map.90 = (f32[6,8,256]{2,1,0:T(8,128)}, f32[6,8,256]{2,1,0:T(8,128)}, f32[2,1024,128]{2,1,0:T(8,128)}) custom-call(s32[16]{0:T(128)} %convert_reduce_fusion.1.bounds, s32[1024]{0:T(1024)} %select_reduce_fusion.entries, bf16[512,1280]{1,0:T(8,128)(2,1)} %collective-permute-done.10.w, bf16[3,256,1280]{2,1,0:T(8,128)(2,1)} %bitcast.28, ...), custom_call_target="tpu_custom_call" | custom-call | flops 2013265920 | bytes 8000000 | tf_op jit(solution)/shard_map/pallas_call | solution.py:298
  136.5 8.3 %shard_map.91 = (f32[6,8,256]{2,1,0:T(8,128)}, f32[6,8,256]{2,1,0:T(8,128)}, f32[2,1024,128]{2,1,0:T(8,128)}) custom-call(s32[16]{0:T(128)} %convert_reduce_fusion.1.bounds, s32[1024]{0:T(1024)} %select_reduce_fusion.entries, bf16[512,1280]{1,0:T(8,128)(2,1)} %collective-permute-done.13.w, bf16[3,256,1280]{2,1,0:T(8,128)(2,1)} %bitcast.29, ...), custom_call_target="tpu_custom_call" | custom-call | flops 2013265920 | bytes 8000000 | tf_op jit(solution)/shard_map/pallas_call | solution.py:298
  144.8 8.6 %shard_map.92 = (f32[6,8,256]{2,1,0:T(8,128)}, f32[6,8,256]{2,1,0:T(8,128)}, f32[2,1024,128]{2,1,0:T(8,128)}) custom-call(s32[16]{0:T(128)} %convert_reduce_fusion.1.bounds, s32[1024]{0:T(1024)} %select_reduce_fusion.entries, bf16[512,1280]{1,0:T(8,128)(2,1)} %collective-permute-done.14.w, bf16[3,256,1280]{2,1,0:T(8,128)(2,1)} %bitcast.30, ...), custom_call_target="tpu_custom_call" | custom-call | flops 2013265920 | bytes 8000000 | tf_op jit(solution)/shard_map/pallas_call | solution.py:298
  153.5 0.8 copy-done.2
  154.5 9.0 %shard_map.93 = (bf16[144,256]{1,0:T(8,128)(2,1)}, bf16[144,256]{1,0:T(8,128)(2,1)}, bf16[144,256]{1,0:T(8,128)(2,1)}, bf16[144,256]{1,0:T(8,128)(2,1)}, bf16[14...) custom-call(s32[2]{0:T(128)} %pad_add_fusion.1.where, ...), custom_call_target="tpu_custom_call" | custom-call | flops 2013265920 | bytes 8000000 | tf_op jit(solution)/shard_map/pallas_call | solution.py:307
  163.5 1.1 collective-permute-start.17
  164.6 3.6 %collective-permute-start.18 = (bf16[144,256]{1,0:T(8,128)(2,1)}, bf16[144,256]{1,0:T(8,128)(2,1)S(1)}, u32[]{:S(2)}, u32[]{:S(2)}) collective-permute-start(bf16[144,256]{1,0:T(8,128)(2,1)} %get-tuple-element.56), channel_id=1, source_target_pairs={{0,2},{1,3},{2,0},{3,1},{4,6},{5,7},{6,4},{7,5},{8,10},{9,11},{10,... | collective-permute-start | bytes 221192 | tf_op jit(solution)/shard_map/ppermute | solution.py:334
  169.5 0.8 collective-permute-start.19
  170.3 1.1 collective-permute-start.21
  171.4 0.5 collective-permute-start.22
  171.9 1.8 collective-permute-start.23
  173.8 0.6 pad_add_fusion.lengths
  174.4 3.4 %collective-permute-done.21.refs_5_ = bf16[144,256]{1,0:T(8,128)(2,1)S(1)} collective-permute-done((bf16[144,256]{1,0:T(8,128)(2,1)}, bf16[144,256]{1,0:T(8,128)(2,1)S(1)}, u32[]{:S(2)}, u32[]{:S(2)}) %collective-permute-start.21) | collective-permute-done | bytes 73760 | tf_op jit(solution)/shard_map/ppermute | solution.py:334
  178.8 4.3 %shard_map.94 = (f32[192,128]{1,0:T(8,128)}, f32[8,128]{1,0:T(8,128)}) custom-call(s32[2]{0:T(128)} %pad_add_fusion.lengths, bf16[144,256]{1,0:T(8,128)(2,1)} %get-tuple-element.54.refs_0_, bf16[144,256]{1,0:T(8,128)(2,1)} %copy-done.4, bf16[144,256]{1,0:T(8,128)(2,1)} %copy-done.5, bf16[144,256]{1,0:T(8,128)(2,1)} %copy-done.6, bf16[144,256]{1,0:T(8,128)(2,1)} %copy-done.7, ...), custom_call_target="tpu_custom_call" | custom-call | tf_op jit(solution)/shard_map/pallas_call | solution.py:336
  183.1 1.2 slice.11
  (58 shorter events, 2.3 us)
Async XLA Ops:
  1.8 8.1 %collective-permute-start.3 = (bf16[128,1280]{1,0:T(8,128)(2,1)S(1)}, bf16[128,1280]{1,0:T(8,128)(2,1)S(1)}, u32[]{:S(2)}, u32[]{:S(2)}) collective-permute-start(bf16[128,1280]{1,0:T(8,128)(2,1)S(1)} %bitcast.32), channel_id=1, source_target_pairs={{0,32},{8,40},{16,48},{24,56},{32,64},{40,72},{48,80},{56,88},{64,... | collective-permute-start | bytes 983048 | tf_op jit(solution)/shard_map/ppermute | solution.py:249
  4.0 6.2 %collective-permute-start.1 = (bf16[128,1280]{1,0:T(8,128)(2,1)S(1)}, bf16[128,1280]{1,0:T(8,128)(2,1)S(1)}, u32[]{:S(2)}, u32[]{:S(2)}) collective-permute-start(bf16[128,1280]{1,0:T(8,128)(2,1)S(1)} %bitcast.33), channel_id=1, source_target_pairs={{0,224},{8,232},{16,240},{24,248},{32,0},{40,8},{48,16},{56,24},{6... | collective-permute-start | bytes 983048 | tf_op jit(solution)/shard_map/ppermute | solution.py:249
  9.9 7.1 %collective-permute-start.4 = (bf16[128,1280]{1,0:T(8,128)(2,1)S(1)}, bf16[128,1280]{1,0:T(8,128)(2,1)S(1)}, u32[]{:S(2)}, u32[]{:S(2)}) collective-permute-start(bf16[128,1280]{1,0:T(8,128)(2,1)S(1)} %collective-permute-done.3), channel_id=1, source_target_pairs={{0,32},{8,40},{16,48},{24,56},{32,64},{40,72},{48,80},{56,88},{64,... | collective-permute-start | bytes 983048 | tf_op jit(solution)/shard_map/ppermute | solution.py:249
  18.2 21.4 %collective-permute-start.8 = (bf16[512,1280]{1,0:T(8,128)(2,1)}, bf16[512,1280]{1,0:T(8,128)(2,1)S(1)}, u32[]{:S(2)}, u32[]{:S(2)}) collective-permute-start(bf16[512,1280]{1,0:T(8,128)(2,1)} %pad_maximum_fusion.w), channel_id=1, source_target_pairs={{0,8},{8,16},{16,24},{24,0},{32,40},{40,48},{48,56},{56,32},{64,72... | collective-permute-start | bytes 3932168 | tf_op jit(solution)/shard_map/ppermute | solution.py:249
  19.8 19.7 %collective-permute-start.2 = (bf16[128,1280]{1,0:T(8,128)(2,1)S(1)}, bf16[128,1280]{1,0:T(8,128)(2,1)S(1)}, u32[]{:S(2)}, u32[]{:S(2)}) collective-permute-start(bf16[128,1280]{1,0:T(8,128)(2,1)S(1)} %collective-permute-done.1), channel_id=1, source_target_pairs={{0,224},{8,232},{16,240},{24,248},{32,0},{40,8},{48,16},{56,24},{6... | collective-permute-start | bytes 983048 | tf_op jit(solution)/shard_map/ppermute | solution.py:249
  20.5 22.7 %collective-permute-start.12 = (bf16[512,1280]{1,0:T(8,128)(2,1)}, bf16[512,1280]{1,0:T(8,128)(2,1)}, u32[]{:S(2)}, u32[]{:S(2)}) collective-permute-start(bf16[512,1280]{1,0:T(8,128)(2,1)} %pad_maximum_fusion.w), channel_id=1, source_target_pairs={{0,24},{8,0},{16,8},{24,16},{32,56},{40,32},{48,40},{56,48},{64,88... | collective-permute-start | bytes 3932168 | tf_op jit(solution)/shard_map/ppermute | solution.py:249
  39.6 2.3 %copy-start.14 = (bf16[512,1280]{1,0:T(8,128)(2,1)}, bf16[512,1280]{1,0:T(8,128)(2,1)S(1)}, u32[]{:S(2)}) copy-start(bf16[512,1280]{1,0:T(8,128)(2,1)S(1)} %collective-permute-done.8.w) | copy-start | bytes 3932164
  39.6 21.6 %collective-permute-start.9 = (bf16[512,1280]{1,0:T(8,128)(2,1)S(1)}, bf16[512,1280]{1,0:T(8,128)(2,1)}, u32[]{:S(2)}, u32[]{:S(2)}) collective-permute-start(bf16[512,1280]{1,0:T(8,128)(2,1)S(1)} %collective-permute-done.8.w), channel_id=1, source_target_pairs={{0,8},{8,16},{16,24},{24,0},{32,40},{40,48},{48,56},{56,32},{64,72... | collective-permute-start | bytes 3932168 | tf_op jit(solution)/shard_map/ppermute | solution.py:249
  39.6 1.4 collective-permute-start.6
  40.3 1.4 collective-permute-start.5
  41.0 0.8 collective-permute-start.7
  41.8 22.3 %copy-start = (bf16[512,1280]{1,0:T(8,128)(2,1)}, bf16[512,1280]{1,0:T(8,128)(2,1)S(1)}, u32[]{:S(2)}) copy-start(bf16[512,1280]{1,0:T(8,128)(2,1)S(1)} %constant_dynamic-update-slice_fusion.w0) | copy-start | bytes 3932164
  41.8 22.7 %copy-start.1 = (bf16[4,192,1280]{2,1,0:T(8,128)(2,1)S(1)}, bf16[4,192,1280]{2,1,0:T(8,128)(2,1)}, u32[]{:S(2)}) copy-start(bf16[4,192,1280]{2,1,0:T(8,128)(2,1)} %param.7) | copy-start | bytes 5898244
  41.9 23.6 %copy-start.11 = (s32[4,128]{1,0:T(4,128)S(1)}, s32[4,128]{1,0:T(4,128)}, u32[]{:S(2)}) copy-start(s32[4,128]{1,0:T(4,128)} %param.9) | copy-start | bytes 6148
  41.9 23.7 %copy-start.12 = (s32[32]{0:T(128)S(1)}, s32[32]{0:T(128)}, u32[]{:S(2)}) copy-start(s32[32]{0:T(128)} %constant.156.clone) | copy-start | bytes 388
  41.9 23.7 %copy-start.13 = (s32[32]{0:T(128)S(1)}, s32[32]{0:T(128)}, u32[]{:S(2)}) copy-start(s32[32]{0:T(128)} %constant.157.clone) | copy-start | bytes 388
  64.2 17.1 %collective-permute-start.13 = (bf16[512,1280]{1,0:T(8,128)(2,1)}, bf16[512,1280]{1,0:T(8,128)(2,1)}, u32[]{:S(2)}, u32[]{:S(2)}) collective-permute-start(bf16[512,1280]{1,0:T(8,128)(2,1)} %get-tuple-element.66), channel_id=1, source_target_pairs={{0,24},{8,0},{16,8},{24,16},{32,56},{40,32},{48,40},{56,48},{64,88... | collective-permute-start | bytes 3932168 | tf_op jit(solution)/shard_map/ppermute | solution.py:249
  64.5 20.9 %collective-permute-start.16 = (bf16[4,192,1280]{2,1,0:T(8,128)(2,1)S(1)}, bf16[4,192,1280]{2,1,0:T(8,128)(2,1)}, u32[]{:S(2)}, u32[]{:S(2)}) collective-permute-start(bf16[4,192,1280]{2,1,0:T(8,128)(2,1)S(1)} %copy-done.1), channel_id=1, source_target_pairs={{0,4},{8,12},{16,20},{24,28},{32,36},{40,44},{48,52},{56,60},{64,6... | collective-permute-start | bytes 5898248 | tf_op jit(solution)/shard_map/ppermute | solution.py:256
  65.5 3.7 %collective-permute-start = (s32[4,128]{1,0:T(4,128)S(1)}, s32[4,128]{1,0:T(4,128)S(1)}, u32[]{:S(2)}, u32[]{:S(2)}) collective-permute-start(s32[4,128]{1,0:T(4,128)S(1)} %copy-done.11), channel_id=1, source_target_pairs={{0,4},{8,12},{16,20},{24,28},{32,36},{40,44},{48,52},{56,60},{64,6... | collective-permute-start | bytes 6152 | tf_op jit(solution)/shard_map/ppermute | solution.py:257
  69.3 41.3 %collective-permute-start.10 = (bf16[512,1280]{1,0:T(8,128)(2,1)S(1)}, bf16[512,1280]{1,0:T(8,128)(2,1)}, u32[]{:S(2)}, u32[]{:S(2)}) collective-permute-start(bf16[512,1280]{1,0:T(8,128)(2,1)S(1)} %get-tuple-element.67), channel_id=1, source_target_pairs={{0,8},{8,16},{16,24},{24,0},{32,40},{40,48},{48,56},{56,32},{64,72... | collective-permute-start | bytes 3932168 | tf_op jit(solution)/shard_map/ppermute | solution.py:249
  81.2 32.6 %collective-permute-start.14 = (bf16[512,1280]{1,0:T(8,128)(2,1)}, bf16[512,1280]{1,0:T(8,128)(2,1)}, u32[]{:S(2)}, u32[]{:S(2)}) collective-permute-start(bf16[512,1280]{1,0:T(8,128)(2,1)} %collective-permute-done.13.w), channel_id=1, source_target_pairs={{0,24},{8,0},{16,8},{24,16},{32,56},{40,32},{48,40},{56,48},{64,88... | collective-permute-start | bytes 3932168 | tf_op jit(solution)/shard_map/ppermute | solution.py:249
  111.7 41.7 %collective-permute-start.11 = (bf16[256,1280]{1,0:T(8,128)(2,1)S(1)}, bf16[256,1280]{1,0:T(8,128)(2,1)S(1)}, u32[]{:S(2)}, u32[]{:S(2)}) collective-permute-start(bf16[256,1280]{1,0:T(8,128)(2,1)S(1)} %slice.12), channel_id=1, source_target_pairs={{4,36},{12,44},{20,52},{28,60},{36,68},{44,76},{52,84},{60,92},{68... | collective-permute-start | bytes 1966088 | tf_op jit(solution)/shard_map/ppermute | solution.py:249
  114.9 38.5 %collective-permute-start.15 = (bf16[256,1280]{1,0:T(8,128)(2,1)S(1)}, bf16[256,1280]{1,0:T(8,128)(2,1)S(1)}, u32[]{:S(2)}, u32[]{:S(2)}) collective-permute-start(bf16[256,1280]{1,0:T(8,128)(2,1)S(1)} %slice.13), channel_id=1, source_target_pairs={{4,228},{12,236},{20,244},{28,252},{36,4},{44,12},{52,20},{60,28},... | collective-permute-start | bytes 1966088 | tf_op jit(solution)/shard_map/ppermute | solution.py:249
  153.4 0.8 copy-start.2
  153.5 1.1 copy-start.3
  163.5 7.9 %collective-permute-start.17 = (bf16[144,256]{1,0:T(8,128)(2,1)}, bf16[144,256]{1,0:T(8,128)(2,1)S(1)}, u32[]{:S(2)}, u32[]{:S(2)}) collective-permute-start(bf16[144,256]{1,0:T(8,128)(2,1)} %get-tuple-element.55), channel_id=1, source_target_pairs={{0,1},{1,2},{2,3},{3,0},{4,5},{5,6},{6,7},{7,4},{8,9},{9,10},{10,1... | collective-permute-start | bytes 221192 | tf_op jit(solution)/shard_map/ppermute | solution.py:334
  164.6 7.4 %collective-permute-start.18 = (bf16[144,256]{1,0:T(8,128)(2,1)}, bf16[144,256]{1,0:T(8,128)(2,1)S(1)}, u32[]{:S(2)}, u32[]{:S(2)}) collective-permute-start(bf16[144,256]{1,0:T(8,128)(2,1)} %get-tuple-element.56), channel_id=1, source_target_pairs={{0,2},{1,3},{2,0},{3,1},{4,6},{5,7},{6,4},{7,5},{8,10},{9,11},{10,... | collective-permute-start | bytes 221192 | tf_op jit(solution)/shard_map/ppermute | solution.py:334
  169.5 4.9 %collective-permute-start.19 = (bf16[144,256]{1,0:T(8,128)(2,1)}, bf16[144,256]{1,0:T(8,128)(2,1)S(1)}, u32[]{:S(2)}, u32[]{:S(2)}) collective-permute-start(bf16[144,256]{1,0:T(8,128)(2,1)} %get-tuple-element.57), channel_id=1, source_target_pairs={{0,3},{1,0},{2,1},{3,2},{4,7},{5,4},{6,5},{7,6},{8,11},{9,8},{10,9... | collective-permute-start | bytes 221192 | tf_op jit(solution)/shard_map/ppermute | solution.py:334
  170.3 4.1 %collective-permute-start.20 = (bf16[144,256]{1,0:T(8,128)(2,1)}, bf16[144,256]{1,0:T(8,128)(2,1)S(1)}, u32[]{:S(2)}, u32[]{:S(2)}) collective-permute-start(bf16[144,256]{1,0:T(8,128)(2,1)} %get-tuple-element.58), channel_id=1, source_target_pairs={{0,4},{1,5},{2,6},{3,7},{4,0},{5,1},{6,2},{7,3},{8,12},{9,13},{10,... | collective-permute-start | bytes 221192 | tf_op jit(solution)/shard_map/ppermute | solution.py:334
  170.3 7.5 %collective-permute-start.21 = (bf16[144,256]{1,0:T(8,128)(2,1)}, bf16[144,256]{1,0:T(8,128)(2,1)S(1)}, u32[]{:S(2)}, u32[]{:S(2)}) collective-permute-start(bf16[144,256]{1,0:T(8,128)(2,1)} %get-tuple-element.59), channel_id=1, source_target_pairs={{0,5},{1,6},{2,7},{3,4},{4,1},{5,2},{6,3},{7,0},{8,13},{9,14},{10,... | collective-permute-start | bytes 221192 | tf_op jit(solution)/shard_map/ppermute | solution.py:334
  171.4 6.8 %copy-start.4 = (bf16[144,256]{1,0:T(8,128)(2,1)}, bf16[144,256]{1,0:T(8,128)(2,1)S(1)}, u32[]{:S(2)}) copy-start(bf16[144,256]{1,0:T(8,128)(2,1)S(1)} %collective-permute-done.17.refs_1_) | copy-start | bytes 221188
  171.4 6.4 %collective-permute-start.22 = (bf16[144,256]{1,0:T(8,128)(2,1)}, bf16[144,256]{1,0:T(8,128)(2,1)S(1)}, u32[]{:S(2)}, u32[]{:S(2)}) collective-permute-start(bf16[144,256]{1,0:T(8,128)(2,1)} %get-tuple-element.60), channel_id=1, source_target_pairs={{0,6},{1,7},{2,4},{3,5},{4,2},{5,3},{6,0},{7,1},{8,14},{9,15},{10,... | collective-permute-start | bytes 221192 | tf_op jit(solution)/shard_map/ppermute | solution.py:334
  171.9 6.2 %copy-start.5 = (bf16[144,256]{1,0:T(8,128)(2,1)}, bf16[144,256]{1,0:T(8,128)(2,1)S(1)}, u32[]{:S(2)}) copy-start(bf16[144,256]{1,0:T(8,128)(2,1)S(1)} %collective-permute-done.18.refs_2_) | copy-start | bytes 221188
  171.9 6.2 %collective-permute-start.23 = (bf16[144,256]{1,0:T(8,128)(2,1)}, bf16[144,256]{1,0:T(8,128)(2,1)S(1)}, u32[]{:S(2)}, u32[]{:S(2)}) collective-permute-start(bf16[144,256]{1,0:T(8,128)(2,1)} %get-tuple-element.61), channel_id=1, source_target_pairs={{0,7},{1,4},{2,5},{3,6},{4,3},{5,0},{6,1},{7,2},{8,15},{9,12},{10,... | collective-permute-start | bytes 221192 | tf_op jit(solution)/shard_map/ppermute | solution.py:334
  174.4 3.8 %copy-start.6 = (bf16[144,256]{1,0:T(8,128)(2,1)}, bf16[144,256]{1,0:T(8,128)(2,1)S(1)}, u32[]{:S(2)}) copy-start(bf16[144,256]{1,0:T(8,128)(2,1)S(1)} %collective-permute-done.19.refs_3_) | copy-start | bytes 221188
  174.4 3.8 %copy-start.7 = (bf16[144,256]{1,0:T(8,128)(2,1)}, bf16[144,256]{1,0:T(8,128)(2,1)S(1)}, u32[]{:S(2)}) copy-start(bf16[144,256]{1,0:T(8,128)(2,1)S(1)} %collective-permute-done.20.refs_4_) | copy-start | bytes 221188
  177.8 0.7 copy-start.8
  177.8 0.7 copy-start.9
  178.1 0.6 copy-start.10

commit v2 on v1

v2 whole, which is shorter than its diff:
```python
import functools

import jax
import jax.numpy as jnp
import numpy as np
from jax import lax
from jax.experimental import pallas as pl
from jax.experimental.pallas import tpu as pltpu
from jax.sharding import PartitionSpec as P

negative_fill = -1e30
NZ, NY = 8, 4
TILE = 256
BLOCK = 512
PAIRS = 4
WINDOWS = 12
EARLY = 512
ANY = pl.BlockSpec(memory_space=pl.ANY)
VMEM = pl.BlockSpec(memory_space=pltpu.VMEM)
SMEM = pl.BlockSpec(memory_space=pltpu.SMEM)
LOWEST = -3.0e38


def rec_index(z, y, core):
    return ((z % NZ) * NY + y % NY) * 2 + core


def moves(step0=None, step1=None):
    pairs = []
    for core, step in ((0, step0), (1, step1)):
        if step is None:
            continue
        for z in range(NZ):
            for y in range(NY):
                pairs.append((rec_index(z, y, core), rec_index(*step(z, y, core))))
    return pairs


def other_core(z, y, core):
    return z, y, 1 - core


def up(z, y, core):
    return z + 1, y, core


def down(z, y, core):
    return z - 1, y, core


def mirror(z, y, core):
    return z, 3 - y, core


def beside(z, y, core):
    return z, y ^ 1, core


def place_table():
    table = np.full((2, 2 * NZ), 2 * PAIRS, np.int32)
    order0 = [(-1, 0), (-2, 0), (-1, 1), (-3, 0), (-4, 0), (-2, 1), (-3, 1), (-4, 1)]
    order1 = [(1, 0), (2, 0), (1, 1), (3, 0), (2, 1), (0, 0), (3, 1), (0, 1)]
    for core, order in ((0, order0), (1, order1)):
        for place, (dz, far) in enumerate(order):
            table[core, far * NZ + dz % NZ] = place
    return table


def score_tiles(w_ref, pair, f_ref, first_tile, l_ref, m_ref, s_ref):
    def step(t, _):
        rows = f_ref[pl.ds(pl.multiple_of(t * TILE, TILE), TILE), :]
        tile = lax.dot_general(
            w_ref[pair], rows, (((1,), (1,)), ((), ())), preferred_element_type=jnp.float32
        )
        at = first_tile + t
        l_ref[2 * at] = tile[:, :128]
        l_ref[2 * at + 1] = tile[:, 128:]
        cube = tile.reshape(BLOCK // 8, 8, TILE)
        old = m_ref[at]
        top = jnp.maximum(jnp.max(cube, 0), old)
        s_ref[at] = s_ref[at] * jnp.exp(old - top) + jnp.sum(jnp.exp(cube - top[None]), 0)
        m_ref[at] = top
        return 0

    lax.fori_loop(0, f_ref.shape[0] // TILE, step, 0)


def take_rows(pair, which, bounds, entries, l_ref, p_ref, early=None):
    def one(k, _):
        entry = entries[which, k]
        row = entry // 1024
        item = entry % 1024
        for side in range(2):
            window = (item // 128) * 3 // 2 + side

            def copy(window=window, side=side):
                p_ref[side, pl.ds(item, 1), :] = l_ref[window, pl.ds(row, 1), :]

            if early is None:
                copy()
            else:
                inside = window % (WINDOWS // 2) < EARLY // 128
                pl.when(inside if early else jnp.logical_not(inside))(copy)
        return 0

    lax.fori_loop(bounds[which, pair], bounds[which, pair + 1], one, 0)


def fill_pair(w_ref, pair, one, two):
    w_ref[pair, 0 : BLOCK // 2] = one[...]
    w_ref[pair, BLOCK // 2 : BLOCK] = two[...]


def first_kernel(bounds, entries, one, two, fa, fb, m, s, p, w_ref, l_ref):
    m[...] = jnp.full_like(m, LOWEST)
    s[...] = jnp.zeros_like(s)
    p[...] = jnp.zeros_like(p)
    fill_pair(w_ref, 0, one, two)
    score_tiles(w_ref, 0, fa, 0, l_ref, m, s)
    score_tiles(w_ref, 0, fb, 3, l_ref, m, s)
    take_rows(0, 0, bounds, entries, l_ref, p)


def second_kernel(bounds, entries, one, two, fa, fb, m_in, s_in, p_in, m, s, p, w_ref, l_ref):
    m[...] = m_in[...]
    s[...] = s_in[...]
    p[...] = p_in[...]
    fill_pair(w_ref, 0, one, two)
    score_tiles(w_ref, 0, fa, 0, l_ref, m, s)
    score_tiles(w_ref, 0, fb, 3, l_ref, m, s)
    take_rows(1, 0, bounds, entries, l_ref, p)


def third_kernel(bounds, entries, *refs):
    blocks, (fa, fb, ga, gb, m_in, s_in, p_in), (m, s, p, mb, sb, pb, w_ref, l_ref) = refs[:6], refs[6:13], refs[13:]
    m[...] = m_in[...]
    s[...] = s_in[...]
    p[...] = p_in[...]
    mb[...] = jnp.full_like(mb, LOWEST)
    sb[...] = jnp.zeros_like(sb)
    pb[...] = jnp.zeros_like(pb)
    for pair in range(3):
        fill_pair(w_ref, pair, *blocks[2 * pair : 2 * pair + 2])
    score_tiles(w_ref, 2, fa, 0, l_ref, m, s)
    score_tiles(w_ref, 2, fb, 3, l_ref, m, s)
    take_rows(2, 0, bounds, entries, l_ref, p)

    def over(pair, _):
        score_tiles(w_ref, pair, ga, 0, l_ref, mb, sb)
        score_tiles(w_ref, pair, gb, 3, l_ref, mb, sb)
        take_rows(pair, 1, bounds, entries, l_ref, pb, True)
        return 0

    lax.fori_loop(0, 3, over, 0)


def split_parts(value):
    high = value.astype(jnp.bfloat16).astype(jnp.float32)
    middle = (value - high).astype(jnp.bfloat16).astype(jnp.float32)
    low = value - high - middle
    line = lax.broadcasted_iota(jnp.int32, value.shape, 0)
    parts = jnp.where(line == 0, high, jnp.where(line == 1, middle, jnp.where(line == 2, low, 0.0)))
    return jnp.concatenate([parts, jnp.zeros_like(parts)], 0).astype(jnp.bfloat16)


def joined_parts(lines):
    lines = lines.astype(jnp.float32)
    return lines[0:1] + lines[1:2] + lines[2:3]


def last_kernel(bounds, entries, *refs):
    blocks, (fa, fb, ga, gb, ha, hb), state, (kept, given) = refs[:8], refs[8:14], refs[14:20], refs[20:22]
    m, s, p, mb, sb, pb, lse_ref, w_ref, l_ref = refs[22:]
    for ref, value in zip((m, s, p, mb, sb, pb), state):
        ref[...] = value[...]
    for pair in range(PAIRS):
        fill_pair(w_ref, pair, *blocks[2 * pair : 2 * pair + 2])

    def over(pair, _):
        score_tiles(w_ref, pair, ha, 2, l_ref, mb, sb)
        score_tiles(w_ref, pair, hb, 5, l_ref, mb, sb)
        take_rows(pair, 1, bounds, entries, l_ref, pb, False)
        return 0

    lax.fori_loop(0, PAIRS, over, 0)
    score_tiles(w_ref, 3, ga, 0, l_ref, mb, sb)
    score_tiles(w_ref, 3, gb, 3, l_ref, mb, sb)
    take_rows(3, 1, bounds, entries, l_ref, pb, True)
    score_tiles(w_ref, 3, fa, 0, l_ref, m, s)
    score_tiles(w_ref, 3, fb, 3, l_ref, m, s)
    take_rows(3, 0, bounds, entries, l_ref, p)
    for group, (mm, ss, pp) in enumerate(((m, s, p), (mb, sb, pb))):
        for t in range(WINDOWS // 2):
            top = jnp.max(mm[t], 0, keepdims=True)
            total = jnp.sum(ss[t] * jnp.exp(mm[t] - top), 0, keepdims=True)
            value = jnp.broadcast_to(top + jnp.log(total), (8, TILE))
            lse_ref[2 * t] = value[:, :128]
            lse_ref[2 * t + 1] = value[:, 128:]
        for half, out in enumerate((kept, given)):
            for k in range(4):
                rec = half * 4 + k
                shift = 64 * (rec % 2)
                rows = jnp.concatenate([pp[0, rec * 128 : rec * 128 + 128, :], pp[1, rec * 128 : rec * 128 + 128, :]], 1)
                window = rec * 3 // 2
                value = jnp.concatenate([lse_ref[window], lse_ref[window + 1]], 1)
                if shift:
                    rows = pltpu.roll(rows, TILE - shift, 1)
                    value = pltpu.roll(value, TILE - shift, 1)
                out[group * 4 + k, 0:128, :] = rows.astype(jnp.bfloat16)
                out[group * 4 + k, 128:144, :] = split_parts(value)


def join_kernel(where, mine, theirs, *outs):
    place = where[0]
    for group in range(2):
        for step in range(4):
            rec = group * 4 + (place + step) % 4
            out = outs[group * 4 + step]
            one, two = mine[rec], theirs[rec]
            picked = one[0:128].astype(jnp.float32) + two[0:128].astype(jnp.float32)
            out[0:128, :] = picked.astype(jnp.bfloat16)
            a, b = joined_parts(one[128:144]), joined_parts(two[128:144])
            top = jnp.maximum(a, b)
            value = top + jnp.log(jnp.exp(a - top) + jnp.exp(b - top))
            out[128:144, :] = split_parts(jnp.broadcast_to(value, (8, TILE)))


DEPTH = 8


def align_kernel(lengths, *refs):
    parts, (logprob, path, turned, scores) = refs[:8], refs[8:]
    frames = logprob.shape[0]
    picked = parts[0][0:128, :].astype(jnp.float32)
    for part in parts[1:]:
        picked = picked + part[0:128, :].astype(jnp.float32)
    norms = []
    for part in parts:
        norms.append(joined_parts(part[128:144, :]))
    top = functools.reduce(jnp.maximum, norms)
    norm = top + jnp.log(sum(jnp.exp(value - top) for value in norms))
    table = (picked - norm).T[:frames]
    logprob[...] = table
    lanes = lax.broadcasted_iota(jnp.int32, (1, 128), 1)
    for d in range(DEPTH):
        turned[d] = table if d == 0 else pltpu.roll(table, d, 1)

    def advance(score, first, count):
        copies = [score] + [jnp.where(lanes < d, negative_fill, pltpu.roll(score, d, 1)) for d in range(1, count + 1)]
        for i in range(count):
            for d in range(count - i):
                emitted = turned[d, pl.ds(first + i, 1), :]
                copies[d] = jnp.maximum(copies[d], copies[d + 1]) + emitted
            scores[pl.ds(first + i, 1), :] = copies[0]
        return copies[0]

    score = jnp.where(lanes == 0, table[0:1], negative_fill)
    scores[0:1, :] = score
    score = advance(score, 1, DEPTH - 1)
    lax.fori_loop(1, frames // DEPTH, lambda b, now: advance(now, pl.multiple_of(b * DEPTH, DEPTH), DEPTH), score)
    final = scores[pl.ds(lengths[0] - 1, 1), :]
    hit = jnp.sum(jnp.where(lanes == lengths[1] - 1, final, 0.0), 1, keepdims=True)
    path[...] = jnp.broadcast_to(hit, path.shape)


def label_entries(labels, vocab_index, z, y, core):
    flat = labels.reshape(-1)
    local = flat % (NZ * NY * 256)
    chip = local // 256
    owner_y = chip % NY
    dz = (chip // NY - z) % NZ
    table = jnp.where(core == 0, jnp.asarray(place_table()[0]), jnp.asarray(place_table()[1]))
    kinds = lax.iota(jnp.int32, 2 * NZ)
    kind = jnp.where(owner_y == y, dz, NZ + dz)
    place = jnp.sum(jnp.where(kind[:, None] == kinds[None], table[None], 0), 1)
    mine = (flat // (NZ * NY * 256) == vocab_index) & ((owner_y == y) | (owner_y == 3 - y))
    place = jnp.where(mine, place, 2 * PAIRS)
    pair = place // 2
    column = place % 2 * 256 + local % 256
    ids = lax.iota(jnp.int32, flat.shape[0])
    sort_key = pair * 1024 + ids
    rank = jnp.sum((sort_key[None, :] < sort_key[:, None]).astype(jnp.int32), 1)
    value = column * 1024 + ids
    entries = jnp.sum(jnp.where(rank[:, None] == ids[None, :], value[:, None], 0), 0)
    steps = lax.iota(jnp.int32, 8)
    bounds = jnp.sum((pair[:, None] < steps[None, :]).astype(jnp.int32), 0)
    return bounds, entries


def body(features, head_weight, labels, audio_len, transcript_len):
    rec_dev, frames, width = features.shape
    rows = rec_dev * frames
    vocab_index = lax.axis_index("vocab")
    rec = lax.axis_index("rec")
    core, y, z = rec % 2, rec // 2 % NY, rec // (2 * NY)

    def send(array, step0, step1=None):
        return lax.ppermute(array, "rec", moves(step0, step1 if step1 is not None else None))

    def both(array, step):
        return send(array, step, step)

    own = head_weight.T
    other = both(own, other_core)
    fa = features.reshape(rows, width)
    fb = both(fa, other_core)
    l1 = both(labels, other_core)
    half_labels = jnp.concatenate([labels, l1])
    l2 = both(half_labels, beside)
    is0 = core == 0
    o0 = jnp.concatenate([jnp.where(is0, own, other), jnp.where(is0, other, own)])
    ga = both(fa[:EARLY], beside)
    op1 = send(o0, up, down)
    op2 = send(o0, None, mirror)
    ha = both(fa[EARLY:], beside)
    op3 = send(op1, up, down)
    op4 = both(op1, mirror)
    op5 = send(op3, up, down)
    op7 = send(op3, mirror)
    op6 = send(jnp.where(is0, op5, op4), up, down)
    gb = both(ga, other_core)
    op8 = send(jnp.where(is0, op7, op6), up, down)
    op9 = send(op6, mirror)
    hb = both(ha, other_core)
    s1 = jnp.where(is0, op7, o0)
    s2 = jnp.where(is0, op9, op2)

    ba, ea = label_entries(half_labels, vocab_index, z, y, core)
    bb, eb = label_entries(l2, vocab_index, z, y, core)
    bounds, entries = jnp.stack([ba, bb]), jnp.stack([ea, eb])

    f32 = jnp.float32
    state = (
        jax.ShapeDtypeStruct((WINDOWS // 2, 8, TILE), f32),
        jax.ShapeDtypeStruct((WINDOWS // 2, 8, TILE), f32),
        jax.ShapeDtypeStruct((2, 8 * 128, 128), f32),
    )
    logits_scratch = pltpu.VMEM((WINDOWS, BLOCK, 128), f32)

    def call(kernel, out_shape, operands, pairs, gflop, extra=(), limit=28):
        return pl.pallas_call(
            kernel,
            out_shape=out_shape,
            in_specs=[SMEM, SMEM, *([VMEM] * len(operands))],
            out_specs=[VMEM] * len(out_shape),
            scratch_shapes=[*extra, pltpu.VMEM((pairs, BLOCK, width), jnp.bfloat16), logits_scratch],
            cost_estimate=pl.CostEstimate(flops=int(gflop * 1e9), bytes_accessed=0, transcendentals=0),
            compiler_params=pltpu.CompilerParams(vmem_limit_bytes=limit * 2**20),
        )(bounds, entries, *operands)

    ma = call(first_kernel, state, (op1, op3, fa, fb), 1, 4)
    ma = call(second_kernel, state, (op4, op5, fa, fb, *ma), 1, 4)
    *ma, mb, sb, pb = call(third_kernel, state + state, (op1, op3, op4, op5, op6, s1, fa, fb, ga, gb, *ma), 3, 9)
    packed = jax.ShapeDtypeStruct((8, 144, TILE), jnp.bfloat16)
    kept, given = call(
        last_kernel,
        (packed, packed),
        (op1, op3, op4, op5, op6, s1, op8, s2, fa, fb, ga, gb, ha, hb, *ma, mb, sb, pb),
        PAIRS,
        9,
        [*(pltpu.VMEM(leaf.shape, leaf.dtype) for leaf in state + state), pltpu.VMEM((WINDOWS, 8, 128), f32)],
    )
    taken = both(given, other_core)
    payload = jax.ShapeDtypeStruct((144, TILE), jnp.bfloat16)
    sent = pl.pallas_call(
        join_kernel,
        out_shape=[payload] * 8,
        in_specs=[SMEM, VMEM, VMEM],
        out_specs=[VMEM] * 8,
        compiler_params=pltpu.CompilerParams(vmem_limit_bytes=8 * 2**20),
    )(vocab_index[None], kept, taken)
    vocabs = lax.axis_size("vocab")
    groups = lax.axis_size("rec")
    got = []
    for side in range(2):
        for step in range(vocabs):
            part = sent[side * 4 + step]
            if side or step:
                pairs = [
                    (g * vocabs + v, (g ^ (2 * side)) * vocabs + (v + step) % vocabs)
                    for g in range(groups)
                    for v in range(vocabs)
                ]
                part = lax.ppermute(part, ("rec", "vocab"), pairs)
            got.append(part)
    log_prob, path = pl.pallas_call(
        align_kernel,
        out_shape=[jax.ShapeDtypeStruct((frames, 128), f32), jax.ShapeDtypeStruct((8, 128), f32)],
        in_specs=[SMEM, *([VMEM] * 8)],
        out_specs=[VMEM] * 2,
        scratch_shapes=[pltpu.VMEM((DEPTH, frames, 128), f32), pltpu.VMEM((frames, 128), f32)],
        compiler_params=pltpu.CompilerParams(vmem_limit_bytes=8 * 2**20),
    )(jnp.concatenate([audio_len, transcript_len]), *got)
    return log_prob[None], path[0, :1]


def solution(mesh):
    placed = (
        P("rec", None, None),
        P(None, ("vocab", "rec")),
        P("rec", None),
        P(("rec", "vocab")),
        P(("rec", "vocab")),
    )

    return jax.shard_map(
        body,
        mesh=mesh,
        in_specs=placed,
        out_specs=(P(("rec", "vocab"), None, None), P(("rec", "vocab"))),
        check_vma=False,
    )
```

time: 185 us -> 169 us (0.914); the launches traced: 184 us -> 166 us
  starting transfers between devices: 31.9 us -> 58.7 us
  Pallas kernels: 72.3 us -> 49 us
  waiting for transfers between devices: 63.3 us -> 45.9 us
  other arithmetic: 8.03 us -> 4.68 us
    pallas_call x8 -> x5, Pallas kernels: 68 us -> 45.4 us  [the longest x4 45.1 us: call(): pl.pallas_call(kernel, out_shape=out_shape, in_specs=[SMEM, SMEM, *[VMEM]...]
    ppermute x17 -> x18, waiting for transfers between devices: 59.6 us -> 42.7 us  [send(): lax.ppermute(array, 'rec', moves(step0, step1 if step1 is not None else N...]
    ppermute x7, starting transfers between devices: 8.99 us -> 23.7 us  [body(): part = lax.ppermute(part, ('rec', 'vocab'), pairs)]
    ppermute x17 -> x18, starting transfers between devices: 23 us -> 35 us  [send(): lax.ppermute(array, 'rec', moves(step0, step1 if step1 is not None else N...]
  transfers between devices with their start and end apart: 24 -> 25, of which waited for: 9 -> 7; matrix products, arithmetic and copies ran while one was open for 3% -> 5% of each run, Pallas kernels for 32% -> 17%
where the time goes in v2:
time: 169 us; the launch traced here: 166 us
  starting transfers between devices  58.7 us (35%)
  Pallas kernels  49 us (29%)
  waiting for transfers between devices  45.9 us (27%)
  local copies, waits for them, and re-layouts  5.9 us (3%)
  other arithmetic  4.68 us (3%)
  between operations  2.25 us (1%)
    pallas_call x4, Pallas kernels, call(): pl.pallas_call(kernel, out_shape=out_shape, in_specs=[SMEM, SMEM, *[VMEM]...  45.1 us
    ppermute x18, waiting for transfers between devices, send(): lax.ppermute(array, 'rec', moves(step0, step1 if step1 is not None else N...  42.7 us
    ppermute x18, starting transfers between devices, send(): lax.ppermute(array, 'rec', moves(step0, step1 if step1 is not None else N...  35 us
    ppermute x7, starting transfers between devices, body(): part = lax.ppermute(part, ('rec', 'vocab'), pairs)  23.7 us
    pallas_call x1, Pallas kernels, body(): pl.pallas_call(align_kernel, out_shape=[jax.ShapeDtypeStruct((frames, 128...  3.61 us
  transfers between devices with their start and end apart: 25, of which 7 were waited for; matrix products, arithmetic and copies ran while one was open for 5% of the time, Pallas kernels for 17%

profile of v2, /device:TPU:1, one launch (start us, length us, event | category | flops | bytes accessed | tf_op | source)
XLA Modules:
  0.0 166.4 jit_solution(11333101063502571567)
XLA Ops:
  0.6 2.0 %copy.12 = bf16[1280,128]{0,1:T(8,128)(2,1)} copy(bf16[1280,128]{1,0:T(8,128)(2,1)} %param.10) | data formatting | bytes 655360 | tf_op args[1]
  2.7 3.2 %collective-permute-start.2 = (bf16[128,1280]{1,0:T(8,128)(2,1)}, bf16[128,1280]{1,0:T(8,128)(2,1)}, u32[]{:S(2)}, u32[]{:S(2)}) collective-permute-start(bf16[128,1280]{1,0:T(8,128)(2,1)} %bitcast.7), channel_id=1, source_target_pairs={{0,4},{8,12},{16,20},{24,28},{32,36},{40,44},{48,52},{56,60},{64,6... | collective-permute-start | bytes 983048 | tf_op jit(solution)/shard_map/ppermute | solution.py:298
  5.9 0.5 collective-permute-start.12
  6.4 2.5 %slice.12 = bf16[512,1280]{1,0:T(8,128)(2,1)} slice(bf16[768,1280]{1,0:T(8,128)(2,1)} %bitcast.86), slice={[0:512], [0:1280]} | slice | bytes 2621440 | tf_op jit(solution)/shard_map/slice | solution.py:312
  8.8 0.9 slice.13
  9.7 1.5 collective-permute-start.15
  11.3 0.1 collective-permute-start.1
  11.4 1.1 broadcast_select_fusion.5
  12.6 5.2 %collective-permute-start.3 = (bf16[256,1280]{1,0:T(8,128)(2,1)S(1)}, bf16[256,1280]{1,0:T(8,128)(2,1)S(1)}, u32[]{:S(2)}, u32[]{:S(2)}) collective-permute-start(bf16[256,1280]{1,0:T(8,128)(2,1)S(1)} %pad_maximum_fusion), channel_id=1, source_target_pairs={{0,32},{8,40},{16,48},{24,56},{32,64},{40,72},{48,80},{56,88},{64,... | collective-permute-start | bytes 1966088 | tf_op jit(solution)/shard_map/ppermute | solution.py:298
  17.8 35.7 %collective-permute-done.1 = s32[8,128]{1,0:T(8,128)S(1)} collective-permute-done((s32[8,128]{1,0:T(8,128)S(1)}, s32[8,128]{1,0:T(8,128)S(1)}, u32[]{:S(2)}, u32[]{:S(2)}) %collective-permute-start.1) | collective-permute-done | bytes 4128 | tf_op jit(solution)/shard_map/ppermute | solution.py:298
  53.6 0.1 select_reduce_fusion.3
  53.7 0.6 convert_reduce_fusion.1
  54.3 0.1 convert_reduce_fusion.3
  54.4 3.9 %collective-permute-start.4 = (bf16[256,1280]{1,0:T(8,128)(2,1)S(1)}, bf16[256,1280]{1,0:T(8,128)(2,1)S(1)}, u32[]{:S(2)}, u32[]{:S(2)}) collective-permute-start(bf16[256,1280]{1,0:T(8,128)(2,1)S(1)} %collective-permute-done.3.one.refs_0_), channel_id=1, source_target_pairs={{0,32},{8,40},{16,48},{24,56},{32,64},{40,72},{48,80},{56,88},{64,... | collective-permute-start | bytes 1966088 | tf_op jit(solution)/shard_map/ppermute | solution.py:298
  58.4 0.1 convert_reduce_fusion.2
  58.5 0.6 convert_reduce_fusion
  59.1 0.7 select_reduce_fusion.1
  59.7 2.8 %collective-permute-start.5 = (bf16[256,1280]{1,0:T(8,128)(2,1)S(1)}, bf16[256,1280]{1,0:T(8,128)(2,1)S(1)}, u32[]{:S(2)}, u32[]{:S(2)}) collective-permute-start(bf16[256,1280]{1,0:T(8,128)(2,1)S(1)} %collective-permute-done.3.one.refs_0_), channel_id=1, source_target_pairs={{0,24},{8,16},{16,8},{24,0},{32,56},{40,48},{48,40},{56,32},{64,88... | collective-permute-start | bytes 1966088 | tf_op jit(solution)/shard_map/ppermute | solution.py:298
  62.6 3.3 %collective-permute-done.4.two.refs_1_ = bf16[256,1280]{1,0:T(8,128)(2,1)S(1)} collective-permute-done((bf16[256,1280]{1,0:T(8,128)(2,1)S(1)}, bf16[256,1280]{1,0:T(8,128)(2,1)S(1)}, u32[]{:S(2)}, u32[]{:S(2)}) %collective-permute-start.4) | collective-permute-done | bytes 655392 | tf_op jit(solution)/shard_map/ppermute | solution.py:298
  65.9 3.4 %collective-permute-start.6 = (bf16[256,1280]{1,0:T(8,128)(2,1)S(1)}, bf16[256,1280]{1,0:T(8,128)(2,1)S(1)}, u32[]{:S(2)}, u32[]{:S(2)}) collective-permute-start(bf16[256,1280]{1,0:T(8,128)(2,1)S(1)} %collective-permute-done.4.two.refs_1_), channel_id=1, source_target_pairs={{0,32},{8,40},{16,48},{24,56},{32,64},{40,72},{48,80},{56,88},{64,... | collective-permute-start | bytes 1966088 | tf_op jit(solution)/shard_map/ppermute | solution.py:298
  69.3 0.7 select_reduce_fusion
  70.0 4.6 %collective-permute-start.11 = (bf16[256,1280]{1,0:T(8,128)(2,1)S(1)}, bf16[256,1280]{1,0:T(8,128)(2,1)S(1)}, u32[]{:S(2)}, u32[]{:S(2)}) collective-permute-start(bf16[256,1280]{1,0:T(8,128)(2,1)S(1)} %pad_maximum_fusion), channel_id=1, source_target_pairs={{4,28},{12,20},{20,12},{28,4},{36,60},{44,52},{52,44},{60,36},{68,... | collective-permute-start | bytes 1966088 | tf_op jit(solution)/shard_map/ppermute | solution.py:298
  74.7 0.1 collective-permute-start.16
  74.8 0.7 collective-permute-done.5.one.refs_2_
  75.5 1.3 collective-permute-done.6.two.refs_3_
  76.8 0.7 collective-permute-start.8
  77.6 3.2 %collective-permute-start.7 = (bf16[256,1280]{1,0:T(8,128)(2,1)S(1)}, bf16[256,1280]{1,0:T(8,128)(2,1)S(1)}, u32[]{:S(2)}, u32[]{:S(2)}) collective-permute-start(bf16[256,1280]{1,0:T(8,128)(2,1)S(1)} %broadcast_select_fusion.3), channel_id=1, source_target_pairs={{0,32},{8,40},{16,48},{24,56},{32,64},{40,72},{48,80},{56,88},{64,... | collective-permute-start | bytes 1966088 | tf_op jit(solution)/shard_map/ppermute | solution.py:298
  80.8 6.1 %shard_map.104 = (f32[6,8,256]{2,1,0:T(8,128)S(1)}, f32[6,8,256]{2,1,0:T(8,128)S(1)}, f32[2,1024,128]{2,1,0:T(8,128)S(1)}) custom-call(s32[2,8]{1,0:T(2,128)S(1)} %pad_add_fusion.2.bounds, s32[2,1024]{1,0:T(2,128)S(1)} %pad_add_fusion.entries, bf16[256,1280]{1,0:T(8,128)(2,1)S(1)} %collective-permute-done.3.one.refs_0_, ...), custom_call_target="tpu_custom_call" | custom-call | flops 4000000000 | tf_op jit(solution)/shard_map/pallas_call | solution.py:341
  86.9 6.1 %shard_map.105 = (f32[6,8,256]{2,1,0:T(8,128)S(1)}, f32[6,8,256]{2,1,0:T(8,128)S(1)}, f32[2,1024,128]{2,1,0:T(8,128)S(1)}) custom-call(s32[2,8]{1,0:T(2,128)S(1)} %pad_add_fusion.2.bounds, s32[2,1024]{1,0:T(2,128)S(1)} %pad_add_fusion.entries, bf16[256,1280]{1,0:T(8,128)(2,1)S(1)} %collective-permute-done.5.one.refs_2_, ...), custom_call_target="tpu_custom_call" | custom-call | flops 4000000000 | tf_op jit(solution)/shard_map/pallas_call | solution.py:341
  93.1 0.3 broadcast_select_fusion.1
  93.4 1.3 collective-permute-start.9
  94.7 0.7 collective-permute-start.10
  95.4 16.0 %shard_map.106 = (f32[6,8,256]{2,1,0:T(8,128)S(1)}, f32[6,8,256]{2,1,0:T(8,128)S(1)}, f32[2,1024,128]{2,1,0:T(8,128)S(1)}, f32[6,8,256]{2,1,0:T(8,128)S(1)}, f32...) custom-call(s32[2,8]{1,0:T(2,128)S(1)} %pad_add_fusion.2.bounds, s32[2,1024]{1,0:T(2,128)S(1)} %pad_add_fusion.entries, ...), custom_call_target="tpu_custom_call" | custom-call | flops 8999999488 | tf_op jit(solution)/shard_map/pallas_call | solution.py:341
  111.4 0.1 broadcast_select_fusion.refs_7_
  111.5 16.9 %shard_map.107 = (bf16[8,144,256]{2,1,0:T(8,128)(2,1)S(1)}, bf16[8,144,256]{2,1,0:T(8,128)(2,1)S(1)}) custom-call(s32[2,8]{1,0:T(2,128)S(1)} %pad_add_fusion.2.bounds, s32[2,1024]{1,0:T(2,128)S(1)} %pad_add_fusion.entries, bf16[256,1280]{1,0:T(8,128)(2,1)S(1)} %collective-permute-done.3.one.refs_0_, ...), custom_call_target="tpu_custom_call" | custom-call | flops 8999999488 | tf_op jit(solution)/shard_map/pallas_call | solution.py:341
  128.5 3.7 %collective-permute-start.17 = (bf16[8,144,256]{2,1,0:T(8,128)(2,1)S(1)}, bf16[8,144,256]{2,1,0:T(8,128)(2,1)S(1)}, u32[]{:S(2)}, u32[]{:S(2)}) collective-permute-start(bf16[8,144,256]{2,1,0:T(8,128)(2,1)S(1)} %get-tuple-element.39), channel_id=1, source_target_pairs={{0,4},{8,12},{16,20},{24,28},{32,36},{40,44},{48,52},{56,60},{64,6... | collective-permute-start | bytes 1769480 | tf_op jit(solution)/shard_map/ppermute | solution.py:298
  132.1 1.6 collective-permute-done.17.theirs
  133.8 0.2 shard_map.108
  134.0 2.1 %collective-permute-start.18 = (bf16[144,256]{1,0:T(8,128)(2,1)S(1)}, bf16[144,256]{1,0:T(8,128)(2,1)S(1)}, u32[]{:S(2)}, u32[]{:S(2)}) collective-permute-start(bf16[144,256]{1,0:T(8,128)(2,1)S(1)} %get-tuple-element.41), channel_id=1, source_target_pairs={{0,1},{1,2},{2,3},{3,0},{4,5},{5,6},{6,7},{7,4},{8,9},{9,10},{10,1... | collective-permute-start | bytes 221192 | tf_op jit(solution)/shard_map/ppermute | solution.py:384
  136.2 5.7 %collective-permute-start.19 = (bf16[144,256]{1,0:T(8,128)(2,1)S(1)}, bf16[144,256]{1,0:T(8,128)(2,1)S(1)}, u32[]{:S(2)}, u32[]{:S(2)}) collective-permute-start(bf16[144,256]{1,0:T(8,128)(2,1)S(1)} %get-tuple-element.42), channel_id=1, source_target_pairs={{0,2},{1,3},{2,0},{3,1},{4,6},{5,7},{6,4},{7,5},{8,10},{9,11},{10,... | collective-permute-start | bytes 221192 | tf_op jit(solution)/shard_map/ppermute | solution.py:384
  143.2 2.0 %collective-permute-start.20 = (bf16[144,256]{1,0:T(8,128)(2,1)S(1)}, bf16[144,256]{1,0:T(8,128)(2,1)S(1)}, u32[]{:S(2)}, u32[]{:S(2)}) collective-permute-start(bf16[144,256]{1,0:T(8,128)(2,1)S(1)} %get-tuple-element.43), channel_id=1, source_target_pairs={{0,3},{1,0},{2,1},{3,2},{4,7},{5,4},{6,5},{7,6},{8,11},{9,8},{10,9... | collective-permute-start | bytes 221192 | tf_op jit(solution)/shard_map/ppermute | solution.py:384
  145.2 10.1 %collective-permute-start.21 = (bf16[144,256]{1,0:T(8,128)(2,1)S(1)}, bf16[144,256]{1,0:T(8,128)(2,1)S(1)}, u32[]{:S(2)}, u32[]{:S(2)}) collective-permute-start(bf16[144,256]{1,0:T(8,128)(2,1)S(1)} %get-tuple-element.44), channel_id=1, source_target_pairs={{0,8},{1,9},{2,10},{3,11},{4,12},{5,13},{6,14},{7,15},{8,0},{9,1},... | collective-permute-start | bytes 221192 | tf_op jit(solution)/shard_map/ppermute | solution.py:384
  155.3 2.2 %collective-permute-start.23 = (bf16[144,256]{1,0:T(8,128)(2,1)S(1)}, bf16[144,256]{1,0:T(8,128)(2,1)S(1)}, u32[]{:S(2)}, u32[]{:S(2)}) collective-permute-start(bf16[144,256]{1,0:T(8,128)(2,1)S(1)} %get-tuple-element.46), channel_id=1, source_target_pairs={{0,10},{1,11},{2,8},{3,9},{4,14},{5,15},{6,12},{7,13},{8,2},{9,3},... | collective-permute-start | bytes 221192 | tf_op jit(solution)/shard_map/ppermute | solution.py:384
  157.5 1.5 collective-permute-start.24
  159.1 2.2 %collective-permute-done.22.refs_5_ = bf16[144,256]{1,0:T(8,128)(2,1)S(1)} collective-permute-done((bf16[144,256]{1,0:T(8,128)(2,1)S(1)}, bf16[144,256]{1,0:T(8,128)(2,1)S(1)}, u32[]{:S(2)}, u32[]{:S(2)}) %collective-permute-start.22) | collective-permute-done | bytes 73760 | tf_op jit(solution)/shard_map/ppermute | solution.py:384
  161.3 0.9 collective-permute-done.23.refs_6_
  162.2 3.6 %shard_map.109 = (f32[192,128]{1,0:T(8,128)}, f32[8,128]{1,0:T(8,128)S(1)}) custom-call(s32[2]{0:T(128)S(1)} %pad_add_fusion.3.lengths, bf16[144,256]{1,0:T(8,128)(2,1)S(1)} %get-tuple-element.40.refs_0_, bf16[144,256]{1,0:T(8,128)(2,1)S(1)} %collective-permute-done.18.refs_1_, bf16[144,256]{1,0:T(8,128)(2,1)S(1)} %collective-permute-done.19.refs_2_, ...), custom_call_target="tpu_custom_call" | custom-call | tf_op jit(solution)/shard_map/pallas_call | solution.py:386
  165.8 0.5 slice.11
  (42 shorter events, 0.5 us)
Async XLA Ops:
  0.6 8.2 %copy-start = (bf16[4,192,1280]{2,1,0:T(8,128)(2,1)S(1)}, bf16[4,192,1280]{2,1,0:T(8,128)(2,1)}, u32[]{:S(2)}) copy-start(bf16[4,192,1280]{2,1,0:T(8,128)(2,1)} %param.9) | copy-start | bytes 5898244
  2.7 8.8 %collective-permute-start.2 = (bf16[128,1280]{1,0:T(8,128)(2,1)}, bf16[128,1280]{1,0:T(8,128)(2,1)}, u32[]{:S(2)}, u32[]{:S(2)}) collective-permute-start(bf16[128,1280]{1,0:T(8,128)(2,1)} %bitcast.7), channel_id=1, source_target_pairs={{0,4},{8,12},{16,20},{24,28},{32,36},{40,44},{48,52},{56,60},{64,6... | collective-permute-start | bytes 983048 | tf_op jit(solution)/shard_map/ppermute | solution.py:298
  5.9 5.4 %collective-permute-start = (s32[4,128]{1,0:T(4,128)}, s32[4,128]{1,0:T(4,128)S(1)}, u32[]{:S(2)}, u32[]{:S(2)}) collective-permute-start(s32[4,128]{1,0:T(4,128)} %param.11), channel_id=1, source_target_pairs={{0,4},{8,12},{16,20},{24,28},{32,36},{40,44},{48,52},{56,60},{64,6... | collective-permute-start | bytes 6152 | tf_op jit(solution)/shard_map/ppermute | solution.py:298
  5.9 5.3 %copy-start.2 = (s32[16]{0:T(128)S(1)}, s32[16]{0:T(128)}, u32[]{:S(2)}) copy-start(s32[16]{0:T(128)} %constant.202.clone) | copy-start | bytes 196
  5.9 5.3 %copy-start.3 = (s32[16]{0:T(128)S(1)}, s32[16]{0:T(128)}, u32[]{:S(2)}) copy-start(s32[16]{0:T(128)} %constant.203.clone) | copy-start | bytes 196
  5.9 5.4 %copy-start.1 = (s32[4,128]{1,0:T(4,128)S(1)}, s32[4,128]{1,0:T(4,128)}, u32[]{:S(2)}) copy-start(s32[4,128]{1,0:T(4,128)} %param.11) | copy-start | bytes 6148
  5.9 71.7 %collective-permute-start.12 = (bf16[768,1280]{1,0:T(8,128)(2,1)}, bf16[768,1280]{1,0:T(8,128)(2,1)}, u32[]{:S(2)}, u32[]{:S(2)}) collective-permute-start(bf16[768,1280]{1,0:T(8,128)(2,1)} %bitcast.85), channel_id=1, source_target_pairs={{0,4},{8,12},{16,20},{24,28},{32,36},{40,44},{48,52},{56,60},{64,6... | collective-permute-start | bytes 5898248 | tf_op jit(solution)/shard_map/ppermute | solution.py:298
  8.8 65.8 %collective-permute-start.13 = (bf16[512,1280]{1,0:T(8,128)(2,1)}, bf16[512,1280]{1,0:T(8,128)(2,1)S(1)}, u32[]{:S(2)}, u32[]{:S(2)}) collective-permute-start(bf16[512,1280]{1,0:T(8,128)(2,1)} %slice.12), channel_id=1, source_target_pairs={{0,8},{8,0},{16,24},{24,16},{32,40},{40,32},{48,56},{56,48},{64,72... | collective-permute-start | bytes 3932168 | tf_op jit(solution)/shard_map/ppermute | solution.py:298
  9.7 60.3 %collective-permute-start.15 = (bf16[256,1280]{1,0:T(8,128)(2,1)}, bf16[256,1280]{1,0:T(8,128)(2,1)}, u32[]{:S(2)}, u32[]{:S(2)}) collective-permute-start(bf16[256,1280]{1,0:T(8,128)(2,1)} %slice.13), channel_id=1, source_target_pairs={{0,8},{8,0},{16,24},{24,16},{32,40},{40,32},{48,56},{56,48},{64,72... | collective-permute-start | bytes 1966088 | tf_op jit(solution)/shard_map/ppermute | solution.py:298
  11.3 42.2 %collective-permute-start.1 = (s32[8,128]{1,0:T(8,128)S(1)}, s32[8,128]{1,0:T(8,128)S(1)}, u32[]{:S(2)}, u32[]{:S(2)}) collective-permute-start(s32[8,128]{1,0:T(8,128)S(1)} %pad_add_fusion.1), channel_id=1, source_target_pairs={{0,8},{8,0},{16,24},{24,16},{32,40},{40,32},{48,56},{56,48},{64,72... | collective-permute-start | bytes 12296 | tf_op jit(solution)/shard_map/ppermute | solution.py:298
  12.6 41.8 %collective-permute-start.3 = (bf16[256,1280]{1,0:T(8,128)(2,1)S(1)}, bf16[256,1280]{1,0:T(8,128)(2,1)S(1)}, u32[]{:S(2)}, u32[]{:S(2)}) collective-permute-start(bf16[256,1280]{1,0:T(8,128)(2,1)S(1)} %pad_maximum_fusion), channel_id=1, source_target_pairs={{0,32},{8,40},{16,48},{24,56},{32,64},{40,72},{48,80},{56,88},{64,... | collective-permute-start | bytes 1966088 | tf_op jit(solution)/shard_map/ppermute | solution.py:298
  54.4 11.5 %collective-permute-start.4 = (bf16[256,1280]{1,0:T(8,128)(2,1)S(1)}, bf16[256,1280]{1,0:T(8,128)(2,1)S(1)}, u32[]{:S(2)}, u32[]{:S(2)}) collective-permute-start(bf16[256,1280]{1,0:T(8,128)(2,1)S(1)} %collective-permute-done.3.one.refs_0_), channel_id=1, source_target_pairs={{0,32},{8,40},{16,48},{24,56},{32,64},{40,72},{48,80},{56,88},{64,... | collective-permute-start | bytes 1966088 | tf_op jit(solution)/shard_map/ppermute | solution.py:298
  59.7 15.8 %collective-permute-start.5 = (bf16[256,1280]{1,0:T(8,128)(2,1)S(1)}, bf16[256,1280]{1,0:T(8,128)(2,1)S(1)}, u32[]{:S(2)}, u32[]{:S(2)}) collective-permute-start(bf16[256,1280]{1,0:T(8,128)(2,1)S(1)} %collective-permute-done.3.one.refs_0_), channel_id=1, source_target_pairs={{0,24},{8,16},{16,8},{24,0},{32,56},{40,48},{48,40},{56,32},{64,88... | collective-permute-start | bytes 1966088 | tf_op jit(solution)/shard_map/ppermute | solution.py:298
  65.9 10.9 %collective-permute-start.6 = (bf16[256,1280]{1,0:T(8,128)(2,1)S(1)}, bf16[256,1280]{1,0:T(8,128)(2,1)S(1)}, u32[]{:S(2)}, u32[]{:S(2)}) collective-permute-start(bf16[256,1280]{1,0:T(8,128)(2,1)S(1)} %collective-permute-done.4.two.refs_1_), channel_id=1, source_target_pairs={{0,32},{8,40},{16,48},{24,56},{32,64},{40,72},{48,80},{56,88},{64,... | collective-permute-start | bytes 1966088 | tf_op jit(solution)/shard_map/ppermute | solution.py:298
  70.0 41.4 %collective-permute-start.11 = (bf16[256,1280]{1,0:T(8,128)(2,1)S(1)}, bf16[256,1280]{1,0:T(8,128)(2,1)S(1)}, u32[]{:S(2)}, u32[]{:S(2)}) collective-permute-start(bf16[256,1280]{1,0:T(8,128)(2,1)S(1)} %pad_maximum_fusion), channel_id=1, source_target_pairs={{4,28},{12,20},{20,12},{28,4},{36,60},{44,52},{52,44},{60,36},{68,... | collective-permute-start | bytes 1966088 | tf_op jit(solution)/shard_map/ppermute | solution.py:298
  74.7 36.8 %collective-permute-start.16 = (bf16[256,1280]{1,0:T(8,128)(2,1)}, bf16[256,1280]{1,0:T(8,128)(2,1)S(1)}, u32[]{:S(2)}, u32[]{:S(2)}) collective-permute-start(bf16[256,1280]{1,0:T(8,128)(2,1)} %collective-permute-done.15.refs_12_), channel_id=1, source_target_pairs={{0,4},{8,12},{16,20},{24,28},{32,36},{40,44},{48,52},{56,60},{64,6... | collective-permute-start | bytes 1966088 | tf_op jit(solution)/shard_map/ppermute | solution.py:298
  75.5 19.9 %collective-permute-start.14 = (bf16[512,1280]{1,0:T(8,128)(2,1)S(1)}, bf16[512,1280]{1,0:T(8,128)(2,1)S(1)}, u32[]{:S(2)}, u32[]{:S(2)}) collective-permute-start(bf16[512,1280]{1,0:T(8,128)(2,1)S(1)} %collective-permute-done.13.refs_8_.refs_10_), channel_id=1, source_target_pairs={{0,4},{8,12},{16,20},{24,28},{32,36},{40,44},{48,52},{56,60},{64,6... | collective-permute-start | bytes 3932168 | tf_op jit(solution)/shard_map/ppermute | solution.py:298
  76.8 16.2 %collective-permute-start.8 = (bf16[256,1280]{1,0:T(8,128)(2,1)S(1)}, bf16[256,1280]{1,0:T(8,128)(2,1)S(1)}, u32[]{:S(2)}, u32[]{:S(2)}) collective-permute-start(bf16[256,1280]{1,0:T(8,128)(2,1)S(1)} %collective-permute-done.4.two.refs_1_), channel_id=1, source_target_pairs={{0,24},{8,16},{16,8},{24,0},{32,56},{40,48},{48,40},{56,32},{64,88... | collective-permute-start | bytes 1966088 | tf_op jit(solution)/shard_map/ppermute | solution.py:298
  77.6 15.5 %collective-permute-start.7 = (bf16[256,1280]{1,0:T(8,128)(2,1)S(1)}, bf16[256,1280]{1,0:T(8,128)(2,1)S(1)}, u32[]{:S(2)}, u32[]{:S(2)}) collective-permute-start(bf16[256,1280]{1,0:T(8,128)(2,1)S(1)} %broadcast_select_fusion.3), channel_id=1, source_target_pairs={{0,32},{8,40},{16,48},{24,56},{32,64},{40,72},{48,80},{56,88},{64,... | collective-permute-start | bytes 1966088 | tf_op jit(solution)/shard_map/ppermute | solution.py:298
  93.4 18.1 %collective-permute-start.9 = (bf16[256,1280]{1,0:T(8,128)(2,1)S(1)}, bf16[256,1280]{1,0:T(8,128)(2,1)S(1)}, u32[]{:S(2)}, u32[]{:S(2)}) collective-permute-start(bf16[256,1280]{1,0:T(8,128)(2,1)S(1)} %get-tuple-element.58), channel_id=1, source_target_pairs={{0,32},{8,40},{16,48},{24,56},{32,64},{40,72},{48,80},{56,88},{64,... | collective-permute-start | bytes 1966088 | tf_op jit(solution)/shard_map/ppermute | solution.py:298
  94.7 16.7 %collective-permute-start.10 = (bf16[256,1280]{1,0:T(8,128)(2,1)S(1)}, bf16[256,1280]{1,0:T(8,128)(2,1)S(1)}, u32[]{:S(2)}, u32[]{:S(2)}) collective-permute-start(bf16[256,1280]{1,0:T(8,128)(2,1)S(1)} %collective-permute-done.7.refs_4_), channel_id=1, source_target_pairs={{0,24},{8,16},{16,8},{24,0},{32,56},{40,48},{48,40},{56,32},{64,88... | collective-permute-start | bytes 1966088 | tf_op jit(solution)/shard_map/ppermute | solution.py:298
  128.5 5.3 %collective-permute-start.17 = (bf16[8,144,256]{2,1,0:T(8,128)(2,1)S(1)}, bf16[8,144,256]{2,1,0:T(8,128)(2,1)S(1)}, u32[]{:S(2)}, u32[]{:S(2)}) collective-permute-start(bf16[8,144,256]{2,1,0:T(8,128)(2,1)S(1)} %get-tuple-element.39), channel_id=1, source_target_pairs={{0,4},{8,12},{16,20},{24,28},{32,36},{40,44},{48,52},{56,60},{64,6... | collective-permute-start | bytes 1769480 | tf_op jit(solution)/shard_map/ppermute | solution.py:298
  134.0 21.3 %collective-permute-start.18 = (bf16[144,256]{1,0:T(8,128)(2,1)S(1)}, bf16[144,256]{1,0:T(8,128)(2,1)S(1)}, u32[]{:S(2)}, u32[]{:S(2)}) collective-permute-start(bf16[144,256]{1,0:T(8,128)(2,1)S(1)} %get-tuple-element.41), channel_id=1, source_target_pairs={{0,1},{1,2},{2,3},{3,0},{4,5},{5,6},{6,7},{7,4},{8,9},{9,10},{10,1... | collective-permute-start | bytes 221192 | tf_op jit(solution)/shard_map/ppermute | solution.py:384
  136.2 21.4 %collective-permute-start.19 = (bf16[144,256]{1,0:T(8,128)(2,1)S(1)}, bf16[144,256]{1,0:T(8,128)(2,1)S(1)}, u32[]{:S(2)}, u32[]{:S(2)}) collective-permute-start(bf16[144,256]{1,0:T(8,128)(2,1)S(1)} %get-tuple-element.42), channel_id=1, source_target_pairs={{0,2},{1,3},{2,0},{3,1},{4,6},{5,7},{6,4},{7,5},{8,10},{9,11},{10,... | collective-permute-start | bytes 221192 | tf_op jit(solution)/shard_map/ppermute | solution.py:384
  143.2 15.9 %collective-permute-start.20 = (bf16[144,256]{1,0:T(8,128)(2,1)S(1)}, bf16[144,256]{1,0:T(8,128)(2,1)S(1)}, u32[]{:S(2)}, u32[]{:S(2)}) collective-permute-start(bf16[144,256]{1,0:T(8,128)(2,1)S(1)} %get-tuple-element.43), channel_id=1, source_target_pairs={{0,3},{1,0},{2,1},{3,2},{4,7},{5,4},{6,5},{7,6},{8,11},{9,8},{10,9... | collective-permute-start | bytes 221192 | tf_op jit(solution)/shard_map/ppermute | solution.py:384
  145.2 13.8 %collective-permute-start.21 = (bf16[144,256]{1,0:T(8,128)(2,1)S(1)}, bf16[144,256]{1,0:T(8,128)(2,1)S(1)}, u32[]{:S(2)}, u32[]{:S(2)}) collective-permute-start(bf16[144,256]{1,0:T(8,128)(2,1)S(1)} %get-tuple-element.44), channel_id=1, source_target_pairs={{0,8},{1,9},{2,10},{3,11},{4,12},{5,13},{6,14},{7,15},{8,0},{9,1},... | collective-permute-start | bytes 221192 | tf_op jit(solution)/shard_map/ppermute | solution.py:384
  155.3 6.0 %collective-permute-start.22 = (bf16[144,256]{1,0:T(8,128)(2,1)S(1)}, bf16[144,256]{1,0:T(8,128)(2,1)S(1)}, u32[]{:S(2)}, u32[]{:S(2)}) collective-permute-start(bf16[144,256]{1,0:T(8,128)(2,1)S(1)} %get-tuple-element.45), channel_id=1, source_target_pairs={{0,9},{1,10},{2,11},{3,8},{4,13},{5,14},{6,15},{7,12},{8,1},{9,2},... | collective-permute-start | bytes 221192 | tf_op jit(solution)/shard_map/ppermute | solution.py:384
  155.3 6.9 %collective-permute-start.23 = (bf16[144,256]{1,0:T(8,128)(2,1)S(1)}, bf16[144,256]{1,0:T(8,128)(2,1)S(1)}, u32[]{:S(2)}, u32[]{:S(2)}) collective-permute-start(bf16[144,256]{1,0:T(8,128)(2,1)S(1)} %get-tuple-element.46), channel_id=1, source_target_pairs={{0,10},{1,11},{2,8},{3,9},{4,14},{5,15},{6,12},{7,13},{8,2},{9,3},... | collective-permute-start | bytes 221192 | tf_op jit(solution)/shard_map/ppermute | solution.py:384
  157.5 4.7 %collective-permute-start.24 = (bf16[144,256]{1,0:T(8,128)(2,1)S(1)}, bf16[144,256]{1,0:T(8,128)(2,1)S(1)}, u32[]{:S(2)}, u32[]{:S(2)}) collective-permute-start(bf16[144,256]{1,0:T(8,128)(2,1)S(1)} %get-tuple-element.47), channel_id=1, source_target_pairs={{0,11},{1,8},{2,9},{3,10},{4,15},{5,12},{6,13},{7,14},{8,3},{9,0},... | collective-permute-start | bytes 221192 | tf_op jit(solution)/shard_map/ppermute | solution.py:384

commit v3 on v2

--- a/solution.py
+++ b/solution.py
@@ -7,6 +7,7 @@
 from jax.experimental import pallas as pl
 from jax.experimental.pallas import tpu as pltpu
 from jax.sharding import PartitionSpec as P
+
 
 negative_fill = -1e30
 NZ, NY = 8, 4
@@ -56,6 +57,10 @@
     return z, y ^ 1, core
 
 
+def across(z, y, core):
+    return z, y ^ 1, 1 - core
+
+
 def place_table():
     table = np.full((2, 2 * NZ), 2 * PAIRS, np.int32)
     order0 = [(-1, 0), (-2, 0), (-1, 1), (-3, 0), (-4, 0), (-2, 1), (-3, 1), (-4, 1)]
@@ -66,23 +71,39 @@
     return table
 
 
-def score_tiles(w_ref, pair, f_ref, first_tile, l_ref, m_ref, s_ref):
-    def step(t, _):
-        rows = f_ref[pl.ds(pl.multiple_of(t * TILE, TILE), TILE), :]
+def score_jobs(w_ref, pair, jobs):
+    def multiply(job):
+        f_ref, t, at, l_ref = job[:4]
         tile = lax.dot_general(
-            w_ref[pair], rows, (((1,), (1,)), ((), ())), preferred_element_type=jnp.float32
+            w_ref[pair],
+            f_ref[t * TILE : (t + 1) * TILE, :],
+            (((1,), (1,)), ((), ())),
+            preferred_element_type=jnp.float32,
         )
-        at = first_tile + t
         l_ref[2 * at] = tile[:, :128]
         l_ref[2 * at + 1] = tile[:, 128:]
-        cube = tile.reshape(BLOCK // 8, 8, TILE)
-        old = m_ref[at]
-        top = jnp.maximum(jnp.max(cube, 0), old)
-        s_ref[at] = s_ref[at] * jnp.exp(old - top) + jnp.sum(jnp.exp(cube - top[None]), 0)
-        m_ref[at] = top
-        return 0
-
-    lax.fori_loop(0, f_ref.shape[0] // TILE, step, 0)
+
+    def reduce(job):
+        at, l_ref, m_ref, s_ref = job[2:]
+        for side in range(2):
+            lanes = slice(128 * side, 128 * side + 128)
+            cube = l_ref[2 * at + side].reshape(BLOCK // 8, 8, 128)
+            old = m_ref[at, :, lanes]
+            top = jnp.maximum(jnp.max(cube, 0), old)
+            s_ref[at, :, lanes] = s_ref[at, :, lanes] * jnp.exp(old - top) + jnp.sum(jnp.exp(cube - top[None]), 0)
+            m_ref[at, :, lanes] = top
+
+    multiply(jobs[0])
+    for now, later in zip(jobs, jobs[1:]):
+        multiply(later)
+        reduce(now)
+    reduce(jobs[-1])
+
+
+def jobs_of(parts, l_ref, m_ref, s_ref):
+    return [
+        (f_ref, t, first + t, l_ref, m_ref, s_ref) for f_ref, first in parts for t in range(f_ref.shape[0] // TILE)
+    ]
 
 
 def take_rows(pair, which, bounds, entries, l_ref, p_ref, early=None):
@@ -116,8 +137,7 @@
     s[...] = jnp.zeros_like(s)
     p[...] = jnp.zeros_like(p)
     fill_pair(w_ref, 0, one, two)
-    score_tiles(w_ref, 0, fa, 0, l_ref, m, s)
-    score_tiles(w_ref, 0, fb, 3, l_ref, m, s)
+    score_jobs(w_ref, 0, jobs_of(((fa, 0), (fb, 3)), l_ref, m, s))
     take_rows(0, 0, bounds, entries, l_ref, p)
 
 
@@ -126,8 +146,7 @@
     s[...] = s_in[...]
     p[...] = p_in[...]
     fill_pair(w_ref, 0, one, two)
-    score_tiles(w_ref, 0, fa, 0, l_ref, m, s)
-    score_tiles(w_ref, 0, fb, 3, l_ref, m, s)
+    score_jobs(w_ref, 0, jobs_of(((fa, 0), (fb, 3)), l_ref, m, s))
     take_rows(1, 0, bounds, entries, l_ref, p)
 
 
@@ -141,13 +160,11 @@
     pb[...] = jnp.zeros_like(pb)
     for pair in range(3):
         fill_pair(w_ref, pair, *blocks[2 * pair : 2 * pair + 2])
-    score_tiles(w_ref, 2, fa, 0, l_ref, m, s)
-    score_tiles(w_ref, 2, fb, 3, l_ref, m, s)
+    score_jobs(w_ref, 2, jobs_of(((fa, 0), (fb, 3)), l_ref, m, s))
     take_rows(2, 0, bounds, entries, l_ref, p)
 
     def over(pair, _):
-        score_tiles(w_ref, pair, ga, 0, l_ref, mb, sb)
-        score_tiles(w_ref, pair, gb, 3, l_ref, mb, sb)
+        score_jobs(w_ref, pair, jobs_of(((ga, 0), (gb, 3)), l_ref, mb, sb))
         take_rows(pair, 1, bounds, entries, l_ref, pb, True)
         return 0
 
@@ -170,24 +187,21 @@
 
 def last_kernel(bounds, entries, *refs):
     blocks, (fa, fb, ga, gb, ha, hb), state, (kept, given) = refs[:8], refs[8:14], refs[14:20], refs[20:22]
-    m, s, p, mb, sb, pb, lse_ref, w_ref, l_ref = refs[22:]
+    m, s, p, mb, sb, pb, lse_ref, lb_ref, w_ref, l_ref = refs[22:]
     for ref, value in zip((m, s, p, mb, sb, pb), state):
         ref[...] = value[...]
     for pair in range(PAIRS):
         fill_pair(w_ref, pair, *blocks[2 * pair : 2 * pair + 2])
 
     def over(pair, _):
-        score_tiles(w_ref, pair, ha, 2, l_ref, mb, sb)
-        score_tiles(w_ref, pair, hb, 5, l_ref, mb, sb)
-        take_rows(pair, 1, bounds, entries, l_ref, pb, False)
+        score_jobs(w_ref, pair, jobs_of(((ha, 2), (hb, 5)), lb_ref, mb, sb))
+        take_rows(pair, 1, bounds, entries, lb_ref, pb, False)
         return 0
 
     lax.fori_loop(0, PAIRS, over, 0)
-    score_tiles(w_ref, 3, ga, 0, l_ref, mb, sb)
-    score_tiles(w_ref, 3, gb, 3, l_ref, mb, sb)
-    take_rows(3, 1, bounds, entries, l_ref, pb, True)
-    score_tiles(w_ref, 3, fa, 0, l_ref, m, s)
-    score_tiles(w_ref, 3, fb, 3, l_ref, m, s)
+    later = jobs_of(((ga, 0), (gb, 3)), lb_ref, mb, sb)
+    score_jobs(w_ref, 3, later + jobs_of(((fa, 0), (fb, 3)), l_ref, m, s))
+    take_rows(3, 1, bounds, entries, lb_ref, pb, True)
     take_rows(3, 0, bounds, entries, l_ref, p)
     for group, (mm, ss, pp) in enumerate(((m, s, p), (mb, sb, pb))):
         for t in range(WINDOWS // 2):
@@ -210,33 +224,30 @@
                 out[group * 4 + k, 128:144, :] = split_parts(value)
 
 
-def join_kernel(where, mine, theirs, *outs):
-    place = where[0]
+def join_kernel(where, mine, theirs, out):
+    odd = where[0]
     for group in range(2):
-        for step in range(4):
-            rec = group * 4 + (place + step) % 4
-            out = outs[group * 4 + step]
+        for k in range(4):
+            rec = group * 4 + k
+            to = (group ^ odd) * 4 + k
             one, two = mine[rec], theirs[rec]
             picked = one[0:128].astype(jnp.float32) + two[0:128].astype(jnp.float32)
-            out[0:128, :] = picked.astype(jnp.bfloat16)
+            out[to, 0:128, :] = picked.astype(jnp.bfloat16)
             a, b = joined_parts(one[128:144]), joined_parts(two[128:144])
             top = jnp.maximum(a, b)
             value = top + jnp.log(jnp.exp(a - top) + jnp.exp(b - top))
-            out[128:144, :] = split_parts(jnp.broadcast_to(value, (8, TILE)))
+            out[to, 128:144, :] = split_parts(jnp.broadcast_to(value, (8, TILE)))
 
 
 DEPTH = 8
 
 
-def align_kernel(lengths, *refs):
-    parts, (logprob, path, turned, scores) = refs[:8], refs[8:]
+def align_kernel(lengths, parts, logprob, path, turned, scores):
     frames = logprob.shape[0]
-    picked = parts[0][0:128, :].astype(jnp.float32)
-    for part in parts[1:]:
-        picked = picked + part[0:128, :].astype(jnp.float32)
-    norms = []
-    for part in parts:
-        norms.append(joined_parts(part[128:144, :]))
+    picked = parts[0, 0:128, :].astype(jnp.float32)
+    for k in range(1, 8):
+        picked = picked + parts[k, 0:128, :].astype(jnp.float32)
+    norms = [joined_parts(parts[k, 128:144, :]) for k in range(8)]
     top = functools.reduce(jnp.maximum, norms)
     norm = top + jnp.log(sum(jnp.exp(value - top) for value in norms))
     table = (picked - norm).T[:frames]
@@ -302,16 +313,16 @@
 
     own = head_weight.T
     other = both(own, other_core)
+    is0 = core == 0
+    o0 = jnp.concatenate([jnp.where(is0, own, other), jnp.where(is0, other, own)])
+    op1 = send(o0, up, down)
+    op2 = send(o0, None, mirror)
     fa = features.reshape(rows, width)
     fb = both(fa, other_core)
     l1 = both(labels, other_core)
-    half_labels = jnp.concatenate([labels, l1])
-    l2 = both(half_labels, beside)
-    is0 = core == 0
-    o0 = jnp.concatenate([jnp.where(is0, own, other), jnp.where(is0, other, own)])
+    l2 = both(labels, beside)
+    l3 = both(labels, across)
     ga = both(fa[:EARLY], beside)
-    op1 = send(o0, up, down)
-    op2 = send(o0, None, mirror)
     ha = both(fa[EARLY:], beside)
     op3 = send(op1, up, down)
     op4 = both(op1, mirror)
@@ -325,8 +336,8 @@
     s1 = jnp.where(is0, op7, o0)
     s2 = jnp.where(is0, op9, op2)
 
-    ba, ea = label_entries(half_labels, vocab_index, z, y, core)
-    bb, eb = label_entries(l2, vocab_index, z, y, core)
+    ba, ea = label_entries(jnp.concatenate([labels, l1]), vocab_index, z, y, core)
+    bb, eb = label_entries(jnp.concatenate([l2, l3]), vocab_index, z, y, core)
     bounds, entries = jnp.stack([ba, bb]), jnp.stack([ea, eb])
 
     f32 = jnp.float32
@@ -337,7 +348,7 @@
     )
     logits_scratch = pltpu.VMEM((WINDOWS, BLOCK, 128), f32)
 
-    def call(kernel, out_shape, operands, pairs, gflop, extra=(), limit=28):
+    def call(kernel, out_shape, operands, pairs, gflop, limit, extra=()):
         return pl.pallas_call(
             kernel,
             out_shape=out_shape,
@@ -348,9 +359,9 @@
             compiler_params=pltpu.CompilerParams(vmem_limit_bytes=limit * 2**20),
         )(bounds, entries, *operands)
 
-    ma = call(first_kernel, state, (op1, op3, fa, fb), 1, 4)
-    ma = call(second_kernel, state, (op4, op5, fa, fb, *ma), 1, 4)
-    *ma, mb, sb, pb = call(third_kernel, state + state, (op1, op3, op4, op5, op6, s1, fa, fb, ga, gb, *ma), 3, 9)
+    ma = call(first_kernel, state, (op1, op3, fa, fb), 1, 4, 14)
+    ma = call(second_kernel, state, (op4, op5, fa, fb, *ma), 1, 4, 14)
+    *ma, mb, sb, pb = call(third_kernel, state + state, (op1, op3, op4, op5, op6, s1, fa, fb, ga, gb, *ma), 3, 9, 18)
     packed = jax.ShapeDtypeStruct((8, 144, TILE), jnp.bfloat16)
     kept, given = call(
         last_kernel,
@@ -358,39 +369,33 @@
         (op1, op3, op4, op5, op6, s1, op8, s2, fa, fb, ga, gb, ha, hb, *ma, mb, sb, pb),
         PAIRS,
         9,
-        [*(pltpu.VMEM(leaf.shape, leaf.dtype) for leaf in state + state), pltpu.VMEM((WINDOWS, 8, 128), f32)],
+        24,
+        [*(pltpu.VMEM(leaf.shape, leaf.dtype) for leaf in state + state), pltpu.VMEM((WINDOWS, 8, 128), f32), logits_scratch],
     )
     taken = both(given, other_core)
-    payload = jax.ShapeDtypeStruct((144, TILE), jnp.bfloat16)
     sent = pl.pallas_call(
         join_kernel,
-        out_shape=[payload] * 8,
+        out_shape=packed,
         in_specs=[SMEM, VMEM, VMEM],
-        out_specs=[VMEM] * 8,
+        out_specs=VMEM,
         compiler_params=pltpu.CompilerParams(vmem_limit_bytes=8 * 2**20),
-    )(vocab_index[None], kept, taken)
+    )((y % 2)[None], kept, taken)
     vocabs = lax.axis_size("vocab")
-    groups = lax.axis_size("rec")
-    got = []
-    for side in range(2):
-        for step in range(vocabs):
-            part = sent[side * 4 + step]
-            if side or step:
-                pairs = [
-                    (g * vocabs + v, (g ^ (2 * side)) * vocabs + (v + step) % vocabs)
-                    for g in range(groups)
-                    for v in range(vocabs)
-                ]
-                part = lax.ppermute(part, ("rec", "vocab"), pairs)
-            got.append(part)
+    owners = [
+        [rec_index(z, y + side, core) * vocabs + v for side in range(2) for v in range(vocabs)]
+        for z in range(NZ)
+        for y in range(0, NY, 2)
+        for core in range(2)
+    ]
+    got = lax.all_to_all(sent, ("rec", "vocab"), 0, 0, tiled=True, axis_index_groups=owners)
     log_prob, path = pl.pallas_call(
         align_kernel,
         out_shape=[jax.ShapeDtypeStruct((frames, 128), f32), jax.ShapeDtypeStruct((8, 128), f32)],
-        in_specs=[SMEM, *([VMEM] * 8)],
+        in_specs=[SMEM, VMEM],
         out_specs=[VMEM] * 2,
         scratch_shapes=[pltpu.VMEM((DEPTH, frames, 128), f32), pltpu.VMEM((frames, 128), f32)],
         compiler_params=pltpu.CompilerParams(vmem_limit_bytes=8 * 2**20),
-    )(jnp.concatenate([audio_len, transcript_len]), *got)
+    )(jnp.concatenate([audio_len, transcript_len]), got)
     return log_prob[None], path[0, :1]
 
 

time: 169 us -> 142 us (0.84); the launches traced: 166 us -> 141 us
  waiting for transfers between devices: 45.9 us -> 36 us
  Pallas kernels: 49 us -> 40.9 us
  starting transfers between devices: 58.7 us -> 52 us
    ppermute x7 -> x0, starting transfers between devices: 23.7 us -> none  [body(): part = lax.ppermute(part, ('rec', 'vocab'), pairs)]
    all_to_all x0 -> x1, starting transfers between devices: none -> 16.3 us  [body(): lax.all_to_all(sent, ('rec', 'vocab'), 0, 0, tiled=True, axis_index_group...]
    ppermute x18 -> x19, waiting for transfers between devices: 42.7 us -> 26.5 us  [send(): lax.ppermute(array, 'rec', moves(step0, step1 if step1 is not None else N...]
    all_to_all x0 -> x1, waiting for transfers between devices: none -> 9.58 us  [body(): lax.all_to_all(sent, ('rec', 'vocab'), 0, 0, tiled=True, axis_index_group...]
    pallas_call x4, Pallas kernels: 45.1 us -> 36.3 us  [call(): pl.pallas_call(kernel, out_shape=out_shape, in_specs=[SMEM, SMEM, *[VMEM]...]
    ppermute x7 -> x0, waiting for transfers between devices: 3.16 us -> none  [body(): part = lax.ppermute(part, ('rec', 'vocab'), pairs)]
    ppermute x18 -> x19, starting transfers between devices: 35 us -> 35.7 us  [send(): lax.ppermute(array, 'rec', moves(step0, step1 if step1 is not None else N...]
  transfers between devices with their start and end apart: 25 -> 20, of which waited for: 7 -> 5; matrix products, arithmetic and copies ran while one was open for 5% -> 7% of each run, Pallas kernels for 17% -> 15%
where the time goes in v3:
time: 142 us; the launch traced here: 141 us
  starting transfers between devices  52 us (37%)
  Pallas kernels  40.9 us (29%)
  waiting for transfers between devices  36 us (25%)
  other arithmetic  5.29 us (4%)
  local copies, waits for them, and re-layouts  4.71 us (3%)
  between operations  2.19 us (2%)
    pallas_call x4, Pallas kernels, call(): pl.pallas_call(kernel, out_shape=out_shape, in_specs=[SMEM, SMEM, *[VMEM]...  36.3 us
    ppermute x19, starting transfers between devices, send(): lax.ppermute(array, 'rec', moves(step0, step1 if step1 is not None else N...  35.7 us
    ppermute x19, waiting for transfers between devices, send(): lax.ppermute(array, 'rec', moves(step0, step1 if step1 is not None else N...  26.5 us
    all_to_all x1, starting transfers between devices, body(): lax.all_to_all(sent, ('rec', 'vocab'), 0, 0, tiled=True, axis_index_group...  16.3 us
    all_to_all x1, waiting for transfers between devices, body(): lax.all_to_all(sent, ('rec', 'vocab'), 0, 0, tiled=True, axis_index_group...  9.58 us
    pallas_call x1, Pallas kernels, body(): pl.pallas_call(align_kernel, out_shape=[jax.ShapeDtypeStruct((frames, 128...  3.61 us
  transfers between devices with their start and end apart: 20, of which 5 were waited for; matrix products, arithmetic and copies ran while one was open for 7% of the time, Pallas kernels for 15%

profile of v3, /device:TPU:1, one launch (start us, length us, event | category | flops | bytes accessed | tf_op | source)
XLA Modules:
  0.0 141.2 jit_solution(14010163193418504418)
XLA Ops:
  0.6 0.0 copy-start
  0.6 2.2 %collective-permute-start.1 = (s32[4,128]{1,0:T(4,128)}, s32[4,128]{1,0:T(4,128)S(1)}, u32[]{:S(2)}, u32[]{:S(2)}) collective-permute-start(s32[4,128]{1,0:T(4,128)} %param.11), channel_id=1, source_target_pairs={{0,8},{8,0},{16,24},{24,16},{32,40},{40,32},{48,56},{56,48},{64,72... | collective-permute-start | bytes 6152 | tf_op jit(solution)/shard_map/ppermute | solution.py:309
  2.8 2.7 %collective-permute-start.2 = (s32[4,128]{1,0:T(4,128)}, s32[4,128]{1,0:T(4,128)S(1)}, u32[]{:S(2)}, u32[]{:S(2)}) collective-permute-start(s32[4,128]{1,0:T(4,128)} %param.11), channel_id=1, source_target_pairs={{0,12},{8,4},{16,28},{24,20},{32,44},{40,36},{48,60},{56,52},{64,7... | collective-permute-start | bytes 6152 | tf_op jit(solution)/shard_map/ppermute | solution.py:309
  5.6 1.9 %copy.12 = bf16[1280,128]{0,1:T(8,128)(2,1)} copy(bf16[1280,128]{1,0:T(8,128)(2,1)} %param.10) | data formatting | bytes 655360 | tf_op args[1]
  7.4 0.5 collective-permute-start.3
  8.0 0.0 collective-permute-start.13
  8.0 0.7 broadcast_select_fusion.6
  8.6 1.4 %slice.12 = bf16[512,1280]{1,0:T(8,128)(2,1)S(1)} slice(bf16[768,1280]{1,0:T(8,128)(2,1)} %bitcast.46), slice={[0:512], [0:1280]} | slice | bytes 2621440 | tf_op jit(solution)/shard_map/slice | solution.py:325
  10.0 0.9 slice.13
  10.9 0.1 collective-permute-start.14
  11.1 1.4 %collective-permute-start.16 = (bf16[256,1280]{1,0:T(8,128)(2,1)}, bf16[256,1280]{1,0:T(8,128)(2,1)S(1)}, u32[]{:S(2)}, u32[]{:S(2)}) collective-permute-start(bf16[256,1280]{1,0:T(8,128)(2,1)} %slice.13), channel_id=1, source_target_pairs={{0,8},{8,0},{16,24},{24,16},{32,40},{40,32},{48,56},{56,48},{64,72... | collective-permute-start | bytes 1966088 | tf_op jit(solution)/shard_map/ppermute | solution.py:309
  12.6 1.1 broadcast_select_fusion.5
  13.7 3.9 %collective-permute-start.4 = (bf16[256,1280]{1,0:T(8,128)(2,1)S(1)}, bf16[256,1280]{1,0:T(8,128)(2,1)S(1)}, u32[]{:S(2)}, u32[]{:S(2)}) collective-permute-start(bf16[256,1280]{1,0:T(8,128)(2,1)S(1)} %pad_maximum_fusion), channel_id=1, source_target_pairs={{0,32},{8,40},{16,48},{24,56},{32,64},{40,72},{48,80},{56,88},{64,... | collective-permute-start | bytes 1966088 | tf_op jit(solution)/shard_map/ppermute | solution.py:309
  17.7 0.1 select_reduce_fusion.3
  17.9 0.6 convert_reduce_fusion.1
  18.4 0.1 convert_reduce_fusion.3
  18.6 6.6 %collective-permute-done.4.one.refs_0_ = bf16[256,1280]{1,0:T(8,128)(2,1)S(1)} collective-permute-done((bf16[256,1280]{1,0:T(8,128)(2,1)S(1)}, bf16[256,1280]{1,0:T(8,128)(2,1)S(1)}, u32[]{:S(2)}, u32[]{:S(2)}) %collective-permute-start.4) | collective-permute-done | bytes 655392 | tf_op jit(solution)/shard_map/ppermute | solution.py:309
  25.2 3.1 %collective-permute-start.5 = (bf16[256,1280]{1,0:T(8,128)(2,1)S(1)}, bf16[256,1280]{1,0:T(8,128)(2,1)S(1)}, u32[]{:S(2)}, u32[]{:S(2)}) collective-permute-start(bf16[256,1280]{1,0:T(8,128)(2,1)S(1)} %collective-permute-done.4.one.refs_0_), channel_id=1, source_target_pairs={{0,32},{8,40},{16,48},{24,56},{32,64},{40,72},{48,80},{56,88},{64,... | collective-permute-start | bytes 1966088 | tf_op jit(solution)/shard_map/ppermute | solution.py:309
  28.3 0.1 convert_reduce_fusion.2
  28.5 0.6 convert_reduce_fusion
  29.0 0.7 select_reduce_fusion.1
  29.7 2.8 %collective-permute-start.6 = (bf16[256,1280]{1,0:T(8,128)(2,1)S(1)}, bf16[256,1280]{1,0:T(8,128)(2,1)S(1)}, u32[]{:S(2)}, u32[]{:S(2)}) collective-permute-start(bf16[256,1280]{1,0:T(8,128)(2,1)S(1)} %collective-permute-done.4.one.refs_0_), channel_id=1, source_target_pairs={{0,24},{8,16},{16,8},{24,0},{32,56},{40,48},{48,40},{56,32},{64,88... | collective-permute-start | bytes 1966088 | tf_op jit(solution)/shard_map/ppermute | solution.py:309
  32.5 3.3 %collective-permute-done.5.two.refs_1_ = bf16[256,1280]{1,0:T(8,128)(2,1)S(1)} collective-permute-done((bf16[256,1280]{1,0:T(8,128)(2,1)S(1)}, bf16[256,1280]{1,0:T(8,128)(2,1)S(1)}, u32[]{:S(2)}, u32[]{:S(2)}) %collective-permute-start.5) | collective-permute-done | bytes 655392 | tf_op jit(solution)/shard_map/ppermute | solution.py:309
  35.9 3.4 %collective-permute-start.7 = (bf16[256,1280]{1,0:T(8,128)(2,1)S(1)}, bf16[256,1280]{1,0:T(8,128)(2,1)S(1)}, u32[]{:S(2)}, u32[]{:S(2)}) collective-permute-start(bf16[256,1280]{1,0:T(8,128)(2,1)S(1)} %collective-permute-done.5.two.refs_1_), channel_id=1, source_target_pairs={{0,32},{8,40},{16,48},{24,56},{32,64},{40,72},{48,80},{56,88},{64,... | collective-permute-start | bytes 1966088 | tf_op jit(solution)/shard_map/ppermute | solution.py:309
  39.3 0.7 select_reduce_fusion
  40.0 14.8 %collective-permute-done.16.refs_12_ = bf16[256,1280]{1,0:T(8,128)(2,1)S(1)} collective-permute-done((bf16[256,1280]{1,0:T(8,128)(2,1)}, bf16[256,1280]{1,0:T(8,128)(2,1)S(1)}, u32[]{:S(2)}, u32[]{:S(2)}) %collective-permute-start.16) | collective-permute-done | bytes 655392 | tf_op jit(solution)/shard_map/ppermute | solution.py:309
  54.8 2.9 %collective-permute-start.12 = (bf16[256,1280]{1,0:T(8,128)(2,1)S(1)}, bf16[256,1280]{1,0:T(8,128)(2,1)S(1)}, u32[]{:S(2)}, u32[]{:S(2)}) collective-permute-start(bf16[256,1280]{1,0:T(8,128)(2,1)S(1)} %pad_maximum_fusion), channel_id=1, source_target_pairs={{4,28},{12,20},{20,12},{28,4},{36,60},{44,52},{52,44},{60,36},{68,... | collective-permute-start | bytes 1966088 | tf_op jit(solution)/shard_map/ppermute | solution.py:309
  57.8 0.1 collective-permute-start.17
  57.9 0.5 collective-permute-start.15
  58.4 0.7 collective-permute-start.9
  59.1 0.1 broadcast_select_fusion.3
  59.2 5.8 %collective-permute-start.8 = (bf16[256,1280]{1,0:T(8,128)(2,1)S(1)}, bf16[256,1280]{1,0:T(8,128)(2,1)S(1)}, u32[]{:S(2)}, u32[]{:S(2)}) collective-permute-start(bf16[256,1280]{1,0:T(8,128)(2,1)S(1)} %broadcast_select_fusion.3), channel_id=1, source_target_pairs={{0,32},{8,40},{16,48},{24,56},{32,64},{40,72},{48,80},{56,88},{64,... | collective-permute-start | bytes 1966088 | tf_op jit(solution)/shard_map/ppermute | solution.py:309
  65.0 4.6 %shard_map.104 = (f32[6,8,256]{2,1,0:T(8,128)S(1)}, f32[6,8,256]{2,1,0:T(8,128)S(1)}, f32[2,1024,128]{2,1,0:T(8,128)S(1)}) custom-call(s32[2,8]{1,0:T(2,128)S(1)} %pad_add_fusion.1.bounds, s32[2,1024]{1,0:T(2,128)S(1)} %pad_add_fusion.entries, bf16[256,1280]{1,0:T(8,128)(2,1)S(1)} %collective-permute-done.4.one.refs_0_, ...), custom_call_target="tpu_custom_call" | custom-call | flops 4000000000 | tf_op jit(solution)/shard_map/pallas_call | solution.py:352
  69.6 4.8 %shard_map.105 = (f32[6,8,256]{2,1,0:T(8,128)S(1)}, f32[6,8,256]{2,1,0:T(8,128)S(1)}, f32[2,1024,128]{2,1,0:T(8,128)S(1)}) custom-call(s32[2,8]{1,0:T(2,128)S(1)} %pad_add_fusion.1.bounds, s32[2,1024]{1,0:T(2,128)S(1)} %pad_add_fusion.entries, bf16[256,1280]{1,0:T(8,128)(2,1)S(1)} %collective-permute-done.6.one.refs_2_, ...), custom_call_target="tpu_custom_call" | custom-call | flops 4000000000 | tf_op jit(solution)/shard_map/pallas_call | solution.py:352
  74.4 0.3 broadcast_select_fusion.1
  74.6 1.6 %collective-permute-start.10 = (bf16[256,1280]{1,0:T(8,128)(2,1)S(1)}, bf16[256,1280]{1,0:T(8,128)(2,1)S(1)}, u32[]{:S(2)}, u32[]{:S(2)}) collective-permute-start(bf16[256,1280]{1,0:T(8,128)(2,1)S(1)} %get-tuple-element.42), channel_id=1, source_target_pairs={{0,32},{8,40},{16,48},{24,56},{32,64},{40,72},{48,80},{56,88},{64,... | collective-permute-start | bytes 1966088 | tf_op jit(solution)/shard_map/ppermute | solution.py:309
  76.3 0.7 collective-permute-start.11
  77.0 12.5 %shard_map.106 = (f32[6,8,256]{2,1,0:T(8,128)S(1)}, f32[6,8,256]{2,1,0:T(8,128)S(1)}, f32[2,1024,128]{2,1,0:T(8,128)S(1)}, f32[6,8,256]{2,1,0:T(8,128)S(1)}, f32...) custom-call(s32[2,8]{1,0:T(2,128)S(1)} %pad_add_fusion.1.bounds, s32[2,1024]{1,0:T(2,128)S(1)} %pad_add_fusion.entries, ...), custom_call_target="tpu_custom_call" | custom-call | flops 8999999488 | tf_op jit(solution)/shard_map/pallas_call | solution.py:352
  89.5 0.1 broadcast_select_fusion.refs_7_
  89.6 14.5 %shard_map.107 = (bf16[8,144,256]{2,1,0:T(8,128)(2,1)S(1)}, bf16[8,144,256]{2,1,0:T(8,128)(2,1)S(1)}) custom-call(s32[2,8]{1,0:T(2,128)S(1)} %pad_add_fusion.1.bounds, s32[2,1024]{1,0:T(2,128)S(1)} %pad_add_fusion.entries, bf16[256,1280]{1,0:T(8,128)(2,1)S(1)} %collective-permute-done.4.one.refs_0_, ...), custom_call_target="tpu_custom_call" | custom-call | flops 8999999488 | tf_op jit(solution)/shard_map/pallas_call | solution.py:352
  104.1 3.1 %collective-permute-start.18 = (bf16[8,144,256]{2,1,0:T(8,128)(2,1)S(1)}, bf16[8,144,256]{2,1,0:T(8,128)(2,1)S(1)}, u32[]{:S(2)}, u32[]{:S(2)}) collective-permute-start(bf16[8,144,256]{2,1,0:T(8,128)(2,1)S(1)} %get-tuple-element.31), channel_id=1, source_target_pairs={{0,4},{8,12},{16,20},{24,28},{32,36},{40,44},{48,52},{56,60},{64,6... | collective-permute-start | bytes 1769480 | tf_op jit(solution)/shard_map/ppermute | solution.py:309
  107.2 1.6 %collective-permute-done.18.theirs = bf16[8,144,256]{2,1,0:T(8,128)(2,1)S(1)} collective-permute-done((bf16[8,144,256]{2,1,0:T(8,128)(2,1)S(1)}, bf16[8,144,256]{2,1,0:T(8,128)(2,1)S(1)}, u32[]{:S(2)}, u32[]{:S(2)}) %collective-permute-start.18) | collective-permute-done | bytes 589856 | tf_op jit(solution)/shard_map/ppermute | solution.py:309
  108.8 1.0 shard_map.108
  109.8 16.3 %all-to-all-start = ((bf16[8,144,256]{2,1,0:T(8,128)(2,1)}), bf16[8,144,256]{2,1,0:T(8,128)(2,1)S(1)}, u32[]{:S(2)}, u32[]{:S(2)}) async-start(bf16[8,144,256]{2,1,0:T(8,128)(2,1)} %shard_map.108), calls=%async_computation | async-start | bytes 1179648 | tf_op jit(solution)/shard_map/all_to_all | solution.py:390
  127.4 0.1 pad_add_fusion.2.lengths
  127.5 9.6 %all-to-all-done.parts = bf16[8,144,256]{2,1,0:T(8,128)(2,1)S(1)} async-done(((bf16[8,144,256]{2,1,0:T(8,128)(2,1)}), bf16[8,144,256]{2,1,0:T(8,128)(2,1)S(1)}, u32[]{:S(2)}, u32[]{:S(2)}) %all-to-all-start) | async-done | bytes 589856 | tf_op jit(solution)/shard_map/all_to_all | solution.py:390
  137.1 3.6 %shard_map.109 = (f32[192,128]{1,0:T(8,128)}, f32[8,128]{1,0:T(8,128)S(1)}) custom-call(s32[2]{0:T(128)S(1)} %pad_add_fusion.2.lengths, bf16[8,144,256]{2,1,0:T(8,128)(2,1)S(1)} %all-to-all-done.parts), custom_call_target="tpu_custom_call" | custom-call | tf_op jit(solution)/shard_map/pallas_call | solution.py:391
  140.7 0.5 slice.11
  (27 shorter events, 0.3 us)
Async XLA Ops:
  0.6 9.4 %copy-start = (bf16[4,192,1280]{2,1,0:T(8,128)(2,1)S(1)}, bf16[4,192,1280]{2,1,0:T(8,128)(2,1)}, u32[]{:S(2)}) copy-start(bf16[4,192,1280]{2,1,0:T(8,128)(2,1)} %param.9) | copy-start | bytes 5898244
  0.6 13.1 %collective-permute-start.1 = (s32[4,128]{1,0:T(4,128)}, s32[4,128]{1,0:T(4,128)S(1)}, u32[]{:S(2)}, u32[]{:S(2)}) collective-permute-start(s32[4,128]{1,0:T(4,128)} %param.11), channel_id=1, source_target_pairs={{0,8},{8,0},{16,24},{24,16},{32,40},{40,32},{48,56},{56,48},{64,72... | collective-permute-start | bytes 6152 | tf_op jit(solution)/shard_map/ppermute | solution.py:309
  2.8 14.8 %collective-permute-start.2 = (s32[4,128]{1,0:T(4,128)}, s32[4,128]{1,0:T(4,128)S(1)}, u32[]{:S(2)}, u32[]{:S(2)}) collective-permute-start(s32[4,128]{1,0:T(4,128)} %param.11), channel_id=1, source_target_pairs={{0,12},{8,4},{16,28},{24,20},{32,44},{40,36},{48,60},{56,52},{64,7... | collective-permute-start | bytes 6152 | tf_op jit(solution)/shard_map/ppermute | solution.py:309
  5.6 5.4 %collective-permute-start = (s32[4,128]{1,0:T(4,128)}, s32[4,128]{1,0:T(4,128)S(1)}, u32[]{:S(2)}, u32[]{:S(2)}) collective-permute-start(s32[4,128]{1,0:T(4,128)} %param.11), channel_id=1, source_target_pairs={{0,4},{8,12},{16,20},{24,28},{32,36},{40,44},{48,52},{56,60},{64,6... | collective-permute-start | bytes 6152 | tf_op jit(solution)/shard_map/ppermute | solution.py:309
  7.4 3.7 %collective-permute-start.3 = (bf16[128,1280]{1,0:T(8,128)(2,1)}, bf16[128,1280]{1,0:T(8,128)(2,1)}, u32[]{:S(2)}, u32[]{:S(2)}) collective-permute-start(bf16[128,1280]{1,0:T(8,128)(2,1)} %bitcast.7), channel_id=1, source_target_pairs={{0,4},{8,12},{16,20},{24,28},{32,36},{40,44},{48,52},{56,60},{64,6... | collective-permute-start | bytes 983048 | tf_op jit(solution)/shard_map/ppermute | solution.py:309
  8.0 51.2 %collective-permute-start.13 = (bf16[768,1280]{1,0:T(8,128)(2,1)}, bf16[768,1280]{1,0:T(8,128)(2,1)}, u32[]{:S(2)}, u32[]{:S(2)}) collective-permute-start(bf16[768,1280]{1,0:T(8,128)(2,1)} %bitcast.45), channel_id=1, source_target_pairs={{0,4},{8,12},{16,20},{24,28},{32,36},{40,44},{48,52},{56,60},{64,6... | collective-permute-start | bytes 5898248 | tf_op jit(solution)/shard_map/ppermute | solution.py:309
  8.6 2.4 %copy-start.1 = (s32[4,128]{1,0:T(4,128)S(1)}, s32[4,128]{1,0:T(4,128)}, u32[]{:S(2)}) copy-start(s32[4,128]{1,0:T(4,128)} %param.11) | copy-start | bytes 6148
  10.9 46.8 %collective-permute-start.14 = (bf16[512,1280]{1,0:T(8,128)(2,1)S(1)}, bf16[512,1280]{1,0:T(8,128)(2,1)S(1)}, u32[]{:S(2)}, u32[]{:S(2)}) collective-permute-start(bf16[512,1280]{1,0:T(8,128)(2,1)S(1)} %slice.12), channel_id=1, source_target_pairs={{0,8},{8,0},{16,24},{24,16},{32,40},{40,32},{48,56},{56,48},{64,72... | collective-permute-start | bytes 3932168 | tf_op jit(solution)/shard_map/ppermute | solution.py:309
  11.1 43.7 %collective-permute-start.16 = (bf16[256,1280]{1,0:T(8,128)(2,1)}, bf16[256,1280]{1,0:T(8,128)(2,1)S(1)}, u32[]{:S(2)}, u32[]{:S(2)}) collective-permute-start(bf16[256,1280]{1,0:T(8,128)(2,1)} %slice.13), channel_id=1, source_target_pairs={{0,8},{8,0},{16,24},{24,16},{32,40},{40,32},{48,56},{56,48},{64,72... | collective-permute-start | bytes 1966088 | tf_op jit(solution)/shard_map/ppermute | solution.py:309
  13.7 11.5 %collective-permute-start.4 = (bf16[256,1280]{1,0:T(8,128)(2,1)S(1)}, bf16[256,1280]{1,0:T(8,128)(2,1)S(1)}, u32[]{:S(2)}, u32[]{:S(2)}) collective-permute-start(bf16[256,1280]{1,0:T(8,128)(2,1)S(1)} %pad_maximum_fusion), channel_id=1, source_target_pairs={{0,32},{8,40},{16,48},{24,56},{32,64},{40,72},{48,80},{56,88},{64,... | collective-permute-start | bytes 1966088 | tf_op jit(solution)/shard_map/ppermute | solution.py:309
  25.2 10.6 %collective-permute-start.5 = (bf16[256,1280]{1,0:T(8,128)(2,1)S(1)}, bf16[256,1280]{1,0:T(8,128)(2,1)S(1)}, u32[]{:S(2)}, u32[]{:S(2)}) collective-permute-start(bf16[256,1280]{1,0:T(8,128)(2,1)S(1)} %collective-permute-done.4.one.refs_0_), channel_id=1, source_target_pairs={{0,32},{8,40},{16,48},{24,56},{32,64},{40,72},{48,80},{56,88},{64,... | collective-permute-start | bytes 1966088 | tf_op jit(solution)/shard_map/ppermute | solution.py:309
  29.7 28.2 %collective-permute-start.6 = (bf16[256,1280]{1,0:T(8,128)(2,1)S(1)}, bf16[256,1280]{1,0:T(8,128)(2,1)S(1)}, u32[]{:S(2)}, u32[]{:S(2)}) collective-permute-start(bf16[256,1280]{1,0:T(8,128)(2,1)S(1)} %collective-permute-done.4.one.refs_0_), channel_id=1, source_target_pairs={{0,24},{8,16},{16,8},{24,0},{32,56},{40,48},{48,40},{56,32},{64,88... | collective-permute-start | bytes 1966088 | tf_op jit(solution)/shard_map/ppermute | solution.py:309
  35.9 22.5 %collective-permute-start.7 = (bf16[256,1280]{1,0:T(8,128)(2,1)S(1)}, bf16[256,1280]{1,0:T(8,128)(2,1)S(1)}, u32[]{:S(2)}, u32[]{:S(2)}) collective-permute-start(bf16[256,1280]{1,0:T(8,128)(2,1)S(1)} %collective-permute-done.5.two.refs_1_), channel_id=1, source_target_pairs={{0,32},{8,40},{16,48},{24,56},{32,64},{40,72},{48,80},{56,88},{64,... | collective-permute-start | bytes 1966088 | tf_op jit(solution)/shard_map/ppermute | solution.py:309
  54.8 34.7 %collective-permute-start.12 = (bf16[256,1280]{1,0:T(8,128)(2,1)S(1)}, bf16[256,1280]{1,0:T(8,128)(2,1)S(1)}, u32[]{:S(2)}, u32[]{:S(2)}) collective-permute-start(bf16[256,1280]{1,0:T(8,128)(2,1)S(1)} %pad_maximum_fusion), channel_id=1, source_target_pairs={{4,28},{12,20},{20,12},{28,4},{36,60},{44,52},{52,44},{60,36},{68,... | collective-permute-start | bytes 1966088 | tf_op jit(solution)/shard_map/ppermute | solution.py:309
  57.8 31.8 %collective-permute-start.17 = (bf16[256,1280]{1,0:T(8,128)(2,1)S(1)}, bf16[256,1280]{1,0:T(8,128)(2,1)S(1)}, u32[]{:S(2)}, u32[]{:S(2)}) collective-permute-start(bf16[256,1280]{1,0:T(8,128)(2,1)S(1)} %collective-permute-done.16.refs_12_), channel_id=1, source_target_pairs={{0,4},{8,12},{16,20},{24,28},{32,36},{40,44},{48,52},{56,60},{64,6... | collective-permute-start | bytes 1966088 | tf_op jit(solution)/shard_map/ppermute | solution.py:309
  57.9 19.1 %collective-permute-start.15 = (bf16[512,1280]{1,0:T(8,128)(2,1)S(1)}, bf16[512,1280]{1,0:T(8,128)(2,1)S(1)}, u32[]{:S(2)}, u32[]{:S(2)}) collective-permute-start(bf16[512,1280]{1,0:T(8,128)(2,1)S(1)} %collective-permute-done.14.refs_8_.refs_10_), channel_id=1, source_target_pairs={{0,4},{8,12},{16,20},{24,28},{32,36},{40,44},{48,52},{56,60},{64,6... | collective-permute-start | bytes 3932168 | tf_op jit(solution)/shard_map/ppermute | solution.py:309
  58.4 16.0 %collective-permute-start.9 = (bf16[256,1280]{1,0:T(8,128)(2,1)S(1)}, bf16[256,1280]{1,0:T(8,128)(2,1)S(1)}, u32[]{:S(2)}, u32[]{:S(2)}) collective-permute-start(bf16[256,1280]{1,0:T(8,128)(2,1)S(1)} %collective-permute-done.5.two.refs_1_), channel_id=1, source_target_pairs={{0,24},{8,16},{16,8},{24,0},{32,56},{40,48},{48,40},{56,32},{64,88... | collective-permute-start | bytes 1966088 | tf_op jit(solution)/shard_map/ppermute | solution.py:309
  59.2 15.2 %collective-permute-start.8 = (bf16[256,1280]{1,0:T(8,128)(2,1)S(1)}, bf16[256,1280]{1,0:T(8,128)(2,1)S(1)}, u32[]{:S(2)}, u32[]{:S(2)}) collective-permute-start(bf16[256,1280]{1,0:T(8,128)(2,1)S(1)} %broadcast_select_fusion.3), channel_id=1, source_target_pairs={{0,32},{8,40},{16,48},{24,56},{32,64},{40,72},{48,80},{56,88},{64,... | collective-permute-start | bytes 1966088 | tf_op jit(solution)/shard_map/ppermute | solution.py:309
  74.6 15.0 %collective-permute-start.10 = (bf16[256,1280]{1,0:T(8,128)(2,1)S(1)}, bf16[256,1280]{1,0:T(8,128)(2,1)S(1)}, u32[]{:S(2)}, u32[]{:S(2)}) collective-permute-start(bf16[256,1280]{1,0:T(8,128)(2,1)S(1)} %get-tuple-element.42), channel_id=1, source_target_pairs={{0,32},{8,40},{16,48},{24,56},{32,64},{40,72},{48,80},{56,88},{64,... | collective-permute-start | bytes 1966088 | tf_op jit(solution)/shard_map/ppermute | solution.py:309
  76.3 13.2 %collective-permute-start.11 = (bf16[256,1280]{1,0:T(8,128)(2,1)S(1)}, bf16[256,1280]{1,0:T(8,128)(2,1)S(1)}, u32[]{:S(2)}, u32[]{:S(2)}) collective-permute-start(bf16[256,1280]{1,0:T(8,128)(2,1)S(1)} %collective-permute-done.8.refs_4_), channel_id=1, source_target_pairs={{0,24},{8,16},{16,8},{24,0},{32,56},{40,48},{48,40},{56,32},{64,88... | collective-permute-start | bytes 1966088 | tf_op jit(solution)/shard_map/ppermute | solution.py:309
  104.1 4.7 %collective-permute-start.18 = (bf16[8,144,256]{2,1,0:T(8,128)(2,1)S(1)}, bf16[8,144,256]{2,1,0:T(8,128)(2,1)S(1)}, u32[]{:S(2)}, u32[]{:S(2)}) collective-permute-start(bf16[8,144,256]{2,1,0:T(8,128)(2,1)S(1)} %get-tuple-element.31), channel_id=1, source_target_pairs={{0,4},{8,12},{16,20},{24,28},{32,36},{40,44},{48,52},{56,60},{64,6... | collective-permute-start | bytes 1769480 | tf_op jit(solution)/shard_map/ppermute | solution.py:309
  109.8 27.2 %all-to-all-start = ((bf16[8,144,256]{2,1,0:T(8,128)(2,1)}), bf16[8,144,256]{2,1,0:T(8,128)(2,1)S(1)}, u32[]{:S(2)}, u32[]{:S(2)}) async-start(bf16[8,144,256]{2,1,0:T(8,128)(2,1)} %shard_map.108), calls=%async_computation | async-start | bytes 1179648 | tf_op jit(solution)/shard_map/all_to_all | solution.py:390

commit v4 on v3

--- a/solution.py
+++ b/solution.py
@@ -71,104 +71,109 @@
     return table
 
 
-def score_jobs(w_ref, pair, jobs):
-    def multiply(job):
-        f_ref, t, at, l_ref = job[:4]
+def score_jobs(jobs):
+    def multiply(w, f_ref, t, l_ref, window, *_):
         tile = lax.dot_general(
-            w_ref[pair],
-            f_ref[t * TILE : (t + 1) * TILE, :],
-            (((1,), (1,)), ((), ())),
-            preferred_element_type=jnp.float32,
+            w[...], f_ref[t * TILE : (t + 1) * TILE, :], (((1,), (1,)), ((), ())), preferred_element_type=jnp.float32
         )
-        l_ref[2 * at] = tile[:, :128]
-        l_ref[2 * at + 1] = tile[:, 128:]
-
-    def reduce(job):
-        at, l_ref, m_ref, s_ref = job[2:]
+        l_ref[window] = tile[:, :128]
+        l_ref[window + 1] = tile[:, 128:]
+
+    def reduce(w, f_ref, t, l_ref, window, m_ref, s_ref, at):
         for side in range(2):
             lanes = slice(128 * side, 128 * side + 128)
-            cube = l_ref[2 * at + side].reshape(BLOCK // 8, 8, 128)
+            cube = l_ref[window + side].reshape(w.shape[0] // 8, 8, 128)
             old = m_ref[at, :, lanes]
             top = jnp.maximum(jnp.max(cube, 0), old)
             s_ref[at, :, lanes] = s_ref[at, :, lanes] * jnp.exp(old - top) + jnp.sum(jnp.exp(cube - top[None]), 0)
             m_ref[at, :, lanes] = top
 
-    multiply(jobs[0])
+    multiply(*jobs[0])
     for now, later in zip(jobs, jobs[1:]):
-        multiply(later)
-        reduce(now)
-    reduce(jobs[-1])
-
-
-def jobs_of(parts, l_ref, m_ref, s_ref):
-    return [
-        (f_ref, t, first + t, l_ref, m_ref, s_ref) for f_ref, first in parts for t in range(f_ref.shape[0] // TILE)
-    ]
-
-
-def take_rows(pair, which, bounds, entries, l_ref, p_ref, early=None):
-    def one(k, _):
-        entry = entries[which, k]
-        row = entry // 1024
-        item = entry % 1024
-        for side in range(2):
-            window = (item // 128) * 3 // 2 + side
-
-            def copy(window=window, side=side):
-                p_ref[side, pl.ds(item, 1), :] = l_ref[window, pl.ds(row, 1), :]
-
-            if early is None:
-                copy()
-            else:
-                inside = window % (WINDOWS // 2) < EARLY // 128
-                pl.when(inside if early else jnp.logical_not(inside))(copy)
+        multiply(*later)
+        reduce(*now)
+    reduce(*jobs[-1])
+
+
+def jobs_of(w, parts, l_ref, m_ref, s_ref):
+    jobs = []
+    for f_ref, first in parts:
+        for t in range(f_ref.shape[0] // TILE):
+            jobs.append((w, f_ref, t, l_ref, 2 * len(jobs), m_ref, s_ref, first + t))
+    return jobs
+
+
+GROUP = 8
+
+
+def take_rows(first, last, which, bounds, entries, l_ref, p_ref, early=None):
+    low, high = bounds[which, first], bounds[which, last]
+
+    def group(g, _):
+        found = []
+        for j in range(GROUP):
+            entry = entries[which, jnp.minimum(low + g * GROUP + j, high - 1)]
+            column = (entry >> 10) - first * BLOCK
+            item = entry & 1023
+            for side in range(2):
+                window = (((item >> 7) * 3) >> 1) + side
+                to = item
+                if early is not None:
+                    within = jnp.where(window >= 6, window - 6, window)
+                    far = window >= 6
+                    if early:
+                        inside = within < EARLY // 128
+                        window = jnp.where(far, window - 2, window)
+                    else:
+                        inside = within >= EARLY // 128
+                        window = jnp.where(far, window - 8, window - 4)
+                    window = jnp.where(inside, window, 0)
+                    to = jnp.where(inside, item, 1024 + j)
+                found.append((side, to, l_ref[window, pl.ds(column, 1), :]))
+        for side, to, row in found:
+            p_ref[side, pl.ds(to, 1), :] = row
         return 0
 
-    lax.fori_loop(bounds[which, pair], bounds[which, pair + 1], one, 0)
-
-
-def fill_pair(w_ref, pair, one, two):
-    w_ref[pair, 0 : BLOCK // 2] = one[...]
-    w_ref[pair, BLOCK // 2 : BLOCK] = two[...]
+    lax.fori_loop(0, (high - low + GROUP - 1) >> 3, group, 0)
+
+
+def fill_columns(w_ref, blocks):
+    for k, block in enumerate(blocks):
+        w_ref[k * (BLOCK // 2) : (k + 1) * (BLOCK // 2)] = block[...]
 
 
 def first_kernel(bounds, entries, one, two, fa, fb, m, s, p, w_ref, l_ref):
     m[...] = jnp.full_like(m, LOWEST)
     s[...] = jnp.zeros_like(s)
     p[...] = jnp.zeros_like(p)
-    fill_pair(w_ref, 0, one, two)
-    score_jobs(w_ref, 0, jobs_of(((fa, 0), (fb, 3)), l_ref, m, s))
-    take_rows(0, 0, bounds, entries, l_ref, p)
+    fill_columns(w_ref, (one, two))
+    score_jobs(jobs_of(w_ref, ((fa, 0), (fb, 3)), l_ref, m, s))
+    take_rows(0, 1, 0, bounds, entries, l_ref, p)
 
 
 def second_kernel(bounds, entries, one, two, fa, fb, m_in, s_in, p_in, m, s, p, w_ref, l_ref):
     m[...] = m_in[...]
     s[...] = s_in[...]
     p[...] = p_in[...]
-    fill_pair(w_ref, 0, one, two)
-    score_jobs(w_ref, 0, jobs_of(((fa, 0), (fb, 3)), l_ref, m, s))
-    take_rows(1, 0, bounds, entries, l_ref, p)
+    fill_columns(w_ref, (one, two))
+    score_jobs(jobs_of(w_ref, ((fa, 0), (fb, 3)), l_ref, m, s))
+    take_rows(1, 2, 0, bounds, entries, l_ref, p)
 
 
 def third_kernel(bounds, entries, *refs):
-    blocks, (fa, fb, ga, gb, m_in, s_in, p_in), (m, s, p, mb, sb, pb, w_ref, l_ref) = refs[:6], refs[6:13], refs[13:]
+    blocks, (fa, fb, ga, gb, m_in, s_in, p_in), refs = refs[:6], refs[6:13], refs[13:]
+    m, s, p, mb, sb, pb, lb_ref, w_ref, l_ref = refs
     m[...] = m_in[...]
     s[...] = s_in[...]
     p[...] = p_in[...]
     mb[...] = jnp.full_like(mb, LOWEST)
     sb[...] = jnp.zeros_like(sb)
     pb[...] = jnp.zeros_like(pb)
-    for pair in range(3):
-        fill_pair(w_ref, pair, *blocks[2 * pair : 2 * pair + 2])
-    score_jobs(w_ref, 2, jobs_of(((fa, 0), (fb, 3)), l_ref, m, s))
-    take_rows(2, 0, bounds, entries, l_ref, p)
-
-    def over(pair, _):
-        score_jobs(w_ref, pair, jobs_of(((ga, 0), (gb, 3)), l_ref, mb, sb))
-        take_rows(pair, 1, bounds, entries, l_ref, pb, True)
-        return 0
-
-    lax.fori_loop(0, 3, over, 0)
+    fill_columns(w_ref, blocks)
+    near = jobs_of(w_ref.at[2 * BLOCK : 3 * BLOCK], ((fa, 0), (fb, 3)), l_ref, m, s)
+    score_jobs(near + jobs_of(w_ref, ((ga, 0), (gb, 3)), lb_ref, mb, sb))
+    take_rows(2, 3, 0, bounds, entries, l_ref, p)
+    take_rows(0, 3, 1, bounds, entries, lb_ref, pb, True)
 
 
 def split_parts(value):
@@ -187,22 +192,17 @@
 
 def last_kernel(bounds, entries, *refs):
     blocks, (fa, fb, ga, gb, ha, hb), state, (kept, given) = refs[:8], refs[8:14], refs[14:20], refs[20:22]
-    m, s, p, mb, sb, pb, lse_ref, lb_ref, w_ref, l_ref = refs[22:]
+    m, s, p, mb, sb, pb, lse_ref, lb_ref, lc_ref, w_ref, l_ref = refs[22:]
     for ref, value in zip((m, s, p, mb, sb, pb), state):
         ref[...] = value[...]
-    for pair in range(PAIRS):
-        fill_pair(w_ref, pair, *blocks[2 * pair : 2 * pair + 2])
-
-    def over(pair, _):
-        score_jobs(w_ref, pair, jobs_of(((ha, 2), (hb, 5)), lb_ref, mb, sb))
-        take_rows(pair, 1, bounds, entries, lb_ref, pb, False)
-        return 0
-
-    lax.fori_loop(0, PAIRS, over, 0)
-    later = jobs_of(((ga, 0), (gb, 3)), lb_ref, mb, sb)
-    score_jobs(w_ref, 3, later + jobs_of(((fa, 0), (fb, 3)), l_ref, m, s))
-    take_rows(3, 1, bounds, entries, lb_ref, pb, True)
-    take_rows(3, 0, bounds, entries, l_ref, p)
+    fill_columns(w_ref, blocks)
+    final = w_ref.at[3 * BLOCK : 4 * BLOCK]
+    jobs = jobs_of(w_ref, ((ha, 2), (hb, 5)), lc_ref, mb, sb)
+    jobs += jobs_of(final, ((ga, 0), (gb, 3)), lb_ref, mb, sb)
+    score_jobs(jobs + jobs_of(final, ((fa, 0), (fb, 3)), l_ref, m, s))
+    take_rows(0, 4, 1, bounds, entries, lc_ref, pb, False)
+    take_rows(3, 4, 1, bounds, entries, lb_ref, pb, True)
+    take_rows(3, 4, 0, bounds, entries, l_ref, p)
     for group, (mm, ss, pp) in enumerate(((m, s, p), (mb, sb, pb))):
         for t in range(WINDOWS // 2):
             top = jnp.max(mm[t], 0, keepdims=True)
@@ -226,17 +226,23 @@
 
 def join_kernel(where, mine, theirs, out):
     odd = where[0]
+    early_lanes = lax.broadcasted_iota(jnp.int32, (64, 128), 1) < 64
     for group in range(2):
         for k in range(4):
             rec = group * 4 + k
             to = (group ^ odd) * 4 + k
             one, two = mine[rec], theirs[rec]
             picked = one[0:128].astype(jnp.float32) + two[0:128].astype(jnp.float32)
-            out[to, 0:128, :] = picked.astype(jnp.bfloat16)
+            out[to, 0:128, :] = picked[:, 0:128].astype(jnp.bfloat16)
+            tail = picked[:, 128:256]
+            tail = jnp.where(early_lanes, tail[0:64], pltpu.roll(tail[64:128], 64, 1))
+            out[to, 128:192, :] = tail.astype(jnp.bfloat16)
             a, b = joined_parts(one[128:144]), joined_parts(two[128:144])
             top = jnp.maximum(a, b)
             value = top + jnp.log(jnp.exp(a - top) + jnp.exp(b - top))
-            out[to, 128:144, :] = split_parts(jnp.broadcast_to(value, (8, TILE)))
+            for side in range(2):
+                lanes = jnp.broadcast_to(value[:, 128 * side : 128 * side + 128], (8, 128))
+                out[to, 192 + 16 * side : 208 + 16 * side, :] = split_parts(lanes)
 
 
 DEPTH = 8
@@ -244,13 +250,17 @@
 
 def align_kernel(lengths, parts, logprob, path, turned, scores):
     frames = logprob.shape[0]
-    picked = parts[0, 0:128, :].astype(jnp.float32)
+    picked = parts[0, 0:192, :].astype(jnp.float32)
     for k in range(1, 8):
-        picked = picked + parts[k, 0:128, :].astype(jnp.float32)
-    norms = [joined_parts(parts[k, 128:144, :]) for k in range(8)]
-    top = functools.reduce(jnp.maximum, norms)
-    norm = top + jnp.log(sum(jnp.exp(value - top) for value in norms))
-    table = (picked - norm).T[:frames]
+        picked = picked + parts[k, 0:192, :].astype(jnp.float32)
+    sides = []
+    for side in range(2):
+        rows = slice(192 + 16 * side, 208 + 16 * side)
+        norms = [joined_parts(parts[k, rows, :]) for k in range(8)]
+        top = functools.reduce(jnp.maximum, norms)
+        sides.append(top + jnp.log(sum(jnp.exp(value - top) for value in norms)))
+    tail = jnp.concatenate([picked[128:192], pltpu.roll(picked[128:192], 64, 1)], 0) - sides[1]
+    table = jnp.concatenate([(picked[0:128] - sides[0]).T, tail.T[0:64]], 0)
     logprob[...] = table
     lanes = lax.broadcasted_iota(jnp.int32, (1, 128), 1)
     for d in range(DEPTH):
@@ -287,7 +297,7 @@
     mine = (flat // (NZ * NY * 256) == vocab_index) & ((owner_y == y) | (owner_y == 3 - y))
     place = jnp.where(mine, place, 2 * PAIRS)
     pair = place // 2
-    column = place % 2 * 256 + local % 256
+    column = place * 256 + (local // 128 % 2 ^ core) * 128 + local % 128
     ids = lax.iota(jnp.int32, flat.shape[0])
     sort_key = pair * 1024 + ids
     rank = jnp.sum((sort_key[None, :] < sort_key[:, None]).astype(jnp.int32), 1)
@@ -314,7 +324,7 @@
     own = head_weight.T
     other = both(own, other_core)
     is0 = core == 0
-    o0 = jnp.concatenate([jnp.where(is0, own, other), jnp.where(is0, other, own)])
+    o0 = jnp.concatenate([own, other])
     op1 = send(o0, up, down)
     op2 = send(o0, None, mirror)
     fa = features.reshape(rows, width)
@@ -338,13 +348,14 @@
 
     ba, ea = label_entries(jnp.concatenate([labels, l1]), vocab_index, z, y, core)
     bb, eb = label_entries(jnp.concatenate([l2, l3]), vocab_index, z, y, core)
-    bounds, entries = jnp.stack([ba, bb]), jnp.stack([ea, eb])
+    bounds = jnp.stack([ba, bb])
+    entries = jnp.stack([ea, eb])
 
     f32 = jnp.float32
     state = (
         jax.ShapeDtypeStruct((WINDOWS // 2, 8, TILE), f32),
         jax.ShapeDtypeStruct((WINDOWS // 2, 8, TILE), f32),
-        jax.ShapeDtypeStruct((2, 8 * 128, 128), f32),
+        jax.ShapeDtypeStruct((2, 8 * 128 + GROUP, 128), f32),
     )
     logits_scratch = pltpu.VMEM((WINDOWS, BLOCK, 128), f32)
 
@@ -354,14 +365,22 @@
             out_shape=out_shape,
             in_specs=[SMEM, SMEM, *([VMEM] * len(operands))],
             out_specs=[VMEM] * len(out_shape),
-            scratch_shapes=[*extra, pltpu.VMEM((pairs, BLOCK, width), jnp.bfloat16), logits_scratch],
+            scratch_shapes=[*extra, pltpu.VMEM((pairs * BLOCK, width), jnp.bfloat16), logits_scratch],
             cost_estimate=pl.CostEstimate(flops=int(gflop * 1e9), bytes_accessed=0, transcendentals=0),
             compiler_params=pltpu.CompilerParams(vmem_limit_bytes=limit * 2**20),
         )(bounds, entries, *operands)
 
-    ma = call(first_kernel, state, (op1, op3, fa, fb), 1, 4, 14)
-    ma = call(second_kernel, state, (op4, op5, fa, fb, *ma), 1, 4, 14)
-    *ma, mb, sb, pb = call(third_kernel, state + state, (op1, op3, op4, op5, op6, s1, fa, fb, ga, gb, *ma), 3, 9, 18)
+    ma = call(first_kernel, state, (op1, op3, fa, fb), 1, 4, 8)
+    ma = call(second_kernel, state, (op4, op5, fa, fb, *ma), 1, 4, 8)
+    *ma, mb, sb, pb = call(
+        third_kernel,
+        state + state,
+        (op1, op3, op4, op5, op6, s1, fa, fb, ga, gb, *ma),
+        3,
+        9,
+        17,
+        [pltpu.VMEM((2 * EARLY // 128, 3 * BLOCK, 128), f32)],
+    )
     packed = jax.ShapeDtypeStruct((8, 144, TILE), jnp.bfloat16)
     kept, given = call(
         last_kernel,
@@ -369,13 +388,15 @@
         (op1, op3, op4, op5, op6, s1, op8, s2, fa, fb, ga, gb, ha, hb, *ma, mb, sb, pb),
         PAIRS,
         9,
-        24,
-        [*(pltpu.VMEM(leaf.shape, leaf.dtype) for leaf in state + state), pltpu.VMEM((WINDOWS, 8, 128), f32), logits_scratch],
+        20,
+        [*(pltpu.VMEM(leaf.shape, leaf.dtype) for leaf in state + state), pltpu.VMEM((WINDOWS, 8, 128), f32),
+         pltpu.VMEM((2 * EARLY // 128, BLOCK, 128), f32),
+         pltpu.VMEM((WINDOWS - 2 * EARLY // 128, 4 * BLOCK, 128), f32)],
     )
     taken = both(given, other_core)
     sent = pl.pallas_call(
         join_kernel,
-        out_shape=packed,
+        out_shape=jax.ShapeDtypeStruct((8, 224, 128), jnp.bfloat16),
         in_specs=[SMEM, VMEM, VMEM],
         out_specs=VMEM,
         compiler_params=pltpu.CompilerParams(vmem_limit_bytes=8 * 2**20),

time: 142 us -> 123 us (0.87)
  starting transfers between devices: 52 us -> 42.3 us
  Pallas kernels: 40.9 us -> 33.9 us
    all_to_all x1, starting transfers between devices: 16.3 us -> 5.38 us  [body(): lax.all_to_all(sent, ('rec', 'vocab'), 0, 0, tiled=True, axis_index_group...]
    pallas_call x4, Pallas kernels: 36.3 us -> 29.4 us  [call(): pl.pallas_call(kernel, out_shape=out_shape, in_specs=[SMEM, SMEM, *[VMEM]...]
  transfers between devices with their start and end apart: 20 -> 20, of which waited for: 5 -> 5; matrix products, arithmetic and copies ran while one was open for 7% -> 6% of each run, Pallas kernels for 15% -> 15%
where the time goes in v4:
time: 123 us
  starting transfers between devices  42.3 us (34%)
  waiting for transfers between devices  36.1 us (29%)
  Pallas kernels  33.9 us (28%)
  other arithmetic  4.22 us (3%)
  local copies, waits for them, and re-layouts  4.18 us (3%)
  between operations  2.22 us (2%)
    ppermute x19, starting transfers between devices, send(): lax.ppermute(array, 'rec', moves(step0, step1 if step1 is not None else N...  37 us
    pallas_call x4, Pallas kernels, call(): pl.pallas_call(kernel, out_shape=out_shape, in_specs=[SMEM, SMEM, *[VMEM]...  29.4 us
    ppermute x19, waiting for transfers between devices, send(): lax.ppermute(array, 'rec', moves(step0, step1 if step1 is not None else N...  27.9 us
    all_to_all x1, waiting for transfers between devices, body(): lax.all_to_all(sent, ('rec', 'vocab'), 0, 0, tiled=True, axis_index_group...  8.17 us
    all_to_all x1, starting transfers between devices, body(): lax.all_to_all(sent, ('rec', 'vocab'), 0, 0, tiled=True, axis_index_group...  5.38 us
    pallas_call x1, Pallas kernels, body(): pl.pallas_call(align_kernel, out_shape=[jax.ShapeDtypeStruct((frames, 128...  3.61 us
    slice x1, local copies, waits for them, and re-layouts, body(): ga = both(fa[:EARLY], beside)  2.47 us
  transfers between devices with their start and end apart: 20, of which 5 were waited for; matrix products, arithmetic and copies ran while one was open for 6% of the time, Pallas kernels for 15%

profile of v4, /device:TPU:1, one launch (start us, length us, event | category | flops | bytes accessed | tf_op | source)
XLA Modules:
  0.0 123.0 jit_solution(10247006461716480614)
XLA Ops:
  0.6 0.0 copy-start
  0.6 2.2 %collective-permute-start.1 = (s32[4,128]{1,0:T(4,128)}, s32[4,128]{1,0:T(4,128)S(1)}, u32[]{:S(2)}, u32[]{:S(2)}) collective-permute-start(s32[4,128]{1,0:T(4,128)} %param.11), channel_id=1, source_target_pairs={{0,8},{8,0},{16,24},{24,16},{32,40},{40,32},{48,56},{56,48},{64,72... | collective-permute-start | bytes 6152 | tf_op jit(solution)/shard_map/ppermute | solution.py:319
  2.8 2.7 %collective-permute-start.2 = (s32[4,128]{1,0:T(4,128)}, s32[4,128]{1,0:T(4,128)S(1)}, u32[]{:S(2)}, u32[]{:S(2)}) collective-permute-start(s32[4,128]{1,0:T(4,128)} %param.11), channel_id=1, source_target_pairs={{0,12},{8,4},{16,28},{24,20},{32,44},{40,36},{48,60},{56,52},{64,7... | collective-permute-start | bytes 6152 | tf_op jit(solution)/shard_map/ppermute | solution.py:319
  5.6 1.1 copy.12
  6.7 0.6 collective-permute-start.3
  7.3 0.1 collective-permute-start.13
  7.4 0.7 broadcast_select_fusion.4
  8.1 2.5 %slice.12 = bf16[512,1280]{1,0:T(8,128)(2,1)} slice(bf16[768,1280]{1,0:T(8,128)(2,1)} %bitcast.44), slice={[0:512], [0:1280]} | slice | bytes 2621440 | tf_op jit(solution)/shard_map/slice | solution.py:335
  10.6 0.0 collective-permute-done
  10.6 0.1 collective-permute-start.14
  10.8 0.0 collective-permute-done.3
  10.8 1.5 %collective-permute-start.16 = (bf16[256,1280]{1,0:T(8,128)(2,1)S(1)}, bf16[256,1280]{1,0:T(8,128)(2,1)S(1)}, u32[]{:S(2)}, u32[]{:S(2)}) collective-permute-start(bf16[256,1280]{1,0:T(8,128)(2,1)S(1)} %slice.13), channel_id=1, source_target_pairs={{0,8},{8,0},{16,24},{24,16},{32,40},{40,32},{48,56},{56,48},{64,72... | collective-permute-start | bytes 1966088 | tf_op jit(solution)/shard_map/ppermute | solution.py:319
  12.4 3.9 %collective-permute-start.4 = (bf16[256,1280]{1,0:T(8,128)(2,1)S(1)}, bf16[256,1280]{1,0:T(8,128)(2,1)S(1)}, u32[]{:S(2)}, u32[]{:S(2)}) collective-permute-start(bf16[256,1280]{1,0:T(8,128)(2,1)S(1)} %pad_maximum_fusion), channel_id=1, source_target_pairs={{0,32},{8,40},{16,48},{24,56},{32,64},{40,72},{48,80},{56,88},{64,... | collective-permute-start | bytes 1966088 | tf_op jit(solution)/shard_map/ppermute | solution.py:319
  16.4 0.1 select_reduce_fusion.3
  16.6 7.3 %collective-permute-done.4.one.refs_0_ = bf16[256,1280]{1,0:T(8,128)(2,1)S(1)} collective-permute-done((bf16[256,1280]{1,0:T(8,128)(2,1)S(1)}, bf16[256,1280]{1,0:T(8,128)(2,1)S(1)}, u32[]{:S(2)}, u32[]{:S(2)}) %collective-permute-start.4) | collective-permute-done | bytes 655392 | tf_op jit(solution)/shard_map/ppermute | solution.py:319
  23.8 3.1 %collective-permute-start.5 = (bf16[256,1280]{1,0:T(8,128)(2,1)S(1)}, bf16[256,1280]{1,0:T(8,128)(2,1)S(1)}, u32[]{:S(2)}, u32[]{:S(2)}) collective-permute-start(bf16[256,1280]{1,0:T(8,128)(2,1)S(1)} %collective-permute-done.4.one.refs_0_), channel_id=1, source_target_pairs={{0,32},{8,40},{16,48},{24,56},{32,64},{40,72},{48,80},{56,88},{64,... | collective-permute-start | bytes 1966088 | tf_op jit(solution)/shard_map/ppermute | solution.py:319
  27.0 0.1 convert_reduce_fusion.3
  27.1 0.6 convert_reduce_fusion.1
  27.6 0.6 convert_reduce_fusion
  28.3 2.8 %collective-permute-start.6 = (bf16[256,1280]{1,0:T(8,128)(2,1)S(1)}, bf16[256,1280]{1,0:T(8,128)(2,1)S(1)}, u32[]{:S(2)}, u32[]{:S(2)}) collective-permute-start(bf16[256,1280]{1,0:T(8,128)(2,1)S(1)} %collective-permute-done.4.one.refs_0_), channel_id=1, source_target_pairs={{0,24},{8,16},{16,8},{24,0},{32,56},{40,48},{48,40},{56,32},{64,88... | collective-permute-start | bytes 1966088 | tf_op jit(solution)/shard_map/ppermute | solution.py:319
  31.1 3.4 %collective-permute-done.5.two.refs_1_ = bf16[256,1280]{1,0:T(8,128)(2,1)S(1)} collective-permute-done((bf16[256,1280]{1,0:T(8,128)(2,1)S(1)}, bf16[256,1280]{1,0:T(8,128)(2,1)S(1)}, u32[]{:S(2)}, u32[]{:S(2)}) %collective-permute-start.5) | collective-permute-done | bytes 655392 | tf_op jit(solution)/shard_map/ppermute | solution.py:319
  34.5 3.4 %collective-permute-start.7 = (bf16[256,1280]{1,0:T(8,128)(2,1)S(1)}, bf16[256,1280]{1,0:T(8,128)(2,1)S(1)}, u32[]{:S(2)}, u32[]{:S(2)}) collective-permute-start(bf16[256,1280]{1,0:T(8,128)(2,1)S(1)} %collective-permute-done.5.two.refs_1_), channel_id=1, source_target_pairs={{0,32},{8,40},{16,48},{24,56},{32,64},{40,72},{48,80},{56,88},{64,... | collective-permute-start | bytes 1966088 | tf_op jit(solution)/shard_map/ppermute | solution.py:319
  37.9 0.1 convert_reduce_fusion.2
  38.0 0.7 select_reduce_fusion.1
  38.7 0.7 select_reduce_fusion
  39.4 15.5 %collective-permute-done.16.refs_12_ = bf16[256,1280]{1,0:T(8,128)(2,1)S(1)} collective-permute-done((bf16[256,1280]{1,0:T(8,128)(2,1)S(1)}, bf16[256,1280]{1,0:T(8,128)(2,1)S(1)}, u32[]{:S(2)}, u32[]{:S(2)}) %collective-permute-start.16) | collective-permute-done | bytes 655392 | tf_op jit(solution)/shard_map/ppermute | solution.py:319
  54.9 2.9 %collective-permute-start.12 = (bf16[256,1280]{1,0:T(8,128)(2,1)S(1)}, bf16[256,1280]{1,0:T(8,128)(2,1)S(1)}, u32[]{:S(2)}, u32[]{:S(2)}) collective-permute-start(bf16[256,1280]{1,0:T(8,128)(2,1)S(1)} %pad_maximum_fusion), channel_id=1, source_target_pairs={{4,28},{12,20},{20,12},{28,4},{36,60},{44,52},{52,44},{60,36},{68,... | collective-permute-start | bytes 1966088 | tf_op jit(solution)/shard_map/ppermute | solution.py:319
  57.8 0.1 collective-permute-start.17
  57.9 0.5 collective-permute-start.15
  58.4 0.7 collective-permute-start.9
  59.1 0.1 broadcast_select_fusion.3
  59.2 5.8 %collective-permute-start.8 = (bf16[256,1280]{1,0:T(8,128)(2,1)S(1)}, bf16[256,1280]{1,0:T(8,128)(2,1)S(1)}, u32[]{:S(2)}, u32[]{:S(2)}) collective-permute-start(bf16[256,1280]{1,0:T(8,128)(2,1)S(1)} %broadcast_select_fusion.3), channel_id=1, source_target_pairs={{0,32},{8,40},{16,48},{24,56},{32,64},{40,72},{48,80},{56,88},{64,... | collective-permute-start | bytes 1966088 | tf_op jit(solution)/shard_map/ppermute | solution.py:319
  65.1 4.3 %shard_map.104 = (f32[6,8,256]{2,1,0:T(8,128)S(1)}, f32[6,8,256]{2,1,0:T(8,128)S(1)}, f32[2,1032,128]{2,1,0:T(8,128)S(1)}) custom-call(s32[2,8]{1,0:T(2,128)S(1)} %pad_add_fusion.1.bounds, s32[2,1024]{1,0:T(2,128)S(1)} %pad_add_fusion.entries, bf16[256,1280]{1,0:T(8,128)(2,1)S(1)} %collective-permute-done.4.one.refs_0_, ...), custom_call_target="tpu_custom_call" | custom-call | flops 4000000000 | tf_op jit(solution)/shard_map/pallas_call | solution.py:363
  69.4 4.4 %shard_map.105 = (f32[6,8,256]{2,1,0:T(8,128)S(1)}, f32[6,8,256]{2,1,0:T(8,128)S(1)}, f32[2,1032,128]{2,1,0:T(8,128)S(1)}) custom-call(s32[2,8]{1,0:T(2,128)S(1)} %pad_add_fusion.1.bounds, s32[2,1024]{1,0:T(2,128)S(1)} %pad_add_fusion.entries, bf16[256,1280]{1,0:T(8,128)(2,1)S(1)} %collective-permute-done.6.one.refs_2_, ...), custom_call_target="tpu_custom_call" | custom-call | flops 4000000000 | tf_op jit(solution)/shard_map/pallas_call | solution.py:363
  73.8 0.3 broadcast_select_fusion.1
  74.1 2.2 %collective-permute-start.10 = (bf16[256,1280]{1,0:T(8,128)(2,1)S(1)}, bf16[256,1280]{1,0:T(8,128)(2,1)S(1)}, u32[]{:S(2)}, u32[]{:S(2)}) collective-permute-start(bf16[256,1280]{1,0:T(8,128)(2,1)S(1)} %get-tuple-element.40), channel_id=1, source_target_pairs={{0,32},{8,40},{16,48},{24,56},{32,64},{40,72},{48,80},{56,88},{64,... | collective-permute-start | bytes 1966088 | tf_op jit(solution)/shard_map/ppermute | solution.py:319
  76.4 0.7 collective-permute-start.11
  77.1 10.1 %shard_map.106 = (f32[6,8,256]{2,1,0:T(8,128)S(1)}, f32[6,8,256]{2,1,0:T(8,128)S(1)}, f32[2,1032,128]{2,1,0:T(8,128)S(1)}, f32[6,8,256]{2,1,0:T(8,128)S(1)}, f32...) custom-call(s32[2,8]{1,0:T(2,128)S(1)} %pad_add_fusion.1.bounds, s32[2,1024]{1,0:T(2,128)S(1)} %pad_add_fusion.entries, ...), custom_call_target="tpu_custom_call" | custom-call | flops 8999999488 | tf_op jit(solution)/shard_map/pallas_call | solution.py:363
  87.2 0.1 broadcast_select_fusion.refs_7_
  87.3 10.5 %shard_map.107 = (bf16[8,144,256]{2,1,0:T(8,128)(2,1)S(1)}, bf16[8,144,256]{2,1,0:T(8,128)(2,1)S(1)}) custom-call(s32[2,8]{1,0:T(2,128)S(1)} %pad_add_fusion.1.bounds, s32[2,1024]{1,0:T(2,128)S(1)} %pad_add_fusion.entries, bf16[256,1280]{1,0:T(8,128)(2,1)S(1)} %collective-permute-done.4.one.refs_0_, ...), custom_call_target="tpu_custom_call" | custom-call | flops 8999999488 | tf_op jit(solution)/shard_map/pallas_call | solution.py:363
  97.8 3.5 %collective-permute-start.18 = (bf16[8,144,256]{2,1,0:T(8,128)(2,1)S(1)}, bf16[8,144,256]{2,1,0:T(8,128)(2,1)S(1)}, u32[]{:S(2)}, u32[]{:S(2)}) collective-permute-start(bf16[8,144,256]{2,1,0:T(8,128)(2,1)S(1)} %get-tuple-element.31), channel_id=1, source_target_pairs={{0,4},{8,12},{16,20},{24,28},{32,36},{40,44},{48,52},{56,60},{64,6... | collective-permute-start | bytes 1769480 | tf_op jit(solution)/shard_map/ppermute | solution.py:319
  101.3 1.6 %collective-permute-done.18.theirs = bf16[8,144,256]{2,1,0:T(8,128)(2,1)S(1)} collective-permute-done((bf16[8,144,256]{2,1,0:T(8,128)(2,1)S(1)}, bf16[8,144,256]{2,1,0:T(8,128)(2,1)S(1)}, u32[]{:S(2)}, u32[]{:S(2)}) %collective-permute-start.18) | collective-permute-done | bytes 589856 | tf_op jit(solution)/shard_map/ppermute | solution.py:319
  102.9 1.0 shard_map.108
  103.9 5.4 %all-to-all-start = ((bf16[8,224,128]{2,1,0:T(8,128)(2,1)}), bf16[8,224,128]{2,1,0:T(8,128)(2,1)S(1)}, u32[]{:S(2)}, u32[]{:S(2)}) async-start(bf16[8,224,128]{2,1,0:T(8,128)(2,1)} %shard_map.108), calls=%async_computation | async-start | bytes 917504 | tf_op jit(solution)/shard_map/all_to_all | solution.py:411
  110.6 0.1 pad_add_fusion.2.lengths
  110.7 8.2 %all-to-all-done.parts = bf16[8,224,128]{2,1,0:T(8,128)(2,1)S(1)} async-done(((bf16[8,224,128]{2,1,0:T(8,128)(2,1)}), bf16[8,224,128]{2,1,0:T(8,128)(2,1)S(1)}, u32[]{:S(2)}, u32[]{:S(2)}) %all-to-all-start) | async-done | bytes 458784 | tf_op jit(solution)/shard_map/all_to_all | solution.py:411
  118.8 3.6 %shard_map.109 = (f32[192,128]{1,0:T(8,128)}, f32[8,128]{1,0:T(8,128)S(1)}) custom-call(s32[2]{0:T(128)S(1)} %pad_add_fusion.2.lengths, bf16[8,224,128]{2,1,0:T(8,128)(2,1)S(1)} %all-to-all-done.parts), custom_call_target="tpu_custom_call" | custom-call | tf_op jit(solution)/shard_map/pallas_call | solution.py:412
  122.4 0.5 slice.11
  (26 shorter events, 0.4 us)
Async XLA Ops:
  0.6 9.9 %copy-start = (bf16[4,192,1280]{2,1,0:T(8,128)(2,1)S(1)}, bf16[4,192,1280]{2,1,0:T(8,128)(2,1)}, u32[]{:S(2)}) copy-start(bf16[4,192,1280]{2,1,0:T(8,128)(2,1)} %param.9) | copy-start | bytes 5898244
  0.6 11.7 %collective-permute-start.1 = (s32[4,128]{1,0:T(4,128)}, s32[4,128]{1,0:T(4,128)S(1)}, u32[]{:S(2)}, u32[]{:S(2)}) collective-permute-start(s32[4,128]{1,0:T(4,128)} %param.11), channel_id=1, source_target_pairs={{0,8},{8,0},{16,24},{24,16},{32,40},{40,32},{48,56},{56,48},{64,72... | collective-permute-start | bytes 6152 | tf_op jit(solution)/shard_map/ppermute | solution.py:319
  2.8 13.5 %collective-permute-start.2 = (s32[4,128]{1,0:T(4,128)}, s32[4,128]{1,0:T(4,128)S(1)}, u32[]{:S(2)}, u32[]{:S(2)}) collective-permute-start(s32[4,128]{1,0:T(4,128)} %param.11), channel_id=1, source_target_pairs={{0,12},{8,4},{16,28},{24,20},{32,44},{40,36},{48,60},{56,52},{64,7... | collective-permute-start | bytes 6152 | tf_op jit(solution)/shard_map/ppermute | solution.py:319
  5.6 5.1 %collective-permute-start = (s32[4,128]{1,0:T(4,128)}, s32[4,128]{1,0:T(4,128)S(1)}, u32[]{:S(2)}, u32[]{:S(2)}) collective-permute-start(s32[4,128]{1,0:T(4,128)} %param.11), channel_id=1, source_target_pairs={{0,4},{8,12},{16,20},{24,28},{32,36},{40,44},{48,52},{56,60},{64,6... | collective-permute-start | bytes 6152 | tf_op jit(solution)/shard_map/ppermute | solution.py:319
  6.7 4.1 %collective-permute-start.3 = (bf16[128,1280]{1,0:T(8,128)(2,1)S(1)}, bf16[128,1280]{1,0:T(8,128)(2,1)S(1)}, u32[]{:S(2)}, u32[]{:S(2)}) collective-permute-start(bf16[128,1280]{1,0:T(8,128)(2,1)S(1)} %bitcast.50), channel_id=1, source_target_pairs={{0,4},{8,12},{16,20},{24,28},{32,36},{40,44},{48,52},{56,60},{64,6... | collective-permute-start | bytes 983048 | tf_op jit(solution)/shard_map/ppermute | solution.py:319
  7.3 51.9 %collective-permute-start.13 = (bf16[768,1280]{1,0:T(8,128)(2,1)}, bf16[768,1280]{1,0:T(8,128)(2,1)}, u32[]{:S(2)}, u32[]{:S(2)}) collective-permute-start(bf16[768,1280]{1,0:T(8,128)(2,1)} %bitcast.43), channel_id=1, source_target_pairs={{0,4},{8,12},{16,20},{24,28},{32,36},{40,44},{48,52},{56,60},{64,6... | collective-permute-start | bytes 5898248 | tf_op jit(solution)/shard_map/ppermute | solution.py:319
  8.1 2.7 %copy-start.1 = (s32[4,128]{1,0:T(4,128)S(1)}, s32[4,128]{1,0:T(4,128)}, u32[]{:S(2)}) copy-start(s32[4,128]{1,0:T(4,128)} %param.11) | copy-start | bytes 6148
  10.6 47.2 %collective-permute-start.14 = (bf16[512,1280]{1,0:T(8,128)(2,1)}, bf16[512,1280]{1,0:T(8,128)(2,1)S(1)}, u32[]{:S(2)}, u32[]{:S(2)}) collective-permute-start(bf16[512,1280]{1,0:T(8,128)(2,1)} %slice.12), channel_id=1, source_target_pairs={{0,8},{8,0},{16,24},{24,16},{32,40},{40,32},{48,56},{56,48},{64,72... | collective-permute-start | bytes 3932168 | tf_op jit(solution)/shard_map/ppermute | solution.py:319
  10.8 44.1 %collective-permute-start.16 = (bf16[256,1280]{1,0:T(8,128)(2,1)S(1)}, bf16[256,1280]{1,0:T(8,128)(2,1)S(1)}, u32[]{:S(2)}, u32[]{:S(2)}) collective-permute-start(bf16[256,1280]{1,0:T(8,128)(2,1)S(1)} %slice.13), channel_id=1, source_target_pairs={{0,8},{8,0},{16,24},{24,16},{32,40},{40,32},{48,56},{56,48},{64,72... | collective-permute-start | bytes 1966088 | tf_op jit(solution)/shard_map/ppermute | solution.py:319
  12.4 11.5 %collective-permute-start.4 = (bf16[256,1280]{1,0:T(8,128)(2,1)S(1)}, bf16[256,1280]{1,0:T(8,128)(2,1)S(1)}, u32[]{:S(2)}, u32[]{:S(2)}) collective-permute-start(bf16[256,1280]{1,0:T(8,128)(2,1)S(1)} %pad_maximum_fusion), channel_id=1, source_target_pairs={{0,32},{8,40},{16,48},{24,56},{32,64},{40,72},{48,80},{56,88},{64,... | collective-permute-start | bytes 1966088 | tf_op jit(solution)/shard_map/ppermute | solution.py:319
  23.8 10.6 %collective-permute-start.5 = (bf16[256,1280]{1,0:T(8,128)(2,1)S(1)}, bf16[256,1280]{1,0:T(8,128)(2,1)S(1)}, u32[]{:S(2)}, u32[]{:S(2)}) collective-permute-start(bf16[256,1280]{1,0:T(8,128)(2,1)S(1)} %collective-permute-done.4.one.refs_0_), channel_id=1, source_target_pairs={{0,32},{8,40},{16,48},{24,56},{32,64},{40,72},{48,80},{56,88},{64,... | collective-permute-start | bytes 1966088 | tf_op jit(solution)/shard_map/ppermute | solution.py:319
  28.3 29.7 %collective-permute-start.6 = (bf16[256,1280]{1,0:T(8,128)(2,1)S(1)}, bf16[256,1280]{1,0:T(8,128)(2,1)S(1)}, u32[]{:S(2)}, u32[]{:S(2)}) collective-permute-start(bf16[256,1280]{1,0:T(8,128)(2,1)S(1)} %collective-permute-done.4.one.refs_0_), channel_id=1, source_target_pairs={{0,24},{8,16},{16,8},{24,0},{32,56},{40,48},{48,40},{56,32},{64,88... | collective-permute-start | bytes 1966088 | tf_op jit(solution)/shard_map/ppermute | solution.py:319
  34.5 23.9 %collective-permute-start.7 = (bf16[256,1280]{1,0:T(8,128)(2,1)S(1)}, bf16[256,1280]{1,0:T(8,128)(2,1)S(1)}, u32[]{:S(2)}, u32[]{:S(2)}) collective-permute-start(bf16[256,1280]{1,0:T(8,128)(2,1)S(1)} %collective-permute-done.5.two.refs_1_), channel_id=1, source_target_pairs={{0,32},{8,40},{16,48},{24,56},{32,64},{40,72},{48,80},{56,88},{64,... | collective-permute-start | bytes 1966088 | tf_op jit(solution)/shard_map/ppermute | solution.py:319
  54.9 32.3 %collective-permute-start.12 = (bf16[256,1280]{1,0:T(8,128)(2,1)S(1)}, bf16[256,1280]{1,0:T(8,128)(2,1)S(1)}, u32[]{:S(2)}, u32[]{:S(2)}) collective-permute-start(bf16[256,1280]{1,0:T(8,128)(2,1)S(1)} %pad_maximum_fusion), channel_id=1, source_target_pairs={{4,28},{12,20},{20,12},{28,4},{36,60},{44,52},{52,44},{60,36},{68,... | collective-permute-start | bytes 1966088 | tf_op jit(solution)/shard_map/ppermute | solution.py:319
  57.8 29.4 %collective-permute-start.17 = (bf16[256,1280]{1,0:T(8,128)(2,1)S(1)}, bf16[256,1280]{1,0:T(8,128)(2,1)S(1)}, u32[]{:S(2)}, u32[]{:S(2)}) collective-permute-start(bf16[256,1280]{1,0:T(8,128)(2,1)S(1)} %collective-permute-done.16.refs_12_), channel_id=1, source_target_pairs={{0,4},{8,12},{16,20},{24,28},{32,36},{40,44},{48,52},{56,60},{64,6... | collective-permute-start | bytes 1966088 | tf_op jit(solution)/shard_map/ppermute | solution.py:319
  57.9 19.1 %collective-permute-start.15 = (bf16[512,1280]{1,0:T(8,128)(2,1)S(1)}, bf16[512,1280]{1,0:T(8,128)(2,1)S(1)}, u32[]{:S(2)}, u32[]{:S(2)}) collective-permute-start(bf16[512,1280]{1,0:T(8,128)(2,1)S(1)} %collective-permute-done.14.refs_8_.refs_10_), channel_id=1, source_target_pairs={{0,4},{8,12},{16,20},{24,28},{32,36},{40,44},{48,52},{56,60},{64,6... | collective-permute-start | bytes 3932168 | tf_op jit(solution)/shard_map/ppermute | solution.py:319
  58.4 15.4 %collective-permute-start.9 = (bf16[256,1280]{1,0:T(8,128)(2,1)S(1)}, bf16[256,1280]{1,0:T(8,128)(2,1)S(1)}, u32[]{:S(2)}, u32[]{:S(2)}) collective-permute-start(bf16[256,1280]{1,0:T(8,128)(2,1)S(1)} %collective-permute-done.5.two.refs_1_), channel_id=1, source_target_pairs={{0,24},{8,16},{16,8},{24,0},{32,56},{40,48},{48,40},{56,32},{64,88... | collective-permute-start | bytes 1966088 | tf_op jit(solution)/shard_map/ppermute | solution.py:319
  59.2 14.6 %collective-permute-start.8 = (bf16[256,1280]{1,0:T(8,128)(2,1)S(1)}, bf16[256,1280]{1,0:T(8,128)(2,1)S(1)}, u32[]{:S(2)}, u32[]{:S(2)}) collective-permute-start(bf16[256,1280]{1,0:T(8,128)(2,1)S(1)} %broadcast_select_fusion.3), channel_id=1, source_target_pairs={{0,32},{8,40},{16,48},{24,56},{32,64},{40,72},{48,80},{56,88},{64,... | collective-permute-start | bytes 1966088 | tf_op jit(solution)/shard_map/ppermute | solution.py:319
  74.1 13.2 %collective-permute-start.10 = (bf16[256,1280]{1,0:T(8,128)(2,1)S(1)}, bf16[256,1280]{1,0:T(8,128)(2,1)S(1)}, u32[]{:S(2)}, u32[]{:S(2)}) collective-permute-start(bf16[256,1280]{1,0:T(8,128)(2,1)S(1)} %get-tuple-element.40), channel_id=1, source_target_pairs={{0,32},{8,40},{16,48},{24,56},{32,64},{40,72},{48,80},{56,88},{64,... | collective-permute-start | bytes 1966088 | tf_op jit(solution)/shard_map/ppermute | solution.py:319
  76.4 10.8 %collective-permute-start.11 = (bf16[256,1280]{1,0:T(8,128)(2,1)S(1)}, bf16[256,1280]{1,0:T(8,128)(2,1)S(1)}, u32[]{:S(2)}, u32[]{:S(2)}) collective-permute-start(bf16[256,1280]{1,0:T(8,128)(2,1)S(1)} %collective-permute-done.8.refs_4_), channel_id=1, source_target_pairs={{0,24},{8,16},{16,8},{24,0},{32,56},{40,48},{48,40},{56,32},{64,88... | collective-permute-start | bytes 1966088 | tf_op jit(solution)/shard_map/ppermute | solution.py:319
  97.8 5.1 %collective-permute-start.18 = (bf16[8,144,256]{2,1,0:T(8,128)(2,1)S(1)}, bf16[8,144,256]{2,1,0:T(8,128)(2,1)S(1)}, u32[]{:S(2)}, u32[]{:S(2)}) collective-permute-start(bf16[8,144,256]{2,1,0:T(8,128)(2,1)S(1)} %get-tuple-element.31), channel_id=1, source_target_pairs={{0,4},{8,12},{16,20},{24,28},{32,36},{40,44},{48,52},{56,60},{64,6... | collective-permute-start | bytes 1769480 | tf_op jit(solution)/shard_map/ppermute | solution.py:319
  103.9 14.9 %all-to-all-start = ((bf16[8,224,128]{2,1,0:T(8,128)(2,1)}), bf16[8,224,128]{2,1,0:T(8,128)(2,1)S(1)}, u32[]{:S(2)}, u32[]{:S(2)}) async-start(bf16[8,224,128]{2,1,0:T(8,128)(2,1)} %shard_map.108), calls=%async_computation | async-start | bytes 917504 | tf_op jit(solution)/shard_map/all_to_all | solution.py:411

commit v5 on v4

--- a/solution.py
+++ b/solution.py
@@ -95,11 +95,12 @@
     reduce(*jobs[-1])
 
 
-def jobs_of(w, parts, l_ref, m_ref, s_ref):
+def jobs_of(w, parts, l_ref, m_ref, s_ref, packed=False):
     jobs = []
     for f_ref, first in parts:
         for t in range(f_ref.shape[0] // TILE):
-            jobs.append((w, f_ref, t, l_ref, 2 * len(jobs), m_ref, s_ref, first + t))
+            window = 2 * (len(jobs) if packed else first + t)
+            jobs.append((w, f_ref, t, l_ref, window, m_ref, s_ref, first + t))
     return jobs
 
 
@@ -142,6 +143,19 @@
         w_ref[k * (BLOCK // 2) : (k + 1) * (BLOCK // 2)] = block[...]
 
 
+def prepare_kernel(shard, rows, turned, near, early, late, sems):
+    copies = [
+        pltpu.make_async_copy(rows, near, sems.at[0]),
+        pltpu.make_async_copy(rows.at[0:EARLY], early, sems.at[1]),
+        pltpu.make_async_copy(rows.at[EARLY : rows.shape[0]], late, sems.at[2]),
+    ]
+    for copy in copies:
+        copy.start()
+    turned[...] = shard[...].T
+    for copy in copies:
+        copy.wait()
+
+
 def first_kernel(bounds, entries, one, two, fa, fb, m, s, p, w_ref, l_ref):
     m[...] = jnp.full_like(m, LOWEST)
     s[...] = jnp.zeros_like(s)
@@ -160,20 +174,30 @@
     take_rows(1, 2, 0, bounds, entries, l_ref, p)
 
 
-def third_kernel(bounds, entries, *refs):
-    blocks, (fa, fb, ga, gb, m_in, s_in, p_in), refs = refs[:6], refs[6:13], refs[13:]
-    m, s, p, mb, sb, pb, lb_ref, w_ref, l_ref = refs
-    m[...] = m_in[...]
-    s[...] = s_in[...]
-    p[...] = p_in[...]
+def beside_kernel(bounds, entries, *refs):
+    blocks, (ga, gb), (mb, sb, pb, lb_ref, w_ref, _) = refs[:4], refs[4:6], refs[6:]
     mb[...] = jnp.full_like(mb, LOWEST)
     sb[...] = jnp.zeros_like(sb)
     pb[...] = jnp.zeros_like(pb)
     fill_columns(w_ref, blocks)
-    near = jobs_of(w_ref.at[2 * BLOCK : 3 * BLOCK], ((fa, 0), (fb, 3)), l_ref, m, s)
-    score_jobs(near + jobs_of(w_ref, ((ga, 0), (gb, 3)), lb_ref, mb, sb))
+    score_jobs(jobs_of(w_ref, ((ga, 0), (gb, 3)), lb_ref, mb, sb, True))
+    take_rows(0, 2, 1, bounds, entries, lb_ref, pb, True)
+
+
+def third_kernel(bounds, entries, *refs):
+    blocks, (fa, fb, ga, gb, ha, hb), state, state_out, refs = refs[:6], refs[6:12], refs[12:18], refs[18:24], refs[24:]
+    lb_ref, lc_ref, w_ref, l_ref = refs
+    for ref, value in zip(state_out, state):
+        ref[...] = value[...]
+    m, s, p, mb, sb, pb = state_out
+    fill_columns(w_ref, blocks)
+    newest = w_ref.at[2 * BLOCK : 3 * BLOCK]
+    jobs = jobs_of(newest, ((fa, 0), (fb, 3)), l_ref, m, s)
+    jobs += jobs_of(newest, ((ga, 0), (gb, 3)), lb_ref, mb, sb, True)
+    score_jobs(jobs + jobs_of(w_ref, ((ha, 2), (hb, 5)), lc_ref, mb, sb, True))
     take_rows(2, 3, 0, bounds, entries, l_ref, p)
-    take_rows(0, 3, 1, bounds, entries, lb_ref, pb, True)
+    take_rows(2, 3, 1, bounds, entries, lb_ref, pb, True)
+    take_rows(0, 3, 1, bounds, entries, lc_ref, pb, False)
 
 
 def split_parts(value):
@@ -191,18 +215,15 @@
 
 
 def last_kernel(bounds, entries, *refs):
-    blocks, (fa, fb, ga, gb, ha, hb), state, (kept, given) = refs[:8], refs[8:14], refs[14:20], refs[20:22]
-    m, s, p, mb, sb, pb, lse_ref, lb_ref, lc_ref, w_ref, l_ref = refs[22:]
+    blocks, (fa, fb, ga, gb, ha, hb), state, (kept, given) = refs[:2], refs[2:8], refs[8:14], refs[14:16]
+    m, s, p, mb, sb, pb, lse_ref, lb_ref, w_ref, l_ref = refs[16:]
     for ref, value in zip((m, s, p, mb, sb, pb), state):
         ref[...] = value[...]
     fill_columns(w_ref, blocks)
-    final = w_ref.at[3 * BLOCK : 4 * BLOCK]
-    jobs = jobs_of(w_ref, ((ha, 2), (hb, 5)), lc_ref, mb, sb)
-    jobs += jobs_of(final, ((ga, 0), (gb, 3)), lb_ref, mb, sb)
-    score_jobs(jobs + jobs_of(final, ((fa, 0), (fb, 3)), l_ref, m, s))
-    take_rows(0, 4, 1, bounds, entries, lc_ref, pb, False)
-    take_rows(3, 4, 1, bounds, entries, lb_ref, pb, True)
+    jobs = jobs_of(w_ref, ((fa, 0), (fb, 3)), l_ref, m, s)
+    score_jobs(jobs + jobs_of(w_ref, ((ga, 0), (ha, 2), (gb, 3), (hb, 5)), lb_ref, mb, sb))
     take_rows(3, 4, 0, bounds, entries, l_ref, p)
+    take_rows(3, 4, 1, bounds, entries, lb_ref, pb)
     for group, (mm, ss, pp) in enumerate(((m, s, p), (mb, sb, pb))):
         for t in range(WINDOWS // 2):
             top = jnp.max(mm[t], 0, keepdims=True)
@@ -280,8 +301,7 @@
     score = advance(score, 1, DEPTH - 1)
     lax.fori_loop(1, frames // DEPTH, lambda b, now: advance(now, pl.multiple_of(b * DEPTH, DEPTH), DEPTH), score)
     final = scores[pl.ds(lengths[0] - 1, 1), :]
-    hit = jnp.sum(jnp.where(lanes == lengths[1] - 1, final, 0.0), 1, keepdims=True)
-    path[...] = jnp.broadcast_to(hit, path.shape)
+    path[0] = jnp.sum(jnp.where(lanes == lengths[1] - 1, final, 0.0))
 
 
 def label_entries(labels, vocab_index, z, y, core):
@@ -321,19 +341,29 @@
     def both(array, step):
         return send(array, step, step)
 
-    own = head_weight.T
+    columns = head_weight.shape[1]
+    own, fa, early, late = pl.pallas_call(
+        prepare_kernel,
+        out_shape=[
+            jax.ShapeDtypeStruct(shape, jnp.bfloat16)
+            for shape in ((columns, width), (rows, width), (EARLY, width), (rows - EARLY, width))
+        ],
+        in_specs=[VMEM, ANY],
+        out_specs=[VMEM] * 4,
+        scratch_shapes=[pltpu.SemaphoreType.DMA((3,))],
+        compiler_params=pltpu.CompilerParams(vmem_limit_bytes=8 * 2**20),
+    )(head_weight, features.reshape(rows, width))
     other = both(own, other_core)
     is0 = core == 0
     o0 = jnp.concatenate([own, other])
     op1 = send(o0, up, down)
     op2 = send(o0, None, mirror)
-    fa = features.reshape(rows, width)
     fb = both(fa, other_core)
     l1 = both(labels, other_core)
     l2 = both(labels, beside)
     l3 = both(labels, across)
-    ga = both(fa[:EARLY], beside)
-    ha = both(fa[EARLY:], beside)
+    ga = both(early, beside)
+    ha = both(late, beside)
     op3 = send(op1, up, down)
     op4 = both(op1, mirror)
     op5 = send(op3, up, down)
@@ -370,28 +400,38 @@
             compiler_params=pltpu.CompilerParams(vmem_limit_bytes=limit * 2**20),
         )(bounds, entries, *operands)
 
+    early_windows = 2 * EARLY // 128
     ma = call(first_kernel, state, (op1, op3, fa, fb), 1, 4, 8)
     ma = call(second_kernel, state, (op4, op5, fa, fb, *ma), 1, 4, 8)
-    *ma, mb, sb, pb = call(
+    mb = call(
+        beside_kernel, state, (op1, op3, op4, op5, ga, gb), 2, 4, 14, [pltpu.VMEM((early_windows, 2 * BLOCK, 128), f32)]
+    )
+    states = (*ma, *mb)
+    states = call(
         third_kernel,
         state + state,
-        (op1, op3, op4, op5, op6, s1, fa, fb, ga, gb, *ma),
+        (op1, op3, op4, op5, op6, s1, fa, fb, ga, gb, ha, hb, *states),
         3,
-        9,
-        17,
-        [pltpu.VMEM((2 * EARLY // 128, 3 * BLOCK, 128), f32)],
+        8,
+        16,
+        [
+            pltpu.VMEM((early_windows, BLOCK, 128), f32),
+            pltpu.VMEM((WINDOWS - early_windows, 3 * BLOCK, 128), f32),
+        ],
     )
     packed = jax.ShapeDtypeStruct((8, 144, TILE), jnp.bfloat16)
     kept, given = call(
         last_kernel,
         (packed, packed),
-        (op1, op3, op4, op5, op6, s1, op8, s2, fa, fb, ga, gb, ha, hb, *ma, mb, sb, pb),
-        PAIRS,
-        9,
-        20,
-        [*(pltpu.VMEM(leaf.shape, leaf.dtype) for leaf in state + state), pltpu.VMEM((WINDOWS, 8, 128), f32),
-         pltpu.VMEM((2 * EARLY // 128, BLOCK, 128), f32),
-         pltpu.VMEM((WINDOWS - 2 * EARLY // 128, 4 * BLOCK, 128), f32)],
+        (op8, s2, fa, fb, ga, gb, ha, hb, *states),
+        1,
+        6,
+        16,
+        [
+            *(pltpu.VMEM(leaf.shape, leaf.dtype) for leaf in state + state),
+            pltpu.VMEM((WINDOWS, 8, 128), f32),
+            logits_scratch,
+        ],
     )
     taken = both(given, other_core)
     sent = pl.pallas_call(
@@ -411,13 +451,13 @@
     got = lax.all_to_all(sent, ("rec", "vocab"), 0, 0, tiled=True, axis_index_groups=owners)
     log_prob, path = pl.pallas_call(
         align_kernel,
-        out_shape=[jax.ShapeDtypeStruct((frames, 128), f32), jax.ShapeDtypeStruct((8, 128), f32)],
+        out_shape=[jax.ShapeDtypeStruct((frames, 128), f32), jax.ShapeDtypeStruct((1,), f32)],
         in_specs=[SMEM, VMEM],
-        out_specs=[VMEM] * 2,
+        out_specs=[VMEM, SMEM],
         scratch_shapes=[pltpu.VMEM((DEPTH, frames, 128), f32), pltpu.VMEM((frames, 128), f32)],
         compiler_params=pltpu.CompilerParams(vmem_limit_bytes=8 * 2**20),
     )(jnp.concatenate([audio_len, transcript_len]), got)
-    return log_prob[None], path[0, :1]
+    return log_prob[None], path
 
 
 def solution(mesh):

time: 123 us -> 123 us (level)
  waiting for transfers between devices: 36.1 us -> 34.7 us
    unnamed x5 -> x15, local copies, waits for them, and re-layouts: 1.15 us -> 4.34 us
    slice x3 -> x0, local copies, waits for them, and re-layouts: 3.03 us -> none  [the longest x1 2.47 us: body(): ga = both(fa[:EARLY], beside)]
    pallas_call x4 -> x5, Pallas kernels: 29.4 us -> 27.5 us  [call(): pl.pallas_call(kernel, out_shape=out_shape, in_specs=[SMEM, SMEM, *[VMEM]...]
    ppermute x19, starting transfers between devices: 37 us -> 38.6 us  [send(): lax.ppermute(array, 'rec', moves(step0, step1 if step1 is not None else N...]
    pallas_call x0 -> x1, Pallas kernels: none -> 1.59 us  [body(): pl.pallas_call(prepare_kernel, out_shape=[jax.ShapeDtypeStruct(shape, jnp...]
    ppermute x19, waiting for transfers between devices: 27.9 us -> 26.6 us  [send(): lax.ppermute(array, 'rec', moves(step0, step1 if step1 is not None else N...]
  transfers between devices with their start and end apart: 20 -> 20, of which waited for: 5 -> 5; matrix products, arithmetic and copies ran while one was open for 6% -> 4% of each run, Pallas kernels for 15% -> 18%
where the time goes in v5:
time: 123 us
  starting transfers between devices  43.3 us (35%)
  waiting for transfers between devices  34.7 us (28%)
  Pallas kernels  33.8 us (27%)
  local copies, waits for them, and re-layouts  5.09 us (4%)
  other arithmetic  3.32 us (3%)
  between operations  2.44 us (2%)
    ppermute x19, starting transfers between devices, send(): lax.ppermute(array, 'rec', moves(step0, step1 if step1 is not None else N...  38.6 us
    pallas_call x5, Pallas kernels, call(): pl.pallas_call(kernel, out_shape=out_shape, in_specs=[SMEM, SMEM, *[VMEM]...  27.5 us
    ppermute x19, waiting for transfers between devices, send(): lax.ppermute(array, 'rec', moves(step0, step1 if step1 is not None else N...  26.6 us
    all_to_all x1, waiting for transfers between devices, body(): lax.all_to_all(sent, ('rec', 'vocab'), 0, 0, tiled=True, axis_index_group...  8.17 us
    all_to_all x1, starting transfers between devices, body(): lax.all_to_all(sent, ('rec', 'vocab'), 0, 0, tiled=True, axis_index_group...  4.76 us
    unnamed x15, local copies, waits for them, and re-layouts  4.34 us
    pallas_call x1, Pallas kernels, body(): pl.pallas_call(align_kernel, out_shape=[jax.ShapeDtypeStruct((frames, 128...  3.69 us
  transfers between devices with their start and end apart: 20, of which 5 were waited for; matrix products, arithmetic and copies ran while one was open for 4% of the time, Pallas kernels for 18%

profile of v5, /device:TPU:1, one launch (start us, length us, event | category | flops | bytes accessed | tf_op | source)
XLA Modules:
  0.0 122.7 jit_solution(15785861769683676884)
XLA Ops:
  0.6 0.0 copy-start.5
  0.7 3.3 %collective-permute-start = (s32[4,128]{1,0:T(4,128)}, s32[4,128]{1,0:T(4,128)S(1)}, u32[]{:S(2)}, u32[]{:S(2)}) collective-permute-start(s32[4,128]{1,0:T(4,128)} %param.11), channel_id=1, source_target_pairs={{0,4},{8,12},{16,20},{24,28},{32,36},{40,44},{48,52},{56,60},{64,6... | collective-permute-start | bytes 6152 | tf_op jit(solution)/shard_map/ppermute | solution.py:339
  3.9 1.4 %collective-permute-start.1 = (s32[4,128]{1,0:T(4,128)}, s32[4,128]{1,0:T(4,128)S(1)}, u32[]{:S(2)}, u32[]{:S(2)}) collective-permute-start(s32[4,128]{1,0:T(4,128)} %param.11), channel_id=1, source_target_pairs={{0,8},{8,0},{16,24},{24,16},{32,40},{40,32},{48,56},{56,48},{64,72... | collective-permute-start | bytes 6152 | tf_op jit(solution)/shard_map/ppermute | solution.py:339
  5.4 1.5 %copy-done = bf16[4,192,1280]{2,1,0:T(8,128)(2,1)S(1)} copy-done((bf16[4,192,1280]{2,1,0:T(8,128)(2,1)S(1)}, bf16[4,192,1280]{2,1,0:T(8,128)(2,1)}, u32[]{:S(2)}) %copy-start) | copy-done | bytes 1966104
  6.9 1.0 copy-done.1
  7.9 1.6 %shard_map.104 = (bf16[128,1280]{1,0:T(8,128)(2,1)S(1)}, bf16[768,1280]{1,0:T(8,128)(2,1)S(1)}, bf16[512,1280]{1,0:T(8,128)(2,1)S(1)}, bf16[256,1280]{1,0:T(8,128)(2,1)}) custom-call(bf16[1280,128]{1,0:T(8,128)(2,1)S(1)} %copy-done.1, bf16[768,1280]{1,0:T(8,128)(2,1)S(1)} %bitcast.41), custom_call_target="tpu_custom_call" | custom-call | tf_op jit(solution)/shard_map/pallas_call | solution.py:345
  9.5 1.1 copy-done.2
  10.6 0.7 collective-permute-start.3
  11.3 0.7 constant_dynamic-update-slice_fusion.1
  12.1 1.5 %collective-permute-start.14 = (bf16[512,1280]{1,0:T(8,128)(2,1)}, bf16[512,1280]{1,0:T(8,128)(2,1)S(1)}, u32[]{:S(2)}, u32[]{:S(2)}) collective-permute-start(bf16[512,1280]{1,0:T(8,128)(2,1)} %copy-done.2), channel_id=1, source_target_pairs={{0,8},{8,0},{16,24},{24,16},{32,40},{40,32},{48,56},{56,48},{64,72... | collective-permute-start | bytes 3932168 | tf_op jit(solution)/shard_map/ppermute | solution.py:339
  13.7 0.6 collective-permute-start.13
  14.4 0.1 select_reduce_fusion.3
  14.5 0.8 constant_dynamic-update-slice_fusion
  15.2 3.9 %collective-permute-start.4 = (bf16[256,1280]{1,0:T(8,128)(2,1)}, bf16[256,1280]{1,0:T(8,128)(2,1)S(1)}, u32[]{:S(2)}, u32[]{:S(2)}) collective-permute-start(bf16[256,1280]{1,0:T(8,128)(2,1)} %constant_dynamic-update-slice_fusion), channel_id=1, source_target_pairs={{0,32},{8,40},{16,48},{24,56},{32,64},{40,72},{48,80},{56,88},{64,... | collective-permute-start | bytes 1966088 | tf_op jit(solution)/shard_map/ppermute | solution.py:339
  19.2 0.6 convert_reduce_fusion
  19.7 0.7 select_reduce_fusion
  20.4 6.5 %collective-permute-done.4.one.refs_0_ = bf16[256,1280]{1,0:T(8,128)(2,1)S(1)} collective-permute-done((bf16[256,1280]{1,0:T(8,128)(2,1)}, bf16[256,1280]{1,0:T(8,128)(2,1)S(1)}, u32[]{:S(2)}, u32[]{:S(2)}) %collective-permute-start.4) | collective-permute-done | bytes 655392 | tf_op jit(solution)/shard_map/ppermute | solution.py:339
  27.0 3.0 %collective-permute-start.5 = (bf16[256,1280]{1,0:T(8,128)(2,1)S(1)}, bf16[256,1280]{1,0:T(8,128)(2,1)S(1)}, u32[]{:S(2)}, u32[]{:S(2)}) collective-permute-start(bf16[256,1280]{1,0:T(8,128)(2,1)S(1)} %collective-permute-done.4.one.refs_0_), channel_id=1, source_target_pairs={{0,32},{8,40},{16,48},{24,56},{32,64},{40,72},{48,80},{56,88},{64,... | collective-permute-start | bytes 1966088 | tf_op jit(solution)/shard_map/ppermute | solution.py:339
  30.0 0.6 convert_reduce_fusion.1
  30.6 0.1 convert_reduce_fusion.2
  30.7 0.7 select_reduce_fusion.1
  31.3 2.8 %collective-permute-start.8 = (bf16[256,1280]{1,0:T(8,128)(2,1)S(1)}, bf16[256,1280]{1,0:T(8,128)(2,1)S(1)}, u32[]{:S(2)}, u32[]{:S(2)}) collective-permute-start(bf16[256,1280]{1,0:T(8,128)(2,1)S(1)} %collective-permute-done.4.one.refs_0_), channel_id=1, source_target_pairs={{0,24},{8,16},{16,8},{24,0},{32,56},{40,48},{48,40},{56,32},{64,88... | collective-permute-start | bytes 1966088 | tf_op jit(solution)/shard_map/ppermute | solution.py:339
  34.2 3.3 %collective-permute-done.5.two.refs_1_ = bf16[256,1280]{1,0:T(8,128)(2,1)S(1)} collective-permute-done((bf16[256,1280]{1,0:T(8,128)(2,1)S(1)}, bf16[256,1280]{1,0:T(8,128)(2,1)S(1)}, u32[]{:S(2)}, u32[]{:S(2)}) %collective-permute-start.5) | collective-permute-done | bytes 655392 | tf_op jit(solution)/shard_map/ppermute | solution.py:339
  37.5 3.4 %collective-permute-start.7 = (bf16[256,1280]{1,0:T(8,128)(2,1)S(1)}, bf16[256,1280]{1,0:T(8,128)(2,1)S(1)}, u32[]{:S(2)}, u32[]{:S(2)}) collective-permute-start(bf16[256,1280]{1,0:T(8,128)(2,1)S(1)} %collective-permute-done.5.two.refs_1_), channel_id=1, source_target_pairs={{0,32},{8,40},{16,48},{24,56},{32,64},{40,72},{48,80},{56,88},{64,... | collective-permute-start | bytes 1966088 | tf_op jit(solution)/shard_map/ppermute | solution.py:339
  40.9 0.1 convert_reduce_fusion.3
  41.0 14.8 %collective-permute-done.14.refs_4_.refs_8_ = bf16[512,1280]{1,0:T(8,128)(2,1)S(1)} collective-permute-done((bf16[512,1280]{1,0:T(8,128)(2,1)}, bf16[512,1280]{1,0:T(8,128)(2,1)S(1)}, u32[]{:S(2)}, u32[]{:S(2)}) %collective-permute-start.14) | collective-permute-done | bytes 1310752 | tf_op jit(solution)/shard_map/ppermute | solution.py:339
  55.9 0.9 collective-permute-start.15
  56.7 2.9 %collective-permute-start.12 = (bf16[256,1280]{1,0:T(8,128)(2,1)}, bf16[256,1280]{1,0:T(8,128)(2,1)S(1)}, u32[]{:S(2)}, u32[]{:S(2)}) collective-permute-start(bf16[256,1280]{1,0:T(8,128)(2,1)} %constant_dynamic-update-slice_fusion), channel_id=1, source_target_pairs={{4,28},{12,20},{20,12},{28,4},{36,60},{44,52},{52,44},{60,36},{68,... | collective-permute-start | bytes 1966088 | tf_op jit(solution)/shard_map/ppermute | solution.py:339
  59.7 0.1 collective-permute-start.17
  59.8 3.7 %shard_map.105 = (f32[6,8,256]{2,1,0:T(8,128)S(1)}, f32[6,8,256]{2,1,0:T(8,128)S(1)}, f32[2,1032,128]{2,1,0:T(8,128)S(1)}) custom-call(s32[2,8]{1,0:T(2,128)S(1)} %pad_add_fusion.1.bounds, s32[2,1024]{1,0:T(2,128)S(1)} %pad_add_fusion.entries, bf16[256,1280]{1,0:T(8,128)(2,1)S(1)} %collective-permute-done.4.one.refs_0_, ...), custom_call_target="tpu_custom_call" | custom-call | flops 4000000000 | tf_op jit(solution)/shard_map/pallas_call | solution.py:393
  63.5 0.7 collective-permute-start.6
  64.2 0.1 broadcast_select_fusion.3
  64.3 5.7 %collective-permute-start.9 = (bf16[256,1280]{1,0:T(8,128)(2,1)S(1)}, bf16[256,1280]{1,0:T(8,128)(2,1)S(1)}, u32[]{:S(2)}, u32[]{:S(2)}) collective-permute-start(bf16[256,1280]{1,0:T(8,128)(2,1)S(1)} %broadcast_select_fusion.3), channel_id=1, source_target_pairs={{0,32},{8,40},{16,48},{24,56},{32,64},{40,72},{48,80},{56,88},{64,... | collective-permute-start | bytes 1966088 | tf_op jit(solution)/shard_map/ppermute | solution.py:339
  69.9 3.5 %shard_map.106 = (f32[6,8,256]{2,1,0:T(8,128)S(1)}, f32[6,8,256]{2,1,0:T(8,128)S(1)}, f32[2,1032,128]{2,1,0:T(8,128)S(1)}) custom-call(s32[2,8]{1,0:T(2,128)S(1)} %pad_add_fusion.1.bounds, s32[2,1024]{1,0:T(2,128)S(1)} %pad_add_fusion.entries, bf16[256,1280]{1,0:T(8,128)(2,1)S(1)} %collective-permute-done.8.one.refs_2_, ...), custom_call_target="tpu_custom_call" | custom-call | flops 4000000000 | tf_op jit(solution)/shard_map/pallas_call | solution.py:393
  73.5 4.6 %shard_map.107 = (f32[6,8,256]{2,1,0:T(8,128)S(1)}, f32[6,8,256]{2,1,0:T(8,128)S(1)}, f32[2,1032,128]{2,1,0:T(8,128)S(1)}) custom-call(s32[2,8]{1,0:T(2,128)S(1)} %pad_add_fusion.1.bounds, s32[2,1024]{1,0:T(2,128)S(1)} %pad_add_fusion.entries, bf16[256,1280]{1,0:T(8,128)(2,1)S(1)} %collective-permute-done.4.one.refs_0_, ...), custom_call_target="tpu_custom_call" | custom-call | flops 4000000000 | tf_op jit(solution)/shard_map/pallas_call | solution.py:393
  78.1 0.1 broadcast_select_fusion
  78.2 2.8 %collective-permute-start.10 = (bf16[256,1280]{1,0:T(8,128)(2,1)S(1)}, bf16[256,1280]{1,0:T(8,128)(2,1)S(1)}, u32[]{:S(2)}, u32[]{:S(2)}) collective-permute-start(bf16[256,1280]{1,0:T(8,128)(2,1)S(1)} %get-tuple-element.55), channel_id=1, source_target_pairs={{0,32},{8,40},{16,48},{24,56},{32,64},{40,72},{48,80},{56,88},{64,... | collective-permute-start | bytes 1966088 | tf_op jit(solution)/shard_map/ppermute | solution.py:339
  81.1 0.7 collective-permute-start.11
  81.8 8.6 %shard_map.108 = (f32[6,8,256]{2,1,0:T(8,128)S(1)}, f32[6,8,256]{2,1,0:T(8,128)S(1)}, f32[2,1032,128]{2,1,0:T(8,128)S(1)}, f32[6,8,256]{2,1,0:T(8,128)S(1)}, f32...) custom-call(s32[2,8]{1,0:T(2,128)S(1)} %pad_add_fusion.1.bounds, s32[2,1024]{1,0:T(2,128)S(1)} %pad_add_fusion.entries, ...), custom_call_target="tpu_custom_call" | custom-call | flops 8000000000 | tf_op jit(solution)/shard_map/pallas_call | solution.py:393
  90.4 0.1 broadcast_select_fusion.1.refs_1_
  90.5 7.1 %shard_map.109 = (bf16[8,144,256]{2,1,0:T(8,128)(2,1)S(1)}, bf16[8,144,256]{2,1,0:T(8,128)(2,1)}) custom-call(s32[2,8]{1,0:T(2,128)S(1)} %pad_add_fusion.1.bounds, s32[2,1024]{1,0:T(2,128)S(1)} %pad_add_fusion.entries, bf16[256,1280]{1,0:T(8,128)(2,1)S(1)} %collective-permute-done.10.refs_0_, bf16[256,1280]{1,0:T(8,128)(2,1)S(1)} %broadcast_select_fusion.1.refs_1_, ...), custom_call_target="tpu_custom_call" | custom-call | flops 6000000000 | tf_op jit(solution)/shard_map/pallas_call | solution.py:393
  97.6 4.1 %collective-permute-start.18 = (bf16[8,144,256]{2,1,0:T(8,128)(2,1)}, bf16[8,144,256]{2,1,0:T(8,128)(2,1)S(1)}, u32[]{:S(2)}, u32[]{:S(2)}) collective-permute-start(bf16[8,144,256]{2,1,0:T(8,128)(2,1)} %get-tuple-element.45), channel_id=1, source_target_pairs={{0,4},{8,12},{16,20},{24,28},{32,36},{40,44},{48,52},{56,60},{64,6... | collective-permute-start | bytes 1769480 | tf_op jit(solution)/shard_map/ppermute | solution.py:339
  101.7 1.8 %collective-permute-done.18.theirs = bf16[8,144,256]{2,1,0:T(8,128)(2,1)S(1)} collective-permute-done((bf16[8,144,256]{2,1,0:T(8,128)(2,1)}, bf16[8,144,256]{2,1,0:T(8,128)(2,1)S(1)}, u32[]{:S(2)}, u32[]{:S(2)}) %collective-permute-start.18) | collective-permute-done | bytes 589856 | tf_op jit(solution)/shard_map/ppermute | solution.py:339
  103.5 1.0 shard_map.110
  104.5 4.8 %all-to-all-start = ((bf16[8,224,128]{2,1,0:T(8,128)(2,1)}), bf16[8,224,128]{2,1,0:T(8,128)(2,1)S(1)}, u32[]{:S(2)}, u32[]{:S(2)}) async-start(bf16[8,224,128]{2,1,0:T(8,128)(2,1)} %shard_map.110), calls=%async_computation | async-start | bytes 917504 | tf_op jit(solution)/shard_map/all_to_all | solution.py:451
  110.6 0.1 pad_add_fusion.2.lengths
  110.6 8.2 %all-to-all-done.parts = bf16[8,224,128]{2,1,0:T(8,128)(2,1)S(1)} async-done(((bf16[8,224,128]{2,1,0:T(8,128)(2,1)}), bf16[8,224,128]{2,1,0:T(8,128)(2,1)S(1)}, u32[]{:S(2)}, u32[]{:S(2)}) %all-to-all-start) | async-done | bytes 458784 | tf_op jit(solution)/shard_map/all_to_all | solution.py:451
  118.8 3.7 %shard_map.111 = (f32[192,128]{1,0:T(8,128)}, f32[1]{0:T(128)}) custom-call(s32[2]{0:T(128)S(1)} %pad_add_fusion.2.lengths, bf16[8,224,128]{2,1,0:T(8,128)(2,1)S(1)} %all-to-all-done.parts), custom_call_target="tpu_custom_call" | custom-call | tf_op jit(solution)/shard_map/pallas_call | solution.py:452
  (35 shorter events, 0.3 us)
Async XLA Ops:
  0.6 11.4 %copy-start.5 = (s32[16]{0:T(128)S(1)}, s32[16]{0:T(128)}, u32[]{:S(2)}) copy-start(s32[16]{0:T(128)} %constant.226.clone) | copy-start | bytes 196
  0.6 11.4 %copy-start.6 = (s32[16]{0:T(128)S(1)}, s32[16]{0:T(128)}, u32[]{:S(2)}) copy-start(s32[16]{0:T(128)} %constant.225.clone) | copy-start | bytes 196
  0.7 11.4 %collective-permute-start = (s32[4,128]{1,0:T(4,128)}, s32[4,128]{1,0:T(4,128)S(1)}, u32[]{:S(2)}, u32[]{:S(2)}) collective-permute-start(s32[4,128]{1,0:T(4,128)} %param.11), channel_id=1, source_target_pairs={{0,4},{8,12},{16,20},{24,28},{32,36},{40,44},{48,52},{56,60},{64,6... | collective-permute-start | bytes 6152 | tf_op jit(solution)/shard_map/ppermute | solution.py:339
  3.9 9.7 %collective-permute-start.2 = (s32[4,128]{1,0:T(4,128)}, s32[4,128]{1,0:T(4,128)S(1)}, u32[]{:S(2)}, u32[]{:S(2)}) collective-permute-start(s32[4,128]{1,0:T(4,128)} %param.11), channel_id=1, source_target_pairs={{0,12},{8,4},{16,28},{24,20},{32,44},{40,36},{48,60},{56,52},{64,7... | collective-permute-start | bytes 6152 | tf_op jit(solution)/shard_map/ppermute | solution.py:339
  3.9 10.4 %collective-permute-start.1 = (s32[4,128]{1,0:T(4,128)}, s32[4,128]{1,0:T(4,128)S(1)}, u32[]{:S(2)}, u32[]{:S(2)}) collective-permute-start(s32[4,128]{1,0:T(4,128)} %param.11), channel_id=1, source_target_pairs={{0,8},{8,0},{16,24},{24,16},{32,40},{40,32},{48,56},{56,48},{64,72... | collective-permute-start | bytes 6152 | tf_op jit(solution)/shard_map/ppermute | solution.py:339
  5.4 1.5 %copy-start = (bf16[4,192,1280]{2,1,0:T(8,128)(2,1)S(1)}, bf16[4,192,1280]{2,1,0:T(8,128)(2,1)}, u32[]{:S(2)}) copy-start(bf16[4,192,1280]{2,1,0:T(8,128)(2,1)} %param.9) | copy-start | bytes 5898244
  6.9 1.0 copy-start.1
  7.9 5.7 %copy-start.4 = (s32[4,128]{1,0:T(4,128)S(1)}, s32[4,128]{1,0:T(4,128)}, u32[]{:S(2)}) copy-start(s32[4,128]{1,0:T(4,128)} %param.11) | copy-start | bytes 6148
  9.5 1.1 copy-start.2
  10.6 3.9 %collective-permute-start.3 = (bf16[128,1280]{1,0:T(8,128)(2,1)S(1)}, bf16[128,1280]{1,0:T(8,128)(2,1)S(1)}, u32[]{:S(2)}, u32[]{:S(2)}) collective-permute-start(bf16[128,1280]{1,0:T(8,128)(2,1)S(1)} %get-tuple-element.25), channel_id=1, source_target_pairs={{0,4},{8,12},{16,20},{24,28},{32,36},{40,44},{48,52},{56,60},{64,6... | collective-permute-start | bytes 983048 | tf_op jit(solution)/shard_map/ppermute | solution.py:339
  11.3 45.5 %collective-permute-start.16 = (bf16[256,1280]{1,0:T(8,128)(2,1)}, bf16[256,1280]{1,0:T(8,128)(2,1)S(1)}, u32[]{:S(2)}, u32[]{:S(2)}) collective-permute-start(bf16[256,1280]{1,0:T(8,128)(2,1)} %get-tuple-element.28), channel_id=1, source_target_pairs={{0,8},{8,0},{16,24},{24,16},{32,40},{40,32},{48,56},{56,48},{64,72... | collective-permute-start | bytes 1966088 | tf_op jit(solution)/shard_map/ppermute | solution.py:339
  12.1 43.8 %collective-permute-start.14 = (bf16[512,1280]{1,0:T(8,128)(2,1)}, bf16[512,1280]{1,0:T(8,128)(2,1)S(1)}, u32[]{:S(2)}, u32[]{:S(2)}) collective-permute-start(bf16[512,1280]{1,0:T(8,128)(2,1)} %copy-done.2), channel_id=1, source_target_pairs={{0,8},{8,0},{16,24},{24,16},{32,40},{40,32},{48,56},{56,48},{64,72... | collective-permute-start | bytes 3932168 | tf_op jit(solution)/shard_map/ppermute | solution.py:339
  13.7 46.0 %collective-permute-start.13 = (bf16[768,1280]{1,0:T(8,128)(2,1)S(1)}, bf16[768,1280]{1,0:T(8,128)(2,1)S(1)}, u32[]{:S(2)}, u32[]{:S(2)}) collective-permute-start(bf16[768,1280]{1,0:T(8,128)(2,1)S(1)} %get-tuple-element.26.fa.refs_6_.refs_2_), channel_id=1, source_target_pairs={{0,4},{8,12},{16,20},{24,28},{32,36},{40,44},{48,52},{56,60},{64,6... | collective-permute-start | bytes 5898248 | tf_op jit(solution)/shard_map/ppermute | solution.py:339
  15.2 11.7 %collective-permute-start.4 = (bf16[256,1280]{1,0:T(8,128)(2,1)}, bf16[256,1280]{1,0:T(8,128)(2,1)S(1)}, u32[]{:S(2)}, u32[]{:S(2)}) collective-permute-start(bf16[256,1280]{1,0:T(8,128)(2,1)} %constant_dynamic-update-slice_fusion), channel_id=1, source_target_pairs={{0,32},{8,40},{16,48},{24,56},{32,64},{40,72},{48,80},{56,88},{64,... | collective-permute-start | bytes 1966088 | tf_op jit(solution)/shard_map/ppermute | solution.py:339
  27.0 10.5 %collective-permute-start.5 = (bf16[256,1280]{1,0:T(8,128)(2,1)S(1)}, bf16[256,1280]{1,0:T(8,128)(2,1)S(1)}, u32[]{:S(2)}, u32[]{:S(2)}) collective-permute-start(bf16[256,1280]{1,0:T(8,128)(2,1)S(1)} %collective-permute-done.4.one.refs_0_), channel_id=1, source_target_pairs={{0,32},{8,40},{16,48},{24,56},{32,64},{40,72},{48,80},{56,88},{64,... | collective-permute-start | bytes 1966088 | tf_op jit(solution)/shard_map/ppermute | solution.py:339
  31.3 32.1 %collective-permute-start.8 = (bf16[256,1280]{1,0:T(8,128)(2,1)S(1)}, bf16[256,1280]{1,0:T(8,128)(2,1)S(1)}, u32[]{:S(2)}, u32[]{:S(2)}) collective-permute-start(bf16[256,1280]{1,0:T(8,128)(2,1)S(1)} %collective-permute-done.4.one.refs_0_), channel_id=1, source_target_pairs={{0,24},{8,16},{16,8},{24,0},{32,56},{40,48},{48,40},{56,32},{64,88... | collective-permute-start | bytes 1966088 | tf_op jit(solution)/shard_map/ppermute | solution.py:339
  37.5 26.7 %collective-permute-start.7 = (bf16[256,1280]{1,0:T(8,128)(2,1)S(1)}, bf16[256,1280]{1,0:T(8,128)(2,1)S(1)}, u32[]{:S(2)}, u32[]{:S(2)}) collective-permute-start(bf16[256,1280]{1,0:T(8,128)(2,1)S(1)} %collective-permute-done.5.two.refs_1_), channel_id=1, source_target_pairs={{0,32},{8,40},{16,48},{24,56},{32,64},{40,72},{48,80},{56,88},{64,... | collective-permute-start | bytes 1966088 | tf_op jit(solution)/shard_map/ppermute | solution.py:339
  55.9 17.6 %collective-permute-start.15 = (bf16[512,1280]{1,0:T(8,128)(2,1)S(1)}, bf16[512,1280]{1,0:T(8,128)(2,1)S(1)}, u32[]{:S(2)}, u32[]{:S(2)}) collective-permute-start(bf16[512,1280]{1,0:T(8,128)(2,1)S(1)} %collective-permute-done.14.refs_4_.refs_8_), channel_id=1, source_target_pairs={{0,4},{8,12},{16,20},{24,28},{32,36},{40,44},{48,52},{56,60},{64,6... | collective-permute-start | bytes 3932168 | tf_op jit(solution)/shard_map/ppermute | solution.py:339
  56.7 33.6 %collective-permute-start.12 = (bf16[256,1280]{1,0:T(8,128)(2,1)}, bf16[256,1280]{1,0:T(8,128)(2,1)S(1)}, u32[]{:S(2)}, u32[]{:S(2)}) collective-permute-start(bf16[256,1280]{1,0:T(8,128)(2,1)} %constant_dynamic-update-slice_fusion), channel_id=1, source_target_pairs={{4,28},{12,20},{20,12},{28,4},{36,60},{44,52},{52,44},{60,36},{68,... | collective-permute-start | bytes 1966088 | tf_op jit(solution)/shard_map/ppermute | solution.py:339
  59.7 22.1 %collective-permute-start.17 = (bf16[256,1280]{1,0:T(8,128)(2,1)S(1)}, bf16[256,1280]{1,0:T(8,128)(2,1)S(1)}, u32[]{:S(2)}, u32[]{:S(2)}) collective-permute-start(bf16[256,1280]{1,0:T(8,128)(2,1)S(1)} %collective-permute-done.16.refs_10_.refs_6_), channel_id=1, source_target_pairs={{0,4},{8,12},{16,20},{24,28},{32,36},{40,44},{48,52},{56,60},{64,6... | collective-permute-start | bytes 1966088 | tf_op jit(solution)/shard_map/ppermute | solution.py:339
  63.5 14.6 %collective-permute-start.6 = (bf16[256,1280]{1,0:T(8,128)(2,1)S(1)}, bf16[256,1280]{1,0:T(8,128)(2,1)S(1)}, u32[]{:S(2)}, u32[]{:S(2)}) collective-permute-start(bf16[256,1280]{1,0:T(8,128)(2,1)S(1)} %collective-permute-done.5.two.refs_1_), channel_id=1, source_target_pairs={{0,24},{8,16},{16,8},{24,0},{32,56},{40,48},{48,40},{56,32},{64,88... | collective-permute-start | bytes 1966088 | tf_op jit(solution)/shard_map/ppermute | solution.py:339
  64.3 13.8 %collective-permute-start.9 = (bf16[256,1280]{1,0:T(8,128)(2,1)S(1)}, bf16[256,1280]{1,0:T(8,128)(2,1)S(1)}, u32[]{:S(2)}, u32[]{:S(2)}) collective-permute-start(bf16[256,1280]{1,0:T(8,128)(2,1)S(1)} %broadcast_select_fusion.3), channel_id=1, source_target_pairs={{0,32},{8,40},{16,48},{24,56},{32,64},{40,72},{48,80},{56,88},{64,... | collective-permute-start | bytes 1966088 | tf_op jit(solution)/shard_map/ppermute | solution.py:339
  73.4 4.6 %copy-start.3 = (bf16[256,1280]{1,0:T(8,128)(2,1)S(1)}, bf16[256,1280]{1,0:T(8,128)(2,1)}, u32[]{:S(2)}) copy-start(bf16[256,1280]{1,0:T(8,128)(2,1)} %constant_dynamic-update-slice_fusion) | copy-start | bytes 1966084
  78.2 12.2 %collective-permute-start.10 = (bf16[256,1280]{1,0:T(8,128)(2,1)S(1)}, bf16[256,1280]{1,0:T(8,128)(2,1)S(1)}, u32[]{:S(2)}, u32[]{:S(2)}) collective-permute-start(bf16[256,1280]{1,0:T(8,128)(2,1)S(1)} %get-tuple-element.55), channel_id=1, source_target_pairs={{0,32},{8,40},{16,48},{24,56},{32,64},{40,72},{48,80},{56,88},{64,... | collective-permute-start | bytes 1966088 | tf_op jit(solution)/shard_map/ppermute | solution.py:339
  81.1 9.3 %collective-permute-start.11 = (bf16[256,1280]{1,0:T(8,128)(2,1)S(1)}, bf16[256,1280]{1,0:T(8,128)(2,1)S(1)}, u32[]{:S(2)}, u32[]{:S(2)}) collective-permute-start(bf16[256,1280]{1,0:T(8,128)(2,1)S(1)} %collective-permute-done.9.refs_4_), channel_id=1, source_target_pairs={{0,24},{8,16},{16,8},{24,0},{32,56},{40,48},{48,40},{56,32},{64,88... | collective-permute-start | bytes 1966088 | tf_op jit(solution)/shard_map/ppermute | solution.py:339
  97.6 5.9 %collective-permute-start.18 = (bf16[8,144,256]{2,1,0:T(8,128)(2,1)}, bf16[8,144,256]{2,1,0:T(8,128)(2,1)S(1)}, u32[]{:S(2)}, u32[]{:S(2)}) collective-permute-start(bf16[8,144,256]{2,1,0:T(8,128)(2,1)} %get-tuple-element.45), channel_id=1, source_target_pairs={{0,4},{8,12},{16,20},{24,28},{32,36},{40,44},{48,52},{56,60},{64,6... | collective-permute-start | bytes 1769480 | tf_op jit(solution)/shard_map/ppermute | solution.py:339
  104.5 14.3 %all-to-all-start = ((bf16[8,224,128]{2,1,0:T(8,128)(2,1)}), bf16[8,224,128]{2,1,0:T(8,128)(2,1)S(1)}, u32[]{:S(2)}, u32[]{:S(2)}) async-start(bf16[8,224,128]{2,1,0:T(8,128)(2,1)} %shard_map.110), calls=%async_computation | async-start | bytes 917504 | tf_op jit(solution)/shard_map/all_to_all | solution.py:451
